TPU v7x, 256 devices: a whole 4x4x8 slice. The times are simulated.
256 devices in a mesh: dom: 32 (over y, z), hid: 4 (over x_lo, core), wt: 2 (over x_hi).
Axes of the slice: x: 4 (x_hi: 2, x_lo: 2; x = x_hi * 2 + x_lo), y: 4, z: 8, core: 2. Of those that a mesh axis runs over, the one named last changes fastest.
Arguments:
- store_feat: bfloat16 [131072, 256], P('dom'), may hold values from -6 to 6
- want_in: int32 [32, 32, 128], P('dom'), may hold values from 0 to 4095
- nbr_in: int32 [262144, 10], P('dom'), may hold values from 0 to 4095
- self_in: int32 [262144], P('dom'), may hold values from 0 to 4095
- count_in: int32 [262144], P('dom'), may hold values from 1 to 10
- weight_one: bfloat16 [512, 1024], P('wt', 'hid'), may hold values from -0.375 to 0.375
- want_hid: int32 [32, 32, 128], P('dom'), may hold values from 0 to 8191
- nbr_hid: int32 [65536, 15], P('dom'), may hold values from 0 to 4095
- self_hid: int32 [65536], P('dom'), may hold values from 0 to 4095
- count_hid: int32 [65536], P('dom'), may hold values from 1 to 15
- weight_two: bfloat16 [2048, 1024], P('wt', 'hid'), may hold values from -0.1875 to 0.1875
Outputs:
- seed_embed: bfloat16 [65536, 1024], P('dom', 'hid')
Inputs may be any that keep to these rules, and one draw needn't show every extreme that they name: `count_in`: slots at or past a node's count hold arbitrary positions and are ignored. `count_hid`: slots at or past a seed's count hold arbitrary positions and are ignored.
All inputs are finite; a program needn't handle non-finite values.
Results may differ from a plain program's by a relative error of at most 0.0052.
Values may be sent and summed in bfloat16 or wider, within the bound.
No kernel may reach another device: no remote copies, remote signals or barrier semaphores. Data moves between devices by JAX's collectives and lax.ppermute only.
A program may use at most 128 MiB of HBM per device.

v0:
```python
import math

import jax
import jax.numpy as jnp
from jax import lax
from jax.sharding import PartitionSpec as P


def laid_out(pieces, dim):
    dims = list(pieces.shape[1:])
    dims[dim] *= pieces.shape[0]
    return jnp.moveaxis(pieces, 0, dim).reshape(dims)


def gather_together(arrays, axis, dims):
    ravelled = jnp.concatenate([a.reshape(-1) for a in arrays])
    lines, at, gathered = (lax.all_gather(ravelled, axis), 0, [])
    for a, dim in zip(arrays, dims):
        pieces = lines[:, at : at + a.size].reshape(-1, *a.shape)
        gathered.append(laid_out(pieces, dim))
        at += a.size
    return tuple(gathered)


def sent_together(arrays, axis, dim, along):
    widths = [a.shape[along] for a in arrays]
    both = jnp.concatenate(arrays, axis=along)
    whole = lax.all_gather(both, axis, axis=dim, tiled=True)
    return tuple(jnp.split(whole, [sum(widths[:k]) for k in range(1, len(widths))], axis=along))


def average(lookup, neighbours, counts):
    gathered = jnp.take(lookup, neighbours, axis=0)
    valid_mask = (lax.broadcasted_iota(jnp.int32, neighbours.shape, 1) < counts[:, None]).astype(
        jnp.bfloat16
    )
    summed = jnp.einsum("tk,tkf->tf", valid_mask, gathered, preferred_element_type=jnp.float32)
    return (summed / counts[:, None].astype(jnp.float32)).astype(jnp.bfloat16)


def average_blocks(lookup, neighbours, counts):
    targets = neighbours.shape[0]
    block_rows = math.gcd(targets, 512)
    nblocks = targets // block_rows

    def one_block(pieces):
        return average(lookup, pieces[0], pieces[1])

    result = lax.map(
        one_block,
        (
            neighbours.reshape(nblocks, block_rows, neighbours.shape[1]),
            counts.reshape(nblocks, block_rows),
        ),
    )
    return result.reshape(targets, lookup.shape[1])


def shards(
    store_feat,
    want_in,
    nbr_in,
    self_in,
    count_in,
    weight_one,
    want_hid,
    nbr_hid,
    self_hid,
    count_hid,
    weight_two,
):
    features = store_feat.shape[1]
    w_first, w_second = gather_together((weight_one, weight_two), "wt", (0, 0))
    picked = jnp.take(store_feat, want_in[0], axis=0)
    fetched = lax.all_to_all(picked, "dom", split_axis=0, concat_axis=0, tiled=True)
    lookup = fetched.reshape(-1, features)
    own_rows = jnp.take(lookup, self_in, axis=0)
    mean_rows = average_blocks(lookup, nbr_in, count_in)
    joined = jnp.concatenate([own_rows, mean_rows], 1)
    hidden = jax.nn.relu(jnp.dot(joined, w_first, preferred_element_type=jnp.float32)).astype(
        jnp.bfloat16
    )
    picked_hidden = jnp.take(hidden, want_hid[0], axis=0)
    arrived_hidden = lax.all_to_all(picked_hidden, "dom", split_axis=0, concat_axis=0, tiled=True)
    lookup_hidden = arrived_hidden.reshape(-1, hidden.shape[1])
    own_hidden = jnp.take(lookup_hidden, self_hid, axis=0)
    mean_hidden = average_blocks(lookup_hidden, nbr_hid, count_hid)
    full_own, full_mean = sent_together((own_hidden, mean_hidden), "hid", 1, 0)
    joined_hidden = jnp.concatenate([full_own, full_mean], 1)
    return jnp.dot(joined_hidden, w_second, preferred_element_type=jnp.float32).astype(jnp.bfloat16)


def solution(mesh):
    return jax.shard_map(
        shards,
        mesh=mesh,
        in_specs=(
            P("dom", None),
            P("dom", None, None),
            P("dom", None),
            P("dom"),
            P("dom"),
            P("wt", "hid"),
            P("dom", None, None),
            P("dom", None),
            P("dom"),
            P("dom"),
            P("wt", "hid"),
        ),
        out_specs=P("dom", "hid"),
        check_vma=False,
    )
```

profile of v0, /device:TPU:1, one launch (start us, length us, event | category | flops | bytes accessed | tf_op | source)
XLA Modules:
  0.0 1020.8 jit_solution(701229095005251392)
XLA Ops:
  8.1 16.9 %gather_fusion.2 = bf16[4096,256]{1,0:T(8,128)(2,1)} fusion(bf16[4096,256]{1,0:T(8,128)(2,1)S(1)} %copy-done, s32[4096]{0:T(1024)S(1)} %fusion.29), kind=kCustom, calls=%fused_computation.2 | custom fusion | bytes 4210688 | tf_op jit(solution)/shard_map/jit(_take)/gather | solution.py:74
  28.1 12.2 %all-to-all-start = ((bf16[32,128,256]{2,1,0:T(8,128)(2,1)}), bf16[32,128,256]{2,1,0:T(8,128)(2,1)S(1)}, u32[]{:S(2)}, u32[]{:S(2)}) async-start(bf16[32,128,256]{2,1,0:T(8,128)(2,1)} %broadcast_select_fusion.1), calls=%async_computation | async-start | bytes 4194304 | tf_op jit(solution)/shard_map/all_to_all | solution.py:75
  44.6 30.6 %all-gather.6.cloned.1.call-done = bf16[655360]{0:T(1024)(128)(2,1)} async-done(((bf16[327680]{0:T(1024)(128)(2,1)}), bf16[655360]{0:T(1024)(128)(2,1)}) %all-gather.6.cloned.1.call-update) | async-done | bytes 1310736 | tf_op jit(solution)/shard_map/all_gather | solution.py:17
  79.7 9.4 all-to-all-done
  89.2 563.5 %while.20 = (s32[]{:T(128)}, bf16[16,512,256]{2,1,0:T(8,128)(2,1)}, s32[16,512]{1,0:T(8,128)S(1)}, s32[16,512,10]{2,1,0:T(8,128)}, bf16[4096,256]{1,0:T(8,128)(2,1)S(1)}, /*index=5*/s32[]{:T(128)}) while((s32[]{:T(128)}, bf16[16,512,256]{2,1,0:T(8,128)(2,1)}, s32[16,512]{1,0:T(8,128)S(1)}, s32[16,512,10]{2,1,0:T(8,128)}, ...), condition=%wide.region_1.2_spmd, body=%wide.region_0.1_spmd.sunk | while | flops 4251138 | bytes 14615121 | solution.py:49
  90.3 21.0 %gather_fusion = bf16[5120,256]{1,0:T(8,128)(2,1)} fusion(bf16[4096,256]{1,0:T(8,128)(2,1)S(1)} %get-tuple-element.161, s32[5120]{0:T(1024)S(1)} %broadcast_clamp_fusion.2), kind=kCustom, calls=%fused_computation.clone.1 | custom fusion | bytes 5263360 | tf_op jit(solution)/shard_map/while/body/eval_jaxpr/jit(_take)/gather | solution.py:33
  111.3 6.0 reshape.274
  125.6 21.0 %gather_fusion = bf16[5120,256]{1,0:T(8,128)(2,1)} fusion(bf16[4096,256]{1,0:T(8,128)(2,1)S(1)} %get-tuple-element.161, s32[5120]{0:T(1024)S(1)} %broadcast_clamp_fusion.2), kind=kCustom, calls=%fused_computation.clone.1 | custom fusion | bytes 5263360 | tf_op jit(solution)/shard_map/while/body/eval_jaxpr/jit(_take)/gather | solution.py:33
  146.5 6.0 reshape.274
  160.8 21.0 %gather_fusion = bf16[5120,256]{1,0:T(8,128)(2,1)} fusion(bf16[4096,256]{1,0:T(8,128)(2,1)S(1)} %get-tuple-element.161, s32[5120]{0:T(1024)S(1)} %broadcast_clamp_fusion.2), kind=kCustom, calls=%fused_computation.clone.1 | custom fusion | bytes 5263360 | tf_op jit(solution)/shard_map/while/body/eval_jaxpr/jit(_take)/gather | solution.py:33
  181.7 6.0 reshape.274
  196.0 21.0 %gather_fusion = bf16[5120,256]{1,0:T(8,128)(2,1)} fusion(bf16[4096,256]{1,0:T(8,128)(2,1)S(1)} %get-tuple-element.161, s32[5120]{0:T(1024)S(1)} %broadcast_clamp_fusion.2), kind=kCustom, calls=%fused_computation.clone.1 | custom fusion | bytes 5263360 | tf_op jit(solution)/shard_map/while/body/eval_jaxpr/jit(_take)/gather | solution.py:33
  216.9 6.0 reshape.274
  231.2 21.0 %gather_fusion = bf16[5120,256]{1,0:T(8,128)(2,1)} fusion(bf16[4096,256]{1,0:T(8,128)(2,1)S(1)} %get-tuple-element.161, s32[5120]{0:T(1024)S(1)} %broadcast_clamp_fusion.2), kind=kCustom, calls=%fused_computation.clone.1 | custom fusion | bytes 5263360 | tf_op jit(solution)/shard_map/while/body/eval_jaxpr/jit(_take)/gather | solution.py:33
  252.2 6.0 reshape.274
  266.4 21.0 %gather_fusion = bf16[5120,256]{1,0:T(8,128)(2,1)} fusion(bf16[4096,256]{1,0:T(8,128)(2,1)S(1)} %get-tuple-element.161, s32[5120]{0:T(1024)S(1)} %broadcast_clamp_fusion.2), kind=kCustom, calls=%fused_computation.clone.1 | custom fusion | bytes 5263360 | tf_op jit(solution)/shard_map/while/body/eval_jaxpr/jit(_take)/gather | solution.py:33
  287.4 6.0 reshape.274
  301.6 21.0 %gather_fusion = bf16[5120,256]{1,0:T(8,128)(2,1)} fusion(bf16[4096,256]{1,0:T(8,128)(2,1)S(1)} %get-tuple-element.161, s32[5120]{0:T(1024)S(1)} %broadcast_clamp_fusion.2), kind=kCustom, calls=%fused_computation.clone.1 | custom fusion | bytes 5263360 | tf_op jit(solution)/shard_map/while/body/eval_jaxpr/jit(_take)/gather | solution.py:33
  322.6 6.0 reshape.274
  336.9 21.0 %gather_fusion = bf16[5120,256]{1,0:T(8,128)(2,1)} fusion(bf16[4096,256]{1,0:T(8,128)(2,1)S(1)} %get-tuple-element.161, s32[5120]{0:T(1024)S(1)} %broadcast_clamp_fusion.2), kind=kCustom, calls=%fused_computation.clone.1 | custom fusion | bytes 5263360 | tf_op jit(solution)/shard_map/while/body/eval_jaxpr/jit(_take)/gather | solution.py:33
  372.1 21.0 %gather_fusion = bf16[5120,256]{1,0:T(8,128)(2,1)} fusion(bf16[4096,256]{1,0:T(8,128)(2,1)S(1)} %get-tuple-element.161, s32[5120]{0:T(1024)S(1)} %broadcast_clamp_fusion.2), kind=kCustom, calls=%fused_computation.clone.1 | custom fusion | bytes 5263360 | tf_op jit(solution)/shard_map/while/body/eval_jaxpr/jit(_take)/gather | solution.py:33
  393.0 6.0 reshape.274
  407.3 21.0 %gather_fusion = bf16[5120,256]{1,0:T(8,128)(2,1)} fusion(bf16[4096,256]{1,0:T(8,128)(2,1)S(1)} %get-tuple-element.161, s32[5120]{0:T(1024)S(1)} %broadcast_clamp_fusion.2), kind=kCustom, calls=%fused_computation.clone.1 | custom fusion | bytes 5263360 | tf_op jit(solution)/shard_map/while/body/eval_jaxpr/jit(_take)/gather | solution.py:33
  442.5 21.0 %gather_fusion = bf16[5120,256]{1,0:T(8,128)(2,1)} fusion(bf16[4096,256]{1,0:T(8,128)(2,1)S(1)} %get-tuple-element.161, s32[5120]{0:T(1024)S(1)} %broadcast_clamp_fusion.2), kind=kCustom, calls=%fused_computation.clone.1 | custom fusion | bytes 5263360 | tf_op jit(solution)/shard_map/while/body/eval_jaxpr/jit(_take)/gather | solution.py:33
  463.5 6.0 reshape.274
  477.7 21.0 %gather_fusion = bf16[5120,256]{1,0:T(8,128)(2,1)} fusion(bf16[4096,256]{1,0:T(8,128)(2,1)S(1)} %get-tuple-element.161, s32[5120]{0:T(1024)S(1)} %broadcast_clamp_fusion.2), kind=kCustom, calls=%fused_computation.clone.1 | custom fusion | bytes 5263360 | tf_op jit(solution)/shard_map/while/body/eval_jaxpr/jit(_take)/gather | solution.py:33
  512.9 21.0 %gather_fusion = bf16[5120,256]{1,0:T(8,128)(2,1)} fusion(bf16[4096,256]{1,0:T(8,128)(2,1)S(1)} %get-tuple-element.161, s32[5120]{0:T(1024)S(1)} %broadcast_clamp_fusion.2), kind=kCustom, calls=%fused_computation.clone.1 | custom fusion | bytes 5263360 | tf_op jit(solution)/shard_map/while/body/eval_jaxpr/jit(_take)/gather | solution.py:33
  548.1 21.0 %gather_fusion = bf16[5120,256]{1,0:T(8,128)(2,1)} fusion(bf16[4096,256]{1,0:T(8,128)(2,1)S(1)} %get-tuple-element.161, s32[5120]{0:T(1024)S(1)} %broadcast_clamp_fusion.2), kind=kCustom, calls=%fused_computation.clone.1 | custom fusion | bytes 5263360 | tf_op jit(solution)/shard_map/while/body/eval_jaxpr/jit(_take)/gather | solution.py:33
  569.1 6.0 reshape.274
  583.3 21.0 %gather_fusion = bf16[5120,256]{1,0:T(8,128)(2,1)} fusion(bf16[4096,256]{1,0:T(8,128)(2,1)S(1)} %get-tuple-element.161, s32[5120]{0:T(1024)S(1)} %broadcast_clamp_fusion.2), kind=kCustom, calls=%fused_computation.clone.1 | custom fusion | bytes 5263360 | tf_op jit(solution)/shard_map/while/body/eval_jaxpr/jit(_take)/gather | solution.py:33
  618.6 21.0 %gather_fusion = bf16[5120,256]{1,0:T(8,128)(2,1)} fusion(bf16[4096,256]{1,0:T(8,128)(2,1)S(1)} %get-tuple-element.161, s32[5120]{0:T(1024)S(1)} %broadcast_clamp_fusion.2), kind=kCustom, calls=%fused_computation.clone.1 | custom fusion | bytes 5263360 | tf_op jit(solution)/shard_map/while/body/eval_jaxpr/jit(_take)/gather | solution.py:33
  652.7 33.0 %gather_fusion.3 = bf16[8192,256]{1,0:T(8,128)(2,1)} fusion(bf16[4096,256]{1,0:T(8,128)(2,1)S(1)} %get-tuple-element.184, s32[8192]{0:T(1024)S(1)} %fusion.27), kind=kCustom, calls=%fused_computation.3 | custom fusion | bytes 8421376 | tf_op jit(solution)/shard_map/jit(_take)/gather | solution.py:77
  685.6 6.0 broadcast_select_fusion
  691.6 6.5 fusion.16
  698.1 15.7 %gather_fusion.4 = bf16[4096,256]{1,0:T(8,128)(2,1)S(1)} fusion(bf16[8192,256]{1,0:T(8,128)(2,1)} %fusion.16, s32[4096]{0:T(1024)S(1)} %fusion.31), kind=kCustom, calls=%fused_computation.4 | custom fusion | bytes 4210688 | tf_op jit(solution)/shard_map/jit(_take)/gather | solution.py:83
  715.6 7.0 all-to-all-start.1
  723.3 48.1 %all-to-all-done.1 = bf16[32,128,256]{2,1,0:T(8,128)(2,1)S(1)} async-done(((bf16[32,128,256]{2,1,0:T(8,128)(2,1)}), bf16[32,128,256]{2,1,0:T(8,128)(2,1)S(1)}, u32[]{:S(2)}, u32[]{:S(2)}) %all-to-all-start.1) | async-done | bytes 2097184 | tf_op jit(solution)/shard_map/all_to_all | solution.py:84
  771.4 140.9 %while.21 = (s32[]{:T(128)}, bf16[4,512,256]{2,1,0:T(8,128)(2,1)}, s32[4,512]{1,0:T(4,128)S(1)}, s32[4,512,15]{2,1,0:T(8,128)S(1)}, bf16[4096,256]{1,0:T(8,128)(2,1)S(1)}, /*index=5*/s32[]{:T(128)}) while((s32[]{:T(128)}, bf16[4,512,256]{2,1,0:T(8,128)(2,1)}, s32[4,512]{1,0:T(4,128)S(1)}, s32[4,512,15]{2,1,0:T(8,128)S(1)}, ...), condition=%wide.region_3.4_spmd, body=%wide.region_2.3_spmd.sunk | while | flops 6245890 | bytes 21262928 | solution.py:49
  771.7 22.1 %gather_fusion.1 = bf16[7680,256]{1,0:T(8,128)(2,1)} fusion(bf16[4096,256]{1,0:T(8,128)(2,1)S(1)} %get-tuple-element.179, s32[8192]{0:T(1024)S(1)} %pad_clamp_fusion.2), kind=kCustom, calls=%fused_computation.1.clone.1 | custom fusion | bytes 7895040 | tf_op jit(solution)/shard_map/while/body/eval_jaxpr/jit(_take)/gather | solution.py:33
  793.8 6.7 reshape.278
  806.9 22.1 %gather_fusion.1 = bf16[7680,256]{1,0:T(8,128)(2,1)} fusion(bf16[4096,256]{1,0:T(8,128)(2,1)S(1)} %get-tuple-element.179, s32[8192]{0:T(1024)S(1)} %pad_clamp_fusion.2), kind=kCustom, calls=%fused_computation.1.clone.1 | custom fusion | bytes 7895040 | tf_op jit(solution)/shard_map/while/body/eval_jaxpr/jit(_take)/gather | solution.py:33
  829.0 6.7 reshape.278
  842.1 22.1 %gather_fusion.1 = bf16[7680,256]{1,0:T(8,128)(2,1)} fusion(bf16[4096,256]{1,0:T(8,128)(2,1)S(1)} %get-tuple-element.179, s32[8192]{0:T(1024)S(1)} %pad_clamp_fusion.2), kind=kCustom, calls=%fused_computation.1.clone.1 | custom fusion | bytes 7895040 | tf_op jit(solution)/shard_map/while/body/eval_jaxpr/jit(_take)/gather | solution.py:33
  864.2 6.7 reshape.278
  877.3 22.1 %gather_fusion.1 = bf16[7680,256]{1,0:T(8,128)(2,1)} fusion(bf16[4096,256]{1,0:T(8,128)(2,1)S(1)} %get-tuple-element.179, s32[8192]{0:T(1024)S(1)} %pad_clamp_fusion.2), kind=kCustom, calls=%fused_computation.1.clone.1 | custom fusion | bytes 7895040 | tf_op jit(solution)/shard_map/while/body/eval_jaxpr/jit(_take)/gather | solution.py:33
  899.4 6.7 reshape.278
  912.3 7.5 gather_fusion.5
  923.8 82.8 %all-gather.4.cloned.1.call-done = bf16[4096,1024]{1,0:T(8,128)(2,1)} async-done(((bf16[4096,256]{1,0:T(8,128)(2,1)}), bf16[4096,1024]{1,0:T(8,128)(2,1)}) %all-gather.4.cloned.1.call-update) | async-done | bytes 8388624 | tf_op jit(solution)/shard_map/all_gather | solution.py:28
  (245 shorter events, 220.0 us)
Async XLA Ops:
  6.5 1.6 copy-start
  25.1 15.3 %copy-start.4 = (bf16[1024,256]{1,0:T(8,128)(2,1)S(1)}, bf16[1024,256]{1,0:T(8,128)(2,1)}, u32[]{:S(2)}) copy-start(bf16[1024,256]{1,0:T(8,128)(2,1)} %param.25) | copy-start | bytes 1572868
  25.1 15.7 %copy-start.8 = (bf16[256,256]{1,0:T(8,128)(2,1)S(1)}, bf16[256,256]{1,0:T(8,128)(2,1)}, u32[]{:S(2)}) copy-start(bf16[256,256]{1,0:T(8,128)(2,1)} %param.20) | copy-start | bytes 393220
  28.1 13.7 %copy-start.3 = (s32[8192,10]{0,1:T(8,128)S(1)}, s32[8192,10]{0,1:T(8,128)}, u32[]{:S(2)}) copy-start(s32[8192,10]{0,1:T(8,128)} %param.17) | copy-start | bytes 983044
  28.1 61.1 %all-to-all-start = ((bf16[32,128,256]{2,1,0:T(8,128)(2,1)}), bf16[32,128,256]{2,1,0:T(8,128)(2,1)S(1)}, u32[]{:S(2)}, u32[]{:S(2)}) async-start(bf16[32,128,256]{2,1,0:T(8,128)(2,1)} %broadcast_select_fusion.1), calls=%async_computation | async-start | bytes 4194304 | tf_op jit(solution)/shard_map/all_to_all | solution.py:75
  40.3 4.2 copy-start.11
  40.3 4.2 copy-start.9
  40.3 4.2 copy-start.7
  40.3 34.8 %all-gather.6.cloned.1.call-start = ((), (), s32[]{:S(2)}) async-start(), calls=%async_computation.3 | async-start | bytes 1966080 | tf_op jit(solution)/shard_map/all_gather | solution.py:17
  76.8 12.4 %copy-start.2 = (bf16[2,327680]{1,0:T(2,128)(2,1)}, bf16[2,327680]{1,0:T(2,128)(2,1)S(1)}, u32[]{:S(2)}) copy-start(bf16[2,327680]{1,0:T(2,128)(2,1)S(1)} %reshape.252) | copy-start | bytes 3932164
  685.6 6.0 copy-start.5
  713.9 9.0 copy-start.6
  713.9 9.4 copy-start.12
  713.9 9.4 copy-start.10
  715.6 55.8 %all-to-all-start.1 = ((bf16[32,128,256]{2,1,0:T(8,128)(2,1)}), bf16[32,128,256]{2,1,0:T(8,128)(2,1)S(1)}, u32[]{:S(2)}, u32[]{:S(2)}) async-start(bf16[32,128,256]{2,1,0:T(8,128)(2,1)} %broadcast_select_fusion.2), calls=%async_computation.1 | async-start | bytes 4194304 | tf_op jit(solution)/shard_map/all_to_all | solution.py:84
  722.6 284.0 %all-gather.4.cloned.1.call-start = ((), (), s32[]{:S(2)}) async-start(), calls=%async_computation.2 | async-start | bytes 10485760 | tf_op jit(solution)/shard_map/all_gather | solution.py:28
  920.2 2.9 slice-start
  1010.6 3.3 copy-start.1
Sparse Core Ops, SparseCore 0:
  42.9 32.1 all-gather.5
  923.2 83.3 all-gather.3
where the time goes:
time: 1030 us; the launch traced here: 1020 us
  local copies, waits for them, and re-layouts  636 us (62%)
  waiting for transfers between devices  171 us (17%)
  matrix products  110 us (11%)
  other arithmetic  69.3 us (7%)
  starting transfers between devices  19.4 us (2%)
  between operations  13.7 us (1%)
    gather x40, local copies, waits for them, and re-layouts, average(): gathered = jnp.take(lookup, neighbours, axis=0)  547 us
    dot_general x20, matrix products, average(): jnp.einsum('tk,tkf->tf', valid_mask, gathered, preferred_element_type=jnp...  101 us
    all_gather x1, waiting for transfers between devices, sent_together(): whole = lax.all_gather(both, axis, axis=dim, tiled=True)  82.8 us
    all_to_all x1, waiting for transfers between devices, shards(): lax.all_to_all(picked_hidden, 'dom', split_axis=0, concat_axis=0, tiled=T...  48.1 us
    gather x1, local copies, waits for them, and re-layouts, shards(): own_rows = jnp.take(lookup, self_in, axis=0)  33 us
    all_gather x1, waiting for transfers between devices, gather_together(): lines, at, gathered = (lax.all_gather(ravelled, axis), 0, [])  30.6 us
  transfers between devices with their start and end apart: 4, of which 4 were waited for; matrix products, arithmetic and copies ran while one was open for 1% of the time, Pallas kernels for 0%

commit v1 on v0

v1 whole, which is shorter than its diff:
```python
import jax
import jax.numpy as jnp
from jax import lax
from jax.experimental import pallas as pl
from jax.experimental.pallas import tpu as pltpu
from jax.sharding import Mesh, PartitionSpec as P

BF16 = jnp.bfloat16
F32 = jnp.float32
MIB = 1 << 20
CHIPS = 4
LINE = ("xlo", "wt")
SLOTS = 16
LOW = 256


def spot(x):
    return (x % 2) * 2 + x // 2


UP = [(spot(x), spot((x + 1) % CHIPS)) for x in range(CHIPS)]
DOWN = [(spot(x), spot((x - 1) % CHIPS)) for x in range(CHIPS)]
ACROSS = [(spot(x), spot((x + 2) % CHIPS)) for x in range(CHIPS)]
SWAP = [(0, 1), (1, 0)]


def ring_pieces(block):
    half = block.shape[0] // 2
    below = lax.ppermute(block, LINE, UP)
    above = lax.ppermute(block, LINE, DOWN)
    far_low = lax.ppermute(below[:half], LINE, UP)
    far_high = lax.ppermute(above[half:], LINE, DOWN)
    return block, above, far_low, far_high, below


def place(position, x):
    return ((((position >> 5) - x) & 3) << 10) | ((position >> 7) << 5) | (position & 31)


def codes(neighbours, counts, x):
    targets, fan = neighbours.shape
    neighbours = jnp.pad(neighbours, ((0, 0), (0, SLOTS - fan)))
    at = place(neighbours, x)
    valid = lax.broadcasted_iota(jnp.int32, at.shape, 1) < counts[:, None]
    lane = lax.broadcasted_iota(jnp.int32, at.shape, 0) & (SLOTS - 1)
    high = jnp.where(valid, (at >> 8) * SLOTS + lane, -1)
    low = at & (LOW - 1)
    shape = (targets // SLOTS, SLOTS * SLOTS)
    return high.reshape(shape).astype(F32), low.reshape(shape).astype(F32)


def count_kernel(high_ref, low_ref, out_ref):
    groups = high_ref.shape[0]
    rows = lax.broadcasted_iota(jnp.int32, (LOW, LOW), 0).astype(F32).astype(BF16)
    one = jnp.ones((), BF16)
    zero = jnp.zeros((), BF16)
    for g in range(groups):
        high = high_ref[g : g + 1, :].astype(BF16)
        low = low_ref[g : g + 1, :].astype(BF16)
        left = jnp.where(rows == high, one, zero)
        right = jnp.where(rows == low, one, zero)
        counts = lax.dot_general(left, right, (((1,), (1,)), ((), ())), preferred_element_type=F32)
        counts = counts.astype(BF16)
        for k in range(LOW // SLOTS):
            out_ref[g * SLOTS : (g + 1) * SLOTS, k * LOW : (k + 1) * LOW] = counts[
                k * SLOTS : (k + 1) * SLOTS, :
            ]


def count_matrix(high, low, positions):
    groups, width = high.shape
    step = 8
    return pl.pallas_call(
        count_kernel,
        grid=(groups // step,),
        in_specs=[pl.BlockSpec((step, width), lambda i: (i, 0))] * 2,
        out_specs=pl.BlockSpec((step * SLOTS, positions), lambda i: (i, 0)),
        out_shape=jax.ShapeDtypeStruct((groups * SLOTS, positions), BF16),
        compiler_params=pltpu.CompilerParams(vmem_limit_bytes=16 * MIB),
        cost_estimate=pl.CostEstimate(
            flops=groups * 2 * LOW * LOW * LOW,
            transcendentals=0,
            bytes_accessed=groups * SLOTS * positions * 2,
        ),
        name="count_matrix",
    )(high, low)


def one_hot(index, start, width):
    at = lax.broadcasted_iota(jnp.int32, (index.shape[0], width), 1) + start
    return jnp.where(at == index, 1.0, 0.0).astype(BF16)


def dot(a, b):
    return jnp.dot(a, b, preferred_element_type=F32)


def mean_kernel(counts_ref, own_ref, size_ref, *refs):
    pieces, out_ref = refs[:-1], refs[-1]
    width = out_ref.shape[1] // 2
    own_at = own_ref[...]
    own = jnp.zeros((out_ref.shape[0], width), F32)
    total = own
    start = 0
    for piece in pieces:
        rows = piece.shape[0]
        data = piece[...]
        own = own + dot(one_hot(own_at, start, rows), data)
        total = total + dot(counts_ref[:, start : start + rows], data)
        start += rows
    out_ref[:, :width] = own.astype(BF16)
    out_ref[:, width:] = (total / size_ref[...]).astype(BF16)


def own_and_mean(counts, own_at, sizes, pieces):
    targets, positions = counts.shape
    width = pieces[0].shape[1]
    tile = 256
    return pl.pallas_call(
        mean_kernel,
        grid=(targets // tile,),
        in_specs=[
            pl.BlockSpec((tile, positions), lambda i: (i, 0)),
            pl.BlockSpec((tile, 1), lambda i: (i, 0)),
            pl.BlockSpec((tile, 1), lambda i: (i, 0)),
        ]
        + [pl.BlockSpec(p.shape, lambda i: (0, 0)) for p in pieces],
        out_specs=pl.BlockSpec((tile, 2 * width), lambda i: (i, 0)),
        out_shape=jax.ShapeDtypeStruct((targets, 2 * width), BF16),
        compiler_params=pltpu.CompilerParams(vmem_limit_bytes=24 * MIB),
        cost_estimate=pl.CostEstimate(
            flops=4 * targets * positions * width,
            transcendentals=0,
            bytes_accessed=targets * positions * 2,
        ),
        name="own_and_mean",
    )(counts, own_at, sizes, *pieces)


def project_kernel(mine_ref, other_ref, first_ref, second_ref, out_ref):
    k = mine_ref.shape[1]
    acc = dot(mine_ref[...], first_ref[:k, :]) + dot(other_ref[...], first_ref[k:, :])
    hidden = jnp.maximum(acc, 0.0).astype(BF16)
    out_ref[...] = dot(hidden, second_ref[...]).astype(BF16)


def project(mine, other, first, second):
    rows, k = mine.shape
    tile = 256
    width = second.shape[1]
    return pl.pallas_call(
        project_kernel,
        grid=(rows // tile,),
        in_specs=[
            pl.BlockSpec((tile, k), lambda i: (i, 0)),
            pl.BlockSpec((tile, k), lambda i: (i, 0)),
            pl.BlockSpec(first.shape, lambda i: (0, 0)),
            pl.BlockSpec(second.shape, lambda i: (0, 0)),
        ],
        out_specs=pl.BlockSpec((tile, width), lambda i: (i, 0)),
        out_shape=jax.ShapeDtypeStruct((rows, width), BF16),
        compiler_params=pltpu.CompilerParams(vmem_limit_bytes=20 * MIB),
        cost_estimate=pl.CostEstimate(
            flops=2 * rows * first.shape[1] * (2 * k + width),
            transcendentals=0,
            bytes_accessed=rows * (2 * k + width) * 2,
        ),
        name="project",
    )(mine, other, first, second)


def seed_kernel(counts_ref, own_ref, size_ref, *refs):
    pieces, out_ref = refs[:-1], refs[-1]
    width = out_ref.shape[1]
    own_at = own_ref[...]
    own = jnp.zeros((out_ref.shape[0], width), F32)
    total = own
    start = 0
    for piece in pieces:
        rows = piece.shape[0]
        own = own + dot(one_hot(own_at, start, rows), piece[:, :width])
        total = total + dot(counts_ref[:, start : start + rows], piece[:, width:])
        start += rows
    out_ref[...] = (own + total / size_ref[...]).astype(BF16)


def seeds(counts, own_at, sizes, pieces):
    targets, positions = counts.shape
    width = pieces[0].shape[1] // 2
    tile = 256
    return pl.pallas_call(
        seed_kernel,
        grid=(targets // tile,),
        in_specs=[
            pl.BlockSpec((tile, positions), lambda i: (i, 0)),
            pl.BlockSpec((tile, 1), lambda i: (i, 0)),
            pl.BlockSpec((tile, 1), lambda i: (i, 0)),
        ]
        + [pl.BlockSpec(p.shape, lambda i: (0, 0)) for p in pieces],
        out_specs=pl.BlockSpec((tile, width), lambda i: (i, 0)),
        out_shape=jax.ShapeDtypeStruct((targets, width), BF16),
        compiler_params=pltpu.CompilerParams(vmem_limit_bytes=32 * MIB),
        cost_estimate=pl.CostEstimate(
            flops=4 * targets * positions * width,
            transcendentals=0,
            bytes_accessed=targets * positions * 2,
        ),
        name="seeds",
    )(counts, own_at, sizes, *pieces)


def shards(
    store_feat,
    want_in,
    nbr_in,
    self_in,
    count_in,
    weight_one,
    want_hid,
    nbr_hid,
    self_hid,
    count_hid,
    weight_two,
):
    x = lax.axis_index("wt") * 2 + lax.axis_index("xlo")
    core = lax.axis_index("core")
    parts = want_in.shape[1]
    block = want_in.shape[2] // CHIPS
    half = store_feat.shape[1] // 2

    def mine(wanted):
        return lax.dynamic_slice_in_dim(wanted[0], block * x, block, 1).reshape(-1)

    def exchange(rows):
        pieces = rows.reshape(parts, block, rows.shape[1])
        return lax.all_to_all(pieces, "dom", 0, 0, tiled=True).reshape(rows.shape)

    columns = lax.dynamic_slice_in_dim(store_feat, half * core, half, 1)
    picked = columns.at[mine(want_in)].get(mode="promise_in_bounds")
    inputs = ring_pieces(exchange(picked))

    table = jnp.concatenate([nbr_in, self_in[:, None], count_in[:, None]], 1)
    nodes = table.at[mine(want_hid)].get(mode="promise_in_bounds")
    fan = nbr_in.shape[1]
    sizes = nodes[:, fan + 1]
    counts = count_matrix(*codes(nodes[:, :fan], sizes, x), parts * block * CHIPS)
    own_at = place(nodes[:, fan : fan + 1], x)
    ready = own_and_mean(counts, own_at, sizes[:, None].astype(F32), inputs)

    rows = lax.all_to_all(
        jnp.broadcast_to(weight_one[None], (8, *weight_one.shape)), ("xlo", "core", "wt"), 0, 0, tiled=True
    )
    rows = rows.reshape(4, 2, *weight_one.shape)
    first = jnp.moveaxis(rows, 0, 2).reshape(2, 2, half, 4 * weight_one.shape[1])
    first = jnp.swapaxes(first, 0, 1)
    first = jnp.where(core == 0, first, first[::-1]).reshape(4 * half, -1)
    other_rows = lax.ppermute(weight_two, LINE, ACROSS)
    low = lax.axis_index("wt") == 0
    second = jnp.concatenate(
        [jnp.where(low, weight_two, other_rows), jnp.where(low, other_rows, weight_two)], 1
    )

    counts_two = count_matrix(*codes(nbr_hid, count_hid, x), parts * block * CHIPS)
    arrived = ring_pieces(exchange(ready))
    projected = [
        project(piece, lax.ppermute(piece, "core", SWAP), first, second) for piece in arrived
    ]
    return seeds(
        counts_two, place(self_hid, x)[:, None], count_hid[:, None].astype(F32), projected
    )


def solution(mesh):
    mesh = Mesh(mesh.devices.reshape(32, 2, 2, 2), ("dom", "xlo", "core", "wt"))
    columns = ("xlo", "core")
    return jax.shard_map(
        shards,
        mesh=mesh,
        in_specs=(
            P("dom", None),
            P("dom", None, None),
            P("dom", None),
            P("dom"),
            P("dom"),
            P("wt", columns),
            P("dom", None, None),
            P("dom", None),
            P("dom"),
            P("dom"),
            P("wt", columns),
        ),
        out_specs=P("dom", columns),
        check_vma=False,
    )
```

time: 1030 us -> 166 us (0.16)
  local copies, waits for them, and re-layouts: 636 us -> 43.3 us
  waiting for transfers between devices: 171 us -> 17.7 us
  matrix products: 110 us -> 0 us
  other arithmetic: 69.3 us -> 9.13 us
  Pallas kernels: 0 us -> 46.9 us
  starting transfers between devices: 19.4 us -> 46.6 us
  between operations: 13.7 us -> 0.33 us
    gather x44 -> x2, local copies, waits for them, and re-layouts: 620 us -> 10.5 us  [the longest x1 6.22 us: shards(): nodes = table.at[mine(want_hid)].get(mode='promise_in_bounds')]
    all_gather x2 -> x0, waiting for transfers between devices: 113 us -> none  [the longest x1 82.8 us: sent_together(): whole = lax.all_gather(both, axis, axis=dim, tiled=True)]
    dot_general x22 -> x0, matrix products: 110 us -> none  [the longest x20 101 us: average(): jnp.einsum('tk,tkf->tf', valid_mask, gathered, preferred_element_type=jnp...]
    all_to_all x2 -> x3, waiting for transfers between devices: 57.6 us -> 9.6 us  [the longest x2 9.6 us: exchange(): return lax.all_to_all(pieces, 'dom', 0, 0, tiled=True).reshape(rows.shape)]
    pallas_call x0 -> x9, Pallas kernels: none -> 46.9 us  [the longest x5 15.1 us: project(): pl.pallas_call(project_kernel, grid=(rows // tile,), in_specs=[pl.BlockSp...]
    select_n x24 -> x4, other arithmetic: 26.9 us -> 3.35 us  [the longest x1 2.06 us: shards(): first = jnp.where(core == 0, first, first[::-1]).reshape(4 * half, -1)]
    and x24 -> x2, other arithmetic: 17.7 us -> 0.01 us  [codes(): lane = lax.broadcasted_iota(jnp.int32, at.shape, 0) & SLOTS - 1]
    dynamic_update_slice x20 -> x0, other arithmetic: 17.1 us -> none  [average_blocks(): lax.map(one_block, (neighbours.reshape(nblocks, block_rows, neighbours.sh...]
  transfers between devices with their start and end apart: 4 -> 17, of which waited for: 4 -> 3; matrix products, arithmetic and copies ran while one was open for 1% -> 24% of each run, Pallas kernels for 0% -> 14%
where the time goes in v1:
time: 166 us; the launch traced here: 164 us
  Pallas kernels  46.9 us (28%)
  starting transfers between devices  46.6 us (28%)
  local copies, waits for them, and re-layouts  43.3 us (26%)
  waiting for transfers between devices  17.7 us (11%)
  other arithmetic  9.13 us (6%)
    all_to_all x2, starting transfers between devices, exchange(): return lax.all_to_all(pieces, 'dom', 0, 0, tiled=True).reshape(rows.shape)  21.4 us
    pallas_call x5, Pallas kernels, project(): pl.pallas_call(project_kernel, grid=(rows // tile,), in_specs=[pl.BlockSp...  15.1 us
    pallas_call x1, Pallas kernels, seeds(): pl.pallas_call(seed_kernel, grid=(targets // tile,), in_specs=[pl.BlockSp...  13.8 us
    pallas_call x2, Pallas kernels, count_matrix(): pl.pallas_call(count_kernel, grid=(groups // step,), in_specs=[pl.BlockSp...  11.7 us
    all_to_all x2, waiting for transfers between devices, exchange(): return lax.all_to_all(pieces, 'dom', 0, 0, tiled=True).reshape(rows.shape)  9.6 us
    all_to_all x1, starting transfers between devices, shards(): lax.all_to_all(jnp.broadcast_to(weight_one[None], (8, *weight_one.shape))...  9.18 us
    unnamed x19, local copies, waits for them, and re-layouts  8.32 us
    ppermute x2, waiting for transfers between devices, ring_pieces(): below = lax.ppermute(block, LINE, UP)  7.52 us
  transfers between devices with their start and end apart: 17, of which 3 were waited for; matrix products, arithmetic and copies ran while one was open for 24% of the time, Pallas kernels for 14%

profile of v1, /device:TPU:1, one launch (start us, length us, event | category | flops | bytes accessed | tf_op | source)
XLA Modules:
  0.0 163.9 jit_solution(7370732532000537173)
XLA Ops:
  0.0 1.0 constant_dynamic-slice_fusion
  1.7 4.3 %gather_fusion.1 = bf16[1024,128]{1,0:T(8,128)(2,1)} fusion(bf16[4096,128]{1,0:T(8,128)(2,1)S(1)} %constant_dynamic-slice_fusion.1, s32[1024]{0:T(1024)S(1)} %broadcast_clamp_fusion), kind=kCustom, calls=%fused_computation.1 | custom fusion | bytes 528384 | tf_op jit(solution)/shard_map/gather | solution.py:239
  6.0 12.0 %all-to-all-start = ((bf16[32,32,128]{2,1,0:T(8,128)(2,1)}), bf16[32,32,128]{2,1,0:T(8,128)(2,1)S(1)}, u32[]{:S(2)}, u32[]{:S(2)}) async-start(bf16[32,32,128]{2,1,0:T(8,128)(2,1)} %bitcast.6), calls=%async_computation | async-start | bytes 524288 | tf_op jit(solution)/shard_map/all_to_all | solution.py:236
  18.1 1.1 pad_add_fusion
  19.2 2.7 %copy.41 = s32[8192,12]{1,0:T(8,128)} copy(s32[8192,12]{0,1:T(8,128)S(1)} %pad_add_fusion) | data formatting | bytes 786432 | tf_op jit(solution)/shard_map/concatenate | solution.py:242
  21.9 6.2 %gather_fusion = s32[1024,12]{1,0:T(8,128)} fusion(s32[8192,12]{1,0:T(8,128)} %copy.41, s32[1024]{0:T(1024)S(1)} %broadcast_clamp_fusion.1), kind=kCustom, calls=%fused_computation | custom fusion | bytes 102400 | tf_op jit(solution)/shard_map/gather | solution.py:243
  28.1 1.9 %slice_convert_fusion = (f32[1024,1]{1,0:T(8,128)S(1)}, s32[1024]{0:T(1024)S(1)}, s32[1024,1]{1,0:T(8,128)S(1)}) fusion(s32[1024,12]{1,0:T(8,128)} %gather_fusion, s32[]{:T(128)S(6)} %add.46), kind=kLoop, calls=%fused_computation.8 | loop fusion | flops 10240 | bytes 20484 | tf_op jit(solution)/shard_map/convert_element_type | solution.py:248
  30.0 1.3 collective-permute-start.1
  31.3 1.5 collective-permute-start
  32.8 1.2 copy.51
  34.7 1.8 %copy.44 = f32[1024,16]{1,0:T(8,128)} copy(f32[1024,16]{0,1:T(8,128)} %get-tuple-element.12) | data formatting | bytes 131072 | tf_op jit(solution)/shard_map/convert_element_type | solution.py:49
  36.5 1.3 convert_element_type.37.low_ref
  37.8 1.0 copy.43
  38.8 1.3 convert_element_type.35.high_ref
  40.0 0.9 slice.35
  41.1 0.9 slice.36
  42.0 2.7 %collective-permute-start.3 = (bf16[512,128]{1,0:T(8,128)(2,1)S(1)}, bf16[512,128]{1,0:T(8,128)(2,1)S(1)}, u32[]{:S(2)}, u32[]{:S(2)}) collective-permute-start(bf16[512,128]{1,0:T(8,128)(2,1)S(1)} %slice.36), channel_id=1, source_target_pairs={{0,5},{4,0},{1,4},{5,1},{2,7},{6,2},{3,6},{7,3},{8,13},{12,8},{9,1... | collective-permute-start | bytes 393224 | tf_op jit(solution)/shard_map/ppermute | solution.py:32
  44.7 3.9 %count_matrix.3.counts_ref = bf16[1024,4096]{1,0:T(8,128)(2,1)S(1)} custom-call(f32[64,256]{1,0:T(8,128)S(1)} %convert_element_type.35.high_ref, f32[64,256]{1,0:T(8,128)S(1)} %convert_element_type.37.low_ref), custom_call_target="tpu_custom_call" | custom-call | flops 2147483648 | bytes 8388608 | tf_op jit(solution)/shard_map/count_matrix/pallas_call | solution.py:73
  48.6 6.3 %own_and_mean.1 = bf16[1024,256]{1,0:T(8,128)(2,1)S(1)} custom-call(bf16[1024,4096]{1,0:T(8,128)(2,1)S(1)} %count_matrix.3.counts_ref, s32[1024,1]{1,0:T(8,128)S(1)} %get-tuple-element.9.own_ref, f32[1024,1]{1,0:T(8,128)S(1)} %get-tuple-element.7.size_ref, bf16[1024,128]{1,0:T(8,128)(2,1)S(1)} %bitcast.19, bf16[1024,128]{1,0:T(8,128)(2,1)} %collective-permute-done.refs_1_, ...), custom_call_target="tpu_custom_call" | custom-call | flops 2147483648 | bytes 8388608 | tf_op jit(solution)/shard_map/own_and_mean/pallas_call | solution.py:119
  55.0 0.8 copy-done.2
  55.7 9.4 %all-to-all-start.1 = ((bf16[32,32,256]{2,1,0:T(8,128)(2,1)}), bf16[32,32,256]{2,1,0:T(8,128)(2,1)}, u32[]{:S(2)}, u32[]{:S(2)}) async-start(bf16[32,32,256]{2,1,0:T(8,128)(2,1)} %bitcast.16), calls=%async_computation.1 | async-start | bytes 1048576 | tf_op jit(solution)/shard_map/all_to_all | solution.py:236
  65.5 1.0 and_convert_fusion
  68.1 9.6 %all-to-all-done.1 = bf16[32,32,256]{2,1,0:T(8,128)(2,1)} async-done(((bf16[32,32,256]{2,1,0:T(8,128)(2,1)}), bf16[32,32,256]{2,1,0:T(8,128)(2,1)}, u32[]{:S(2)}, u32[]{:S(2)}) %all-to-all-start.1) | async-done | bytes 524320 | tf_op jit(solution)/shard_map/all_to_all | solution.py:236
  77.7 1.9 %broadcast_in_dim.32 = bf16[8,256,256]{2,1,0:T(8,128)(2,1)} broadcast(bf16[256,256]{1,0:T(8,128)(2,1)} %param.16), dimensions={1,2} | broadcast | bytes 1179648 | tf_op jit(solution)/shard_map/broadcast_in_dim | solution.py:251
  79.6 9.2 %all-to-all-start.2 = ((bf16[8,256,256]{2,1,0:T(8,128)(2,1)}), bf16[8,256,256]{2,1,0:T(8,128)(2,1)}, u32[]{:S(2)}, u32[]{:S(2)}) async-start(bf16[8,256,256]{2,1,0:T(8,128)(2,1)} %broadcast_in_dim.32), calls=%async_computation.2 | async-start | bytes 2097152 | tf_op jit(solution)/shard_map/all_to_all | solution.py:250
  88.8 1.4 collective-permute-start.8
  90.2 7.8 %count_matrix.2.counts_ref = bf16[2048,4096]{1,0:T(8,128)(2,1)S(1)} custom-call(f32[128,256]{1,0:T(8,128)S(1)} %convert_element_type.29.high_ref, f32[128,256]{1,0:T(8,128)S(1)} %convert_element_type.31.low_ref), custom_call_target="tpu_custom_call" | custom-call | flops 4294967296 | bytes 16777216 | tf_op jit(solution)/shard_map/count_matrix/pallas_call | solution.py:73
  98.0 5.7 %copy-done.1 = bf16[2048,4096]{1,0:T(8,128)(2,1)} copy-done((bf16[2048,4096]{1,0:T(8,128)(2,1)}, bf16[2048,4096]{1,0:T(8,128)(2,1)S(1)}, u32[]{:S(2)}) %copy-start.1) | copy-done | bytes 16777240
  103.7 1.3 collective-permute-start.6
  105.4 1.4 copy.49.own_ref
  106.7 0.8 collective-permute-start.4
  107.5 7.5 %collective-permute-done.8.mine_ref = bf16[1024,256]{1,0:T(8,128)(2,1)} collective-permute-done((bf16[1024,256]{1,0:T(8,128)(2,1)}, bf16[1024,256]{1,0:T(8,128)(2,1)}, u32[]{:S(2)}, u32[]{:S(2)}) %collective-permute-start.8) | collective-permute-done | bytes 524320 | tf_op jit(solution)/shard_map/ppermute | solution.py:29
  115.0 1.7 %slice.37 = bf16[512,256]{1,0:T(8,128)(2,1)} slice(bf16[1024,256]{1,0:T(8,128)(2,1)} %collective-permute-done.8.mine_ref), slice={[0:512], [0:256]} | slice | bytes 524288 | tf_op jit(solution)/shard_map/slice | solution.py:31
  116.7 1.3 broadcast_select_fusion.1
  118.0 1.1 pad_maximum_fusion.second_ref
  119.1 3.0 %copy.47 = bf16[2,256,4,256]{3,2,1,0:T(4,128)(2,1)} copy(bf16[2,256,4,256]{3,1,0,2:T(8,128)(2,1)} %bitcast.11) | data formatting | bytes 2097152 | tf_op jit(solution)/shard_map/transpose | solution.py:254
  122.1 2.6 %reshape.105 = bf16[2,2,128,1024]{3,2,1,0:T(8,128)(2,1)} reshape(bf16[2,256,4,256]{3,2,1,0:T(4,128)(2,1)} %copy.47) | data formatting | bytes 2097152 | tf_op jit(solution)/shard_map/reshape | solution.py:254
  124.7 1.0 slice.38
  125.6 2.8 %collective-permute-start.11 = (bf16[512,256]{1,0:T(8,128)(2,1)S(1)}, bf16[512,256]{1,0:T(8,128)(2,1)S(1)}, u32[]{:S(2)}, u32[]{:S(2)}) collective-permute-start(bf16[512,256]{1,0:T(8,128)(2,1)S(1)} %slice.38), channel_id=1, source_target_pairs={{0,5},{4,0},{1,4},{5,1},{2,7},{6,2},{3,6},{7,3},{8,13},{12,8},{9,1... | collective-permute-start | bytes 786440 | tf_op jit(solution)/shard_map/ppermute | solution.py:32
  128.4 1.3 collective-permute-start.13
  129.7 2.1 %reverse_select_fusion = bf16[2,2,128,1024]{3,2,0,1:T(8,128)(2,1)S(1)} fusion(bf16[2,2,128,1024]{3,2,0,1:T(8,128)(2,1)} %bitcast.26, pred[]{:T(512)S(6)} %eq.6), kind=kLoop, calls=%fused_computation.2 | loop fusion | flops 524288 | bytes 2097153 | tf_op jit(solution)/shard_map/jit(_where)/select_n | solution.py:256
  133.0 1.9 %collective-permute-start.12 = (bf16[512,256]{1,0:T(8,128)(2,1)S(1)}, bf16[512,256]{1,0:T(8,128)(2,1)S(1)}, u32[]{:S(2)}, u32[]{:S(2)}) collective-permute-start(bf16[512,256]{1,0:T(8,128)(2,1)S(1)} %collective-permute-done.11.mine_ref), channel_id=1, source_target_pairs={{0,2},{2,0},{1,3},{3,1},{4,6},{6,4},{5,7},{7,5},{8,10},{10,8},{9,1... | collective-permute-start | bytes 786440 | tf_op jit(solution)/shard_map/ppermute | solution.py:266
  134.9 4.1 %project.5.refs_0_ = bf16[1024,512]{1,0:T(8,128)(2,1)S(1)} custom-call(bf16[1024,256]{1,0:T(8,128)(2,1)} %bitcast.9.mine_ref, bf16[1024,256]{1,0:T(8,128)(2,1)} %collective-permute-done.4.other_ref, bf16[512,1024]{1,0:T(8,128)(2,1)S(1)} %bitcast.20, bf16[1024,512]{1,0:T(8,128)(2,1)S(1)} %copy-done.4), custom_call_target="tpu_custom_call" | custom-call | flops 2147483648 | bytes 2097152 | tf_op jit(solution)/shard_map/project/pallas_call | solution.py:151
  139.1 1.5 project.7.refs_2_
  140.5 1.5 project.8.refs_3_
  142.0 4.0 %project.9.refs_4_ = bf16[1024,512]{1,0:T(8,128)(2,1)S(1)} custom-call(bf16[1024,256]{1,0:T(8,128)(2,1)} %collective-permute-done.8.mine_ref, bf16[1024,256]{1,0:T(8,128)(2,1)S(1)} %collective-permute-done.13.other_ref, bf16[512,1024]{1,0:T(8,128)(2,1)S(1)} %bitcast.23, bf16[1024,512]{1,0:T(8,128)(2,1)S(1)} %copy-done.4), custom_call_target="tpu_custom_call" | custom-call | flops 2147483648 | bytes 2097152 | tf_op jit(solution)/shard_map/project/pallas_call | solution.py:151
  146.0 4.1 %project.6.refs_1_ = bf16[1024,512]{1,0:T(8,128)(2,1)S(1)} custom-call(bf16[1024,256]{1,0:T(8,128)(2,1)} %collective-permute-done.6.mine_ref, bf16[1024,256]{1,0:T(8,128)(2,1)S(1)} %collective-permute-done.7.other_ref, bf16[512,1024]{1,0:T(8,128)(2,1)S(1)} %bitcast.24, bf16[1024,512]{1,0:T(8,128)(2,1)S(1)} %copy-done.4), custom_call_target="tpu_custom_call" | custom-call | flops 2147483648 | bytes 2097152 | tf_op jit(solution)/shard_map/project/pallas_call | solution.py:151
  150.1 13.8 %seeds.1 = bf16[2048,256]{1,0:T(8,128)(2,1)} custom-call(bf16[2048,4096]{1,0:T(8,128)(2,1)} %copy-done.1, s32[2048,1]{1,0:T(8,128)S(1)} %copy-done.3, f32[2048,1]{1,0:T(8,128)S(1)} %copy.50.size_ref, bf16[1024,512]{1,0:T(8,128)(2,1)S(1)} %project.5.refs_0_, bf16[1024,512]{1,0:T(8,128)(2,1)S(1)} %project.6.refs_1_, bf16[512,512]{1,0:T(8,128)(2,1)S(1)} %project.7.refs_2_, ...), custom_call_target="tpu_custom_call" | custom-call | flops 8589934592 | bytes 16777216 | tf_op jit(solution)/shard_map/seeds/pallas_call | solution.py:191
  (54 shorter events, 5.2 us)
Async XLA Ops:
  0.0 1.6 copy-start
  1.6 16.5 %copy-start.5 = (s32[8192]{0:T(1024)S(1)}, s32[8192]{0:T(1024)}, u32[]{:S(2)}) copy-start(s32[8192]{0:T(1024)} %param.15) | copy-start | bytes 98308
  1.6 16.5 %copy-start.6 = (s32[8192]{0:T(1024)S(1)}, s32[8192]{0:T(1024)}, u32[]{:S(2)}) copy-start(s32[8192]{0:T(1024)} %param.14) | copy-start | bytes 98308
  6.0 24.0 %all-to-all-start = ((bf16[32,32,128]{2,1,0:T(8,128)(2,1)}), bf16[32,32,128]{2,1,0:T(8,128)(2,1)S(1)}, u32[]{:S(2)}, u32[]{:S(2)}) async-start(bf16[32,32,128]{2,1,0:T(8,128)(2,1)} %bitcast.6), calls=%async_computation | async-start | bytes 524288 | tf_op jit(solution)/shard_map/all_to_all | solution.py:236
  30.0 10.0 %collective-permute-start.1 = (bf16[1024,128]{1,0:T(8,128)(2,1)S(1)}, bf16[1024,128]{1,0:T(8,128)(2,1)}, u32[]{:S(2)}, u32[]{:S(2)}) collective-permute-start(bf16[1024,128]{1,0:T(8,128)(2,1)S(1)} %bitcast.17), channel_id=1, source_target_pairs={{0,4},{4,1},{1,5},{5,0},{2,6},{6,3},{3,7},{7,2},{8,12},{12,9},{9,1... | collective-permute-start | bytes 786440 | tf_op jit(solution)/shard_map/ppermute | solution.py:29
  31.3 9.8 %collective-permute-start = (bf16[1024,128]{1,0:T(8,128)(2,1)S(1)}, bf16[1024,128]{1,0:T(8,128)(2,1)}, u32[]{:S(2)}, u32[]{:S(2)}) collective-permute-start(bf16[1024,128]{1,0:T(8,128)(2,1)S(1)} %bitcast.18), channel_id=1, source_target_pairs={{0,5},{4,0},{1,4},{5,1},{2,7},{6,2},{3,6},{7,3},{8,13},{12,8},{9,1... | collective-permute-start | bytes 786440 | tf_op jit(solution)/shard_map/ppermute | solution.py:30
  41.0 7.7 %collective-permute-start.2 = (bf16[512,128]{1,0:T(8,128)(2,1)S(1)}, bf16[512,128]{1,0:T(8,128)(2,1)S(1)}, u32[]{:S(2)}, u32[]{:S(2)}) collective-permute-start(bf16[512,128]{1,0:T(8,128)(2,1)S(1)} %slice.35), channel_id=1, source_target_pairs={{0,4},{4,1},{1,5},{5,0},{2,6},{6,3},{3,7},{7,2},{8,12},{12,9},{9,1... | collective-permute-start | bytes 393224 | tf_op jit(solution)/shard_map/ppermute | solution.py:31
  42.0 6.6 %collective-permute-start.3 = (bf16[512,128]{1,0:T(8,128)(2,1)S(1)}, bf16[512,128]{1,0:T(8,128)(2,1)S(1)}, u32[]{:S(2)}, u32[]{:S(2)}) collective-permute-start(bf16[512,128]{1,0:T(8,128)(2,1)S(1)} %slice.36), channel_id=1, source_target_pairs={{0,5},{4,0},{1,4},{5,1},{2,7},{6,2},{3,6},{7,3},{8,13},{12,8},{9,1... | collective-permute-start | bytes 393224 | tf_op jit(solution)/shard_map/ppermute | solution.py:32
  48.6 16.9 %copy-start.7 = (s32[2048]{0:T(1024)S(1)}, s32[2048]{0:T(1024)}, u32[]{:S(2)}) copy-start(s32[2048]{0:T(1024)} %param.20) | copy-start | bytes 24580
  54.9 0.8 copy-start.2
  55.7 21.9 %all-to-all-start.1 = ((bf16[32,32,256]{2,1,0:T(8,128)(2,1)}), bf16[32,32,256]{2,1,0:T(8,128)(2,1)}, u32[]{:S(2)}, u32[]{:S(2)}) async-start(bf16[32,32,256]{2,1,0:T(8,128)(2,1)} %bitcast.16), calls=%async_computation.1 | async-start | bytes 1048576 | tf_op jit(solution)/shard_map/all_to_all | solution.py:236
  65.1 51.6 %collective-permute-start.5 = (bf16[1024,256]{1,0:T(8,128)(2,1)}, bf16[1024,256]{1,0:T(8,128)(2,1)}, u32[]{:S(2)}, u32[]{:S(2)}) collective-permute-start(bf16[1024,256]{1,0:T(8,128)(2,1)} %param.21), channel_id=1, source_target_pairs={{0,1},{4,5},{1,0},{5,4},{2,3},{6,7},{3,2},{7,6},{8,9},{12,13},{9,8... | collective-permute-start | bytes 1572872 | tf_op jit(solution)/shard_map/ppermute | solution.py:257
  79.6 39.5 %all-to-all-start.2 = ((bf16[8,256,256]{2,1,0:T(8,128)(2,1)}), bf16[8,256,256]{2,1,0:T(8,128)(2,1)}, u32[]{:S(2)}, u32[]{:S(2)}) async-start(bf16[8,256,256]{2,1,0:T(8,128)(2,1)} %broadcast_in_dim.32), calls=%async_computation.2 | async-start | bytes 2097152 | tf_op jit(solution)/shard_map/all_to_all | solution.py:250
  88.8 16.2 %copy-start.8 = (s32[2048]{0:T(1024)S(1)}, s32[2048]{0:T(1024)}, u32[]{:S(2)}) copy-start(s32[2048]{0:T(1024)} %param.19) | copy-start | bytes 24580
  88.8 26.3 %collective-permute-start.8 = (bf16[1024,256]{1,0:T(8,128)(2,1)}, bf16[1024,256]{1,0:T(8,128)(2,1)}, u32[]{:S(2)}, u32[]{:S(2)}) collective-permute-start(bf16[1024,256]{1,0:T(8,128)(2,1)} %bitcast.9.mine_ref), channel_id=1, source_target_pairs={{0,4},{4,1},{1,5},{5,0},{2,6},{6,3},{3,7},{7,2},{8,12},{12,9},{9,1... | collective-permute-start | bytes 1572872 | tf_op jit(solution)/shard_map/ppermute | solution.py:29
  97.9 5.7 %copy-start.1 = (bf16[2048,4096]{1,0:T(8,128)(2,1)}, bf16[2048,4096]{1,0:T(8,128)(2,1)S(1)}, u32[]{:S(2)}) copy-start(bf16[2048,4096]{1,0:T(8,128)(2,1)S(1)} %count_matrix.2.counts_ref) | copy-start | bytes 50331652
  103.7 21.0 %collective-permute-start.6 = (bf16[1024,256]{1,0:T(8,128)(2,1)}, bf16[1024,256]{1,0:T(8,128)(2,1)}, u32[]{:S(2)}, u32[]{:S(2)}) collective-permute-start(bf16[1024,256]{1,0:T(8,128)(2,1)} %bitcast.9.mine_ref), channel_id=1, source_target_pairs={{0,5},{4,0},{1,4},{5,1},{2,7},{6,2},{3,6},{7,3},{8,13},{12,8},{9,1... | collective-permute-start | bytes 1572872 | tf_op jit(solution)/shard_map/ppermute | solution.py:30
  106.7 28.2 %collective-permute-start.4 = (bf16[1024,256]{1,0:T(8,128)(2,1)}, bf16[1024,256]{1,0:T(8,128)(2,1)}, u32[]{:S(2)}, u32[]{:S(2)}) collective-permute-start(bf16[1024,256]{1,0:T(8,128)(2,1)} %bitcast.9.mine_ref), channel_id=1, source_target_pairs={{0,2},{2,0},{1,3},{3,1},{4,6},{6,4},{5,7},{7,5},{8,10},{10,8},{9,1... | collective-permute-start | bytes 1572872 | tf_op jit(solution)/shard_map/ppermute | solution.py:266
  116.7 13.0 %collective-permute-start.9 = (bf16[512,256]{1,0:T(8,128)(2,1)}, bf16[512,256]{1,0:T(8,128)(2,1)S(1)}, u32[]{:S(2)}, u32[]{:S(2)}) collective-permute-start(bf16[512,256]{1,0:T(8,128)(2,1)} %slice.37), channel_id=1, source_target_pairs={{0,4},{4,1},{1,5},{5,0},{2,6},{6,3},{3,7},{7,2},{8,12},{12,9},{9,1... | collective-permute-start | bytes 786440 | tf_op jit(solution)/shard_map/ppermute | solution.py:31
  125.6 7.4 %collective-permute-start.11 = (bf16[512,256]{1,0:T(8,128)(2,1)S(1)}, bf16[512,256]{1,0:T(8,128)(2,1)S(1)}, u32[]{:S(2)}, u32[]{:S(2)}) collective-permute-start(bf16[512,256]{1,0:T(8,128)(2,1)S(1)} %slice.38), channel_id=1, source_target_pairs={{0,5},{4,0},{1,4},{5,1},{2,7},{6,2},{3,6},{7,3},{8,13},{12,8},{9,1... | collective-permute-start | bytes 786440 | tf_op jit(solution)/shard_map/ppermute | solution.py:32
  128.4 13.6 %collective-permute-start.13 = (bf16[1024,256]{1,0:T(8,128)(2,1)}, bf16[1024,256]{1,0:T(8,128)(2,1)S(1)}, u32[]{:S(2)}, u32[]{:S(2)}) collective-permute-start(bf16[1024,256]{1,0:T(8,128)(2,1)} %collective-permute-done.8.mine_ref), channel_id=1, source_target_pairs={{0,2},{2,0},{1,3},{3,1},{4,6},{6,4},{5,7},{7,5},{8,10},{10,8},{9,1... | collective-permute-start | bytes 1572872 | tf_op jit(solution)/shard_map/ppermute | solution.py:266
  129.7 9.3 %collective-permute-start.10 = (bf16[512,256]{1,0:T(8,128)(2,1)S(1)}, bf16[512,256]{1,0:T(8,128)(2,1)S(1)}, u32[]{:S(2)}, u32[]{:S(2)}) collective-permute-start(bf16[512,256]{1,0:T(8,128)(2,1)S(1)} %collective-permute-done.9.mine_ref), channel_id=1, source_target_pairs={{0,2},{2,0},{1,3},{3,1},{4,6},{6,4},{5,7},{7,5},{8,10},{10,8},{9,1... | collective-permute-start | bytes 786440 | tf_op jit(solution)/shard_map/ppermute | solution.py:266
  129.7 5.2 %copy-start.4 = (bf16[1024,512]{1,0:T(8,128)(2,1)S(1)}, bf16[1024,512]{1,0:T(8,128)(2,1)}, u32[]{:S(2)}) copy-start(bf16[1024,512]{1,0:T(8,128)(2,1)} %pad_maximum_fusion.second_ref) | copy-start | bytes 3145732
  131.9 14.2 %collective-permute-start.7 = (bf16[1024,256]{1,0:T(8,128)(2,1)}, bf16[1024,256]{1,0:T(8,128)(2,1)S(1)}, u32[]{:S(2)}, u32[]{:S(2)}) collective-permute-start(bf16[1024,256]{1,0:T(8,128)(2,1)} %collective-permute-done.6.mine_ref), channel_id=1, source_target_pairs={{0,2},{2,0},{1,3},{3,1},{4,6},{6,4},{5,7},{7,5},{8,10},{10,8},{9,1... | collective-permute-start | bytes 1572872 | tf_op jit(solution)/shard_map/ppermute | solution.py:266
  133.0 7.5 %collective-permute-start.12 = (bf16[512,256]{1,0:T(8,128)(2,1)S(1)}, bf16[512,256]{1,0:T(8,128)(2,1)S(1)}, u32[]{:S(2)}, u32[]{:S(2)}) collective-permute-start(bf16[512,256]{1,0:T(8,128)(2,1)S(1)} %collective-permute-done.11.mine_ref), channel_id=1, source_target_pairs={{0,2},{2,0},{1,3},{3,1},{4,6},{6,4},{5,7},{7,5},{8,10},{10,8},{9,1... | collective-permute-start | bytes 786440 | tf_op jit(solution)/shard_map/ppermute | solution.py:266
  146.0 4.1 %copy-start.3 = (s32[2048,1]{1,0:T(8,128)S(1)}, s32[2048,1]{1,0:T(8,128)}, u32[]{:S(2)}) copy-start(s32[2048,1]{1,0:T(8,128)} %copy.49.own_ref) | copy-start | bytes 24580

commit v2 on v0

v2 whole, which is shorter than its diff:
```python
import functools

import jax
import jax.numpy as jnp
from jax import lax
from jax.experimental import pallas as pl
from jax.experimental.pallas import tpu as pltpu
from jax.sharding import Mesh, PartitionSpec as P


BF16 = jnp.bfloat16
F32 = jnp.float32
MIB = 1 << 20
CHIPS = 4
LINE = ("xlo", "wt")
SLOTS = 16
FAN = 10
TOKEN = jax.ShapeDtypeStruct((8, 128), jnp.int32)
LOW = 256


def in_vmem(count):
    return [pl.BlockSpec(memory_space=pltpu.VMEM)] * count


def spot(x):
    return (x % 2) * 2 + x // 2


UP = [(spot(x), spot((x + 1) % CHIPS)) for x in range(CHIPS)]
DOWN = [(spot(x), spot((x - 1) % CHIPS)) for x in range(CHIPS)]
ACROSS = [(spot(x), spot((x + 2) % CHIPS)) for x in range(CHIPS)]
SWAP = [(0, 1), (1, 0)]


def send(block, pairs):
    return lax.ppermute(block, LINE, pairs)


def swap(block):
    return lax.ppermute(block, "core", SWAP)


def place(position, x):
    return ((((position >> 5) - x) & 3) << 10) | ((position >> 7) << 5) | (position & 31)


def write_counts(high, low, out_ref, base):
    slot = lax.broadcasted_iota(jnp.int32, (SLOTS, LOW), 0)
    lane = lax.broadcasted_iota(jnp.int32, (SLOTS, LOW), 1)
    expand = jnp.where((lane & (SLOTS - 1)) == slot, 1.0, 0.0).astype(BF16)
    high = dot(high.astype(F32).astype(BF16), expand)
    low = dot(low.astype(F32).astype(BF16), expand)
    target = lax.broadcasted_iota(jnp.int32, high.shape, 0)
    lane = lax.broadcasted_iota(jnp.int32, high.shape, 1)
    mine = (target & (SLOTS - 1)) == (lane >> 4)
    high = jnp.where(mine, high, -1.0).astype(BF16)
    low = jnp.where(mine, low, 0.0)
    rows = lax.broadcasted_iota(jnp.int32, (LOW, LOW), 0).astype(F32).astype(BF16)
    one = jnp.ones((), BF16)
    zero = jnp.zeros((), BF16)
    for g in range(high.shape[0] // SLOTS):
        mine_high = high[g * SLOTS : (g + 1) * SLOTS, :]
        left = jnp.concatenate(
            [jnp.where(mine_high == jnp.full((), k, BF16), one, zero) for k in range(SLOTS)], 0
        )
        mine_low = jnp.sum(low[g * SLOTS : (g + 1) * SLOTS, :], axis=0, keepdims=True).astype(BF16)
        right = jnp.where(rows == mine_low, one, zero)
        counts = lax.dot_general(left, right, (((1,), (1,)), ((), ())), preferred_element_type=F32)
        counts = counts.astype(BF16)
        store_counts(counts, out_ref, base + g * SLOTS)


def store_counts(counts, out_ref, start):
    start = pl.multiple_of(start, SLOTS)
    for k in range(SLOTS):
        out_ref[pl.ds(start, SLOTS), k * LOW : (k + 1) * LOW] = counts[k * SLOTS : (k + 1) * SLOTS, :]


def table_kernel(slots_ref, own_ref, size_ref, out_ref, lines_ref):
    lines_ref[...] = jnp.zeros(lines_ref.shape, jnp.int32)
    lanes = lines_ref.shape[1]
    width = slots_ref.shape[1]
    base = pl.program_id(0) * width
    for b in range(width // lanes):
        at = slice(b * lanes, (b + 1) * lanes)
        lines_ref[:FAN, :] = slots_ref[:, at]
        lines_ref[FAN : FAN + 1, :] = own_ref[:, at]
        lines_ref[FAN + 1 : FAN + 2, :] = size_ref[:, at]
        start = pl.multiple_of(base + b * lanes, lanes)
        out_ref[pl.ds(start, lanes), :] = lines_ref[...].T


def node_table(slots, own, sizes):
    stored = slots.shape[1]
    step = 1024
    return pl.pallas_call(
        table_kernel,
        grid=(stored // step,),
        in_specs=[pl.BlockSpec((a.shape[0], step), lambda i: (0, i)) for a in (slots, own, sizes)],
        out_specs=in_vmem(1)[0],
        out_shape=jax.ShapeDtypeStruct((stored, SLOTS), jnp.int32),
        scratch_shapes=[pltpu.VMEM((SLOTS, 128), jnp.int32)],
        compiler_params=pltpu.CompilerParams(vmem_limit_bytes=2 * MIB),
        name="node_table",
    )(slots, own, sizes)


def node_kernel(request_ref, x_ref, table_ref, nodes_ref, out_ref, token_ref, rows_ref):
    token_ref[...] = jnp.zeros(token_ref.shape, jnp.int32)
    step = rows_ref.shape[0]
    base = pl.multiple_of(pl.program_id(0) * step, step)
    for i in range(step):
        rows_ref[i : i + 1, :] = table_ref[pl.ds(request_ref[base + i], 1), :]
    rows = rows_ref[...]
    nodes_ref[...] = rows
    size = rows[:, FAN + 1 : FAN + 2]
    at = place(rows, x_ref[0])
    valid = lax.broadcasted_iota(jnp.int32, rows.shape, 1) < size
    high = jnp.where(valid, at >> 8, -1)
    write_counts(high, at & (LOW - 1), out_ref, 0)


def node_counts(requests, x, table, positions):
    targets = requests.shape[0]
    step = 256
    return pl.pallas_call(
        node_kernel,
        grid_spec=pltpu.PrefetchScalarGridSpec(
            num_scalar_prefetch=2,
            grid=(targets // step,),
            in_specs=in_vmem(1),
            out_specs=(
                pl.BlockSpec((step, SLOTS), lambda i, r, x: (i, 0)),
                pl.BlockSpec((step, positions), lambda i, r, x: (i, 0)),
                in_vmem(1)[0],
            ),
            scratch_shapes=[pltpu.VMEM((step, SLOTS), jnp.int32)],
        ),
        out_shape=(
            jax.ShapeDtypeStruct((targets, SLOTS), jnp.int32),
            pltpu.HBM((targets, positions), BF16),
            TOKEN,
        ),
        compiler_params=pltpu.CompilerParams(vmem_limit_bytes=10 * MIB),
        cost_estimate=pl.CostEstimate(
            flops=targets * 2 * SLOTS * LOW * LOW, transcendentals=0, bytes_accessed=targets * positions * 2
        ),
        name="node_counts",
    )(requests, x.reshape(1), table)


def codes(neighbours, counts, x):
    targets, fan = neighbours.shape
    at = place(jnp.pad(neighbours, ((0, 0), (0, SLOTS - fan))), x)
    valid = lax.broadcasted_iota(jnp.int32, at.shape, 1) < counts[:, None]
    target = lax.broadcasted_iota(jnp.int32, at.shape, 0) & (SLOTS - 1)
    high = jnp.where(valid, (at >> 8) * SLOTS + target + 1, 0)
    return (high * LOW + (at & (LOW - 1))).reshape(targets // SLOTS, SLOTS * SLOTS)


def slot_kernel(code_ref, *refs):
    out_ref, token_ref = refs[-2:]
    token_ref[...] = jnp.zeros(token_ref.shape, jnp.int32)
    rows = lax.broadcasted_iota(jnp.int32, (LOW, LOW), 0).astype(F32).astype(BF16)
    one = jnp.ones((), BF16)
    zero = jnp.zeros((), BF16)
    code = code_ref[...]
    high = ((code >> 8) - 1).astype(F32)
    low = (code & (LOW - 1)).astype(F32)
    for g in range(code_ref.shape[0]):
        left = jnp.where(rows == high[g : g + 1, :].astype(BF16), one, zero)
        right = jnp.where(rows == low[g : g + 1, :].astype(BF16), one, zero)
        counts = lax.dot_general(left, right, (((1,), (1,)), ((), ())), preferred_element_type=F32)
        store_counts(counts.astype(BF16), out_ref, g * SLOTS)


def slot_counts(code, positions, part, before=None):
    groups, width = code.shape
    step = 16
    steps = groups // step // 2
    earlier = () if before is None else (before,)
    return pl.pallas_call(
        slot_kernel,
        grid=(steps,),
        in_specs=[pl.BlockSpec((step, width), lambda i: (i + part * steps, 0))]
        + [pl.BlockSpec(memory_space=pl.ANY)] * len(earlier),
        out_specs=(
            pl.BlockSpec((step * SLOTS, positions), lambda i: (i + part * steps, 0)),
            in_vmem(1)[0],
        ),
        out_shape=(pltpu.HBM((groups * SLOTS, positions), BF16), TOKEN),
        input_output_aliases={1: 0} if earlier else {},
        compiler_params=pltpu.CompilerParams(vmem_limit_bytes=10 * MIB),
        cost_estimate=pl.CostEstimate(
            flops=groups * LOW * LOW * LOW,
            transcendentals=0,
            bytes_accessed=groups // 2 * SLOTS * positions * 2,
        ),
        name="slot_counts",
    )(code, *earlier)


def weight_kernel(at_ref, *refs):
    blocks, (mine_ref, other_ref, first_ref, second_ref, token_ref) = refs[:-5], refs[-5:]
    token_ref[...] = jnp.zeros(token_ref.shape, jnp.int32)
    x, core = at_ref[0], at_ref[1]
    half = first_ref.shape[1] // 4
    for i, block in enumerate(blocks):
        chip = (x + i // 2) & (CHIPS - 1)
        column = 2 * (chip & 1) + (core if i % 2 == 0 else 1 - core)
        for side in range(2):
            start = pl.multiple_of(half * (core if side == 0 else 1 - core), half)
            at = pl.multiple_of((2 * side + (chip >> 1)) * half, half)
            first_ref[column, pl.ds(at, half), :] = block[pl.ds(start, half), :]
    columns = mine_ref.shape[1]

    @pl.when(x < 2)
    def _():
        second_ref[:, :columns] = mine_ref[...]
        second_ref[:, columns:] = other_ref[...]

    @pl.when(x >= 2)
    def _():
        second_ref[:, :columns] = other_ref[...]
        second_ref[:, columns:] = mine_ref[...]


def assemble(at, blocks, mine, other):
    k, width = blocks[0].shape
    first = (CHIPS, 2 * k, width)
    second = (mine.shape[0], 2 * mine.shape[1])
    return pl.pallas_call(
        weight_kernel,
        grid_spec=pltpu.PrefetchScalarGridSpec(
            num_scalar_prefetch=1,
            grid=(1,),
            in_specs=[
                pl.BlockSpec(b.shape, lambda i, at: (0, 0), pipeline_mode=pl.Buffered(1))
                for b in (*blocks, mine, other)
            ],
            out_specs=tuple(in_vmem(3)),
        ),
        out_shape=(jax.ShapeDtypeStruct(first, BF16), jax.ShapeDtypeStruct(second, BF16), TOKEN),
        compiler_params=pltpu.CompilerParams(vmem_limit_bytes=10 * MIB),
        name="assemble",
    )(at, *blocks, mine, other)


def column(row):
    shape = (row.shape[1], row.shape[1])
    diagonal = lax.broadcasted_iota(jnp.int32, shape, 0) == lax.broadcasted_iota(jnp.int32, shape, 1)
    return jnp.sum(jnp.where(diagonal, row.astype(F32), 0.0), axis=1, keepdims=True)


def dot(a, b):
    return jnp.dot(a, b, preferred_element_type=F32)


def load_rows(out_ref, data_ref, positions):
    for i, at in enumerate(positions):
        out_ref[i : i + 1, :] = data_ref[pl.ds(at, 1), :]


def mean_kernel(tokens, request_ref, place_ref, counts_ref, nodes_ref, *refs):
    pieces, (out_ref, data_ref, wide_ref, own_ref) = refs[tokens:-4], refs[-4:]
    tile, width = out_ref.shape[0], out_ref.shape[1] // 2

    @pl.when(pl.program_id(0) == 0)
    def _():
        start = 0
        for piece in pieces:
            data = piece[...]
            data_ref[start : start + piece.shape[0], :] = data
            wide_ref[start : start + piece.shape[0], :] = data.astype(F32)
            start += piece.shape[0]

    base = pl.program_id(0) * tile
    load_rows(own_ref, wide_ref, [place_ref[request_ref[base + i]] for i in range(tile)])
    size = nodes_ref[:, FAN + 1 : FAN + 2].astype(F32)
    total = dot(counts_ref[...], data_ref[...])
    out_ref[:, width:] = (total / size).astype(BF16)
    out_ref[:, :width] = own_ref[...].astype(BF16)


def own_and_mean(requests, places, counts, nodes, pieces, after):
    targets, positions = counts.shape
    width = pieces[0].shape[1]
    tile = 256
    return pl.pallas_call(
        functools.partial(mean_kernel, len(after)),
        grid_spec=pltpu.PrefetchScalarGridSpec(
            num_scalar_prefetch=2,
            grid=(targets // tile,),
            in_specs=[
                pl.BlockSpec((tile, positions), lambda i, r, p: (i, 0)),
                pl.BlockSpec((tile, SLOTS), lambda i, r, p: (i, 0)),
            ]
            + in_vmem(len(after) + len(pieces)),
            out_specs=pl.BlockSpec((tile, 2 * width), lambda i, r, p: (i, 0)),
            scratch_shapes=[
                pltpu.VMEM((positions, width), BF16),
                pltpu.VMEM((positions, width), F32),
                pltpu.VMEM((tile, width), F32),
            ],
        ),
        out_shape=pltpu.HBM((targets, 2 * width), BF16),
        compiler_params=pltpu.CompilerParams(vmem_limit_bytes=14 * MIB),
        cost_estimate=pl.CostEstimate(
            flops=4 * targets * positions * width,
            transcendentals=0,
            bytes_accessed=targets * positions * 2,
        ),
        name="own_and_mean",
    )(requests, places, pltpu.with_memory_space_constraint(counts, pltpu.HBM), nodes, *after, *pieces)


def project_into(self_ref, near_ref, start, mine_ref, other_ref, first_ref, second_ref):
    rows, k = mine_ref.shape
    tile = min(rows, 512)
    columns = self_ref.shape[1]
    for at in range(0, rows, tile):
        mine, other = mine_ref[at : at + tile, :], other_ref[at : at + tile, :]
        acc = jnp.zeros((tile, 2 * columns), F32)
        for h in range(first_ref.shape[0]):
            pre = dot(mine, first_ref[h, :k, :]) + dot(other, first_ref[h, k:, :])
            hidden = jnp.maximum(pre, 0.0).astype(BF16)
            width = hidden.shape[1]
            acc = acc + dot(hidden, second_ref[h * width : (h + 1) * width, :])
        self_ref[start + at : start + at + tile, :] = acc[:, :columns]
        near_ref[start + at : start + at + tile, :] = acc[:, columns:].astype(BF16)


def project_kernel(tokens, first_ref, second_ref, *refs):
    pieces, outs = refs[tokens:-2], refs[-2:]
    start = 0
    for mine, other in zip(pieces[::2], pieces[1::2]):
        project_into(*outs, start, mine, other, first_ref, second_ref)
        start += mine.shape[0]


def project(first, second, *pieces, after=()):
    rows = sum(p.shape[0] for p in pieces[::2])
    k, width = pieces[0].shape[1], second.shape[1] // 2
    return pl.pallas_call(
        functools.partial(project_kernel, len(after)),
        in_specs=in_vmem(2 + len(after) + len(pieces)),
        out_specs=tuple(in_vmem(2)),
        out_shape=(jax.ShapeDtypeStruct((rows, width), F32), jax.ShapeDtypeStruct((rows, width), BF16)),
        compiler_params=pltpu.CompilerParams(vmem_limit_bytes=8 * MIB),
        cost_estimate=pl.CostEstimate(
            flops=4 * rows * second.shape[0] * (k + width),
            transcendentals=0,
            bytes_accessed=rows * (2 * k + 3 * width) * 2,
        ),
        name="project",
    )(first, second, *after, *pieces)


def seed_kernel(place_ref, counts_ref, size_ref, first_ref, second_ref, *refs):
    pieces, far, (out_ref, self_ref, near_ref, own_ref) = refs[:4], refs[4:-4], refs[-4:]
    tile = out_ref.shape[0]
    block = pieces[0].shape[0]

    @pl.when(pl.program_id(0) == 0)
    def _():
        for out, (own, near) in ((self_ref, pieces[::2]), (near_ref, pieces[1::2])):
            out[:block, :] = own[...]
            out[block : 2 * block, :] = near[:block, :]
            out[3 * block :, :] = near[block:, :]
        start = 2 * block
        for mine, other in zip(far[::2], far[1::2]):
            project_into(self_ref, near_ref, start, mine, other, first_ref, second_ref)
            start += mine.shape[0]

    base = pl.program_id(0) * tile
    load_rows(own_ref, self_ref, [place_ref[base + i] for i in range(tile)])
    total = dot(counts_ref[...], near_ref[...])
    out_ref[...] = (own_ref[...] + total / column(size_ref[...])).astype(BF16)


def seeds(places, counts, sizes, first, second, own, near, far):
    targets, positions = counts.shape
    width = second.shape[1] // 2
    tile = 256
    return pl.pallas_call(
        seed_kernel,
        grid_spec=pltpu.PrefetchScalarGridSpec(
            num_scalar_prefetch=1,
            grid=(targets // tile,),
            in_specs=[
                pl.BlockSpec((tile, positions), lambda i, p: (i, 0)),
                pl.BlockSpec((1, tile), lambda i, p: (0, i)),
            ]
            + in_vmem(6 + len(far)),
            out_specs=pl.BlockSpec((tile, width), lambda i, p: (i, 0)),
            scratch_shapes=[
                pltpu.VMEM((positions, width), F32),
                pltpu.VMEM((positions, width), BF16),
                pltpu.VMEM((tile, width), F32),
            ],
        ),
        out_shape=jax.ShapeDtypeStruct((targets, width), BF16),
        compiler_params=pltpu.CompilerParams(vmem_limit_bytes=18 * MIB),
        cost_estimate=pl.CostEstimate(
            flops=2 * targets * positions * width,
            transcendentals=0,
            bytes_accessed=targets * positions * 2,
        ),
        name="seeds",
    )(places, pltpu.with_memory_space_constraint(counts, pltpu.HBM), sizes, first, second, *own, *near, *far)


def shards(
    store_feat,
    want_in,
    nbr_in,
    self_in,
    count_in,
    weight_one,
    want_hid,
    nbr_hid,
    self_hid,
    count_hid,
    weight_two,
):
    x = lax.axis_index("wt") * 2 + lax.axis_index("xlo")
    core = lax.axis_index("core")
    parts = want_in.shape[1]
    block = want_in.shape[2] // CHIPS
    half = store_feat.shape[1] // 2

    def mine(wanted):
        return lax.dynamic_slice_in_dim(wanted[0], block * x, block, 1).reshape(-1)

    def exchange(rows):
        pieces = rows.reshape(parts, block, rows.shape[1])
        return lax.all_to_all(pieces, "dom", 0, 0, tiled=True).reshape(rows.shape)

    together = lax.optimization_barrier
    positions = parts * block * CHIPS

    picked = store_feat.at[mine(want_in)].get(mode="promise_in_bounds")
    picked = lax.dynamic_slice_in_dim(picked, half * core, half, 1)
    fetched = exchange(picked)

    table = node_table(nbr_in.T, self_in[None], count_in[None])
    requests = mine(want_hid)
    nodes, counts, token = node_counts(requests, x, table, positions)
    fetched, token = together((fetched, token))
    below, above = send(fetched, UP), send(fetched, DOWN)
    code = codes(nbr_hid, count_hid, x)
    places = place(self_in, x)
    below, above, code, places = together((below, above, code, places))
    cut = below.shape[0] // 2
    far_low, far_high = send(below[:cut], UP), send(above[cut:], DOWN)
    counts_two, token_two = slot_counts(code, positions, 0)
    weight_one, token_two = together((weight_one, token_two))
    first_blocks = [weight_one] + [send(weight_one, pairs) for pairs in (DOWN, ACROSS, UP)]
    pieces = (fetched, above, far_low, far_high, below)
    ready = own_and_mean(requests, places, counts, nodes, pieces, (token, token_two))

    ready, weight_two, code, *first_blocks = together((ready, weight_two, code, *first_blocks))
    arrived = exchange(ready)
    other_rows = send(weight_two, ACROSS)
    counts_two, token = slot_counts(code, positions, 1, counts_two)
    first_blocks = [b for block in first_blocks for b in (block, swap(block))]
    own_at = place(self_hid, x)
    arrived, own_at, token, weight_two, other_rows, *first_blocks = together(
        (arrived, own_at, token, weight_two, other_rows, *first_blocks)
    )
    at = jnp.stack([x, core]).astype(jnp.int32)
    first, second, ready = assemble(at, first_blocks, weight_two, other_rows)
    cut = arrived.shape[0] // 2
    low, high = arrived[:cut], arrived[cut:]
    below_low, above_high = send(low, UP), send(high, DOWN)
    below_high, above_low = send(high, UP), send(low, DOWN)
    other = swap(arrived)
    below_low, above_high, other, ready = together((below_low, above_high, other, ready))
    far_low = send(below_low, UP)
    far_high = send(above_high, DOWN)
    own = project(first, second, arrived, other, after=(token, ready))
    below_high, above_low, *own = together((below_high, above_low, *own))
    near = []
    for piece in (above_low, above_high, below_low, below_high):
        near += [piece, swap(piece)]
    near = project(first, second, *near)
    far_low, far_high, *near = together((far_low, far_high, *near))
    far = (far_low, swap(far_low), far_high, swap(far_high))
    return seeds(own_at, counts_two, count_hid[None], first, second, own, near, far)


def solution(mesh):
    mesh = Mesh(mesh.devices.reshape(32, 2, 2, 2), ("dom", "xlo", "core", "wt"))
    columns = ("xlo", "core")
    return jax.shard_map(
        shards,
        mesh=mesh,
        in_specs=(
            P("dom", None),
            P("dom", None, None),
            P("dom", None),
            P("dom"),
            P("dom"),
            P("wt", columns),
            P("dom", None, None),
            P("dom", None),
            P("dom"),
            P("dom"),
            P("wt", columns),
        ),
        out_specs=P("dom", columns),
        check_vma=False,
    )
```

time: 1030 us -> 129 us (0.13)
  local copies, waits for them, and re-layouts: 636 us -> 19.9 us
  waiting for transfers between devices: 171 us -> 3.75 us
  matrix products: 110 us -> 0 us
  other arithmetic: 69.3 us -> 0.9 us
  Pallas kernels: 0 us -> 54 us
  starting transfers between devices: 19.4 us -> 49.7 us
  between operations: 13.7 us -> 0.25 us
    gather x44 -> x1, local copies, waits for them, and re-layouts: 620 us -> 4.98 us  [shards(): picked = store_feat.at[mine(want_in)].get(mode='promise_in_bounds')]
    all_gather x2 -> x0, waiting for transfers between devices: 113 us -> none  [the longest x1 82.8 us: sent_together(): whole = lax.all_gather(both, axis, axis=dim, tiled=True)]
    dot_general x22 -> x0, matrix products: 110 us -> none  [the longest x20 101 us: average(): jnp.einsum('tk,tkf->tf', valid_mask, gathered, preferred_element_type=jnp...]
    all_to_all x2, waiting for transfers between devices: 57.6 us -> 0.32 us  [exchange(): return lax.all_to_all(pieces, 'dom', 0, 0, tiled=True).reshape(rows.shape)]
    pallas_call x0 -> x9, Pallas kernels: none -> 54 us  [the longest x1 16.7 us: seeds(): pl.pallas_call(seed_kernel, grid_spec=pltpu.PrefetchScalarGridSpec(num_sc...]
    ppermute x0 -> x25, starting transfers between devices: none -> 27.6 us  [the longest x14 18.9 us: send(): return lax.ppermute(block, LINE, pairs)]
    select_n x24 -> x1, other arithmetic: 26.9 us -> 0.01 us  [shards(): picked = store_feat.at[mine(want_in)].get(mode='promise_in_bounds')]
    and x24 -> x1, other arithmetic: 17.7 us -> 0.01 us  [codes(): target = lax.broadcasted_iota(jnp.int32, at.shape, 0) & SLOTS - 1]
  transfers between devices with their start and end apart: 4 -> 27, of which waited for: 4 -> 8; matrix products, arithmetic and copies ran while one was open for 1% -> 3% of each run, Pallas kernels for 0% -> 29%
where the time goes in v2:
time: 129 us; the launch traced here: 128 us
  Pallas kernels  54 us (42%)
  starting transfers between devices  49.7 us (39%)
  local copies, waits for them, and re-layouts  19.9 us (15%)
  waiting for transfers between devices  3.75 us (3%)
    all_to_all x2, starting transfers between devices, exchange(): return lax.all_to_all(pieces, 'dom', 0, 0, tiled=True).reshape(rows.shape)  22.1 us
    ppermute x14, starting transfers between devices, send(): return lax.ppermute(block, LINE, pairs)  18.9 us
    pallas_call x1, Pallas kernels, seeds(): pl.pallas_call(seed_kernel, grid_spec=pltpu.PrefetchScalarGridSpec(num_sc...  16.7 us
    pallas_call x2, Pallas kernels, slot_counts(): pl.pallas_call(slot_kernel, grid=(steps,), in_specs=[pl.BlockSpec((step,...  10 us
    unnamed x42, local copies, waits for them, and re-layouts  9.13 us
    pallas_call x1, Pallas kernels, own_and_mean(): pl.pallas_call(functools.partial(mean_kernel, len(after)), grid_spec=pltp...  8.77 us
    ppermute x11, starting transfers between devices, swap(): return lax.ppermute(block, 'core', SWAP)  8.65 us
    pallas_call x2, Pallas kernels, project(): pl.pallas_call(functools.partial(project_kernel, len(after)), in_specs=in...  8.35 us
  transfers between devices with their start and end apart: 27, of which 8 were waited for; matrix products, arithmetic and copies ran while one was open for 3% of the time, Pallas kernels for 29%

profile of v2, /device:TPU:1, one launch (start us, length us, event | category | flops | bytes accessed | tf_op | source)
XLA Modules:
  0.0 128.4 jit_solution(2320155468154607850)
XLA Ops:
  0.0 1.0 constant_dynamic-slice_fusion.1
  1.1 0.5 copy-done
  1.6 5.0 %gather_fusion = bf16[1024,256]{1,0:T(8,128)(2,1)} fusion(bf16[4096,256]{1,0:T(8,128)(2,1)S(1)} %copy-done, s32[1024]{0:T(1024)S(1)} %broadcast_clamp_fusion), kind=kCustom, calls=%fused_computation | custom fusion | bytes 1052672 | tf_op jit(solution)/shard_map/gather | solution.py:443
  6.6 1.7 %constant_dynamic-slice_fusion = bf16[1024,128]{1,0:T(8,128)(2,1)} fusion(bf16[1024,256]{1,0:T(8,128)(2,1)} %gather_fusion, s32[]{:T(128)S(6)} %select_n.23), kind=kLoop, calls=%fused_computation.8 | loop fusion | bytes 524292 | tf_op jit(solution)/shard_map/dynamic_slice | solution.py:444
  8.3 12.0 %all-to-all-start = ((bf16[32,32,128]{2,1,0:T(8,128)(2,1)}), bf16[32,32,128]{2,1,0:T(8,128)(2,1)S(1)}, u32[]{:S(2)}, u32[]{:S(2)}) async-start(bf16[32,32,128]{2,1,0:T(8,128)(2,1)} %bitcast.1), calls=%async_computation | async-start | bytes 524288 | tf_op jit(solution)/shard_map/all_to_all | solution.py:438
  20.4 1.9 %node_table.1.table_ref = s32[8192,16]{1,0:T(8,128)S(1)} custom-call(s32[10,8192]{1,0:T(8,128)S(1)} %bitcast.17, s32[1,8192]{1,0:T(1,128)S(1)} %bitcast.18, s32[1,8192]{1,0:T(1,128)S(1)} %bitcast.19), custom_call_target="tpu_custom_call" | custom-call | tf_op jit(solution)/shard_map/node_table/pallas_call | solution.py:97
  22.3 6.5 %node_counts.1 = (s32[1024,16]{1,0:T(8,128)S(1)}, bf16[1024,4096]{1,0:T(8,128)(2,1)}, s32[8,128]{1,0:T(8,128)S(1)}) custom-call(s32[1024]{0:T(1024)S(1)} %reshape.57.request_ref, s32[1]{0:T(128)} %bitcast.3.x_ref, s32[8192,16]{1,0:T(8,128)S(1)} %node_table.1.table_ref), custom_call_target="tpu_custom_call" | custom-call | flops 2147483648 | bytes 8388608 | tf_op jit(solution)/shard_map/node_counts/pallas_call | solution.py:127
  28.9 0.8 copy-done.5
  30.0 1.2 collective-permute-start
  31.2 1.5 %collective-permute-start.1 = (bf16[1024,128]{1,0:T(8,128)(2,1)S(1)}, bf16[1024,128]{1,0:T(8,128)(2,1)S(1)}, u32[]{:S(2)}, u32[]{:S(2)}) collective-permute-start(bf16[1024,128]{1,0:T(8,128)(2,1)S(1)} %bitcast.15), channel_id=1, source_target_pairs={{0,5},{4,0},{1,4},{5,1},{2,7},{6,2},{3,6},{7,3},{8,13},{12,8},{9,1... | collective-permute-start | bytes 786440 | tf_op jit(solution)/shard_map/ppermute | solution.py:37
  32.7 1.3 %copy.14 = s32[2048,16]{1,0:T(8,128)} copy(s32[2048,16]{0,1:T(8,128)S(1)} %and_add_fusion) | data formatting | bytes 262144 | tf_op jit(solution)/shard_map/add | solution.py:159
  34.1 1.6 %reshape.62.code_ref = s32[128,256]{1,0:T(8,128)S(1)} reshape(s32[2048,16]{1,0:T(8,128)} %copy.14) | data formatting | bytes 262144 | tf_op jit(solution)/shard_map/reshape | solution.py:159
  35.7 0.7 collective-permute-done.refs_6_
  36.4 1.3 %collective-permute-start.2 = (bf16[512,128]{1,0:T(8,128)(2,1)S(1)}, bf16[512,128]{1,0:T(8,128)(2,1)S(1)}, u32[]{:S(2)}, u32[]{:S(2)}) collective-permute-start(bf16[512,128]{1,0:T(8,128)(2,1)S(1)} %slice.12), channel_id=1, source_target_pairs={{0,4},{4,1},{1,5},{5,0},{2,6},{6,3},{3,7},{7,2},{8,12},{12,9},{9,1... | collective-permute-start | bytes 393224 | tf_op jit(solution)/shard_map/ppermute | solution.py:37
  37.7 1.6 %collective-permute-start.3 = (bf16[512,128]{1,0:T(8,128)(2,1)S(1)}, bf16[512,128]{1,0:T(8,128)(2,1)S(1)}, u32[]{:S(2)}, u32[]{:S(2)}) collective-permute-start(bf16[512,128]{1,0:T(8,128)(2,1)S(1)} %slice.13), channel_id=1, source_target_pairs={{0,5},{4,0},{1,4},{5,1},{2,7},{6,2},{3,6},{7,3},{8,13},{12,8},{9,1... | collective-permute-start | bytes 393224 | tf_op jit(solution)/shard_map/ppermute | solution.py:37
  39.3 5.0 %slot_counts.2 = (bf16[2048,4096]{1,0:T(8,128)(2,1)}, s32[8,128]{1,0:T(8,128)S(1)}) custom-call(s32[128,256]{1,0:T(8,128)S(1)} %reshape.62.code_ref), custom_call_target="tpu_custom_call" | custom-call | flops 2147483648 | bytes 8388608 | tf_op jit(solution)/shard_map/slot_counts/pallas_call | solution.py:183
  44.3 1.5 %collective-permute-start.4 = (bf16[256,256]{1,0:T(8,128)(2,1)S(1)}, bf16[256,256]{1,0:T(8,128)(2,1)}, u32[]{:S(2)}, u32[]{:S(2)}) collective-permute-start(bf16[256,256]{1,0:T(8,128)(2,1)S(1)} %copy-done.8), channel_id=1, source_target_pairs={{0,5},{4,0},{1,4},{5,1},{2,7},{6,2},{3,6},{7,3},{8,13},{12,8},{9,1... | collective-permute-start | bytes 393224 | tf_op jit(solution)/shard_map/ppermute | solution.py:37
  46.4 8.8 %own_and_mean.1 = bf16[1024,256]{1,0:T(8,128)(2,1)} custom-call(s32[1024]{0:T(1024)S(1)} %reshape.57.request_ref, s32[8192]{0:T(1024)S(1)} %and_or_fusion.place_ref, bf16[1024,4096]{1,0:T(8,128)(2,1)} %get-tuple-element.62.counts_ref, s32[1024,16]{1,0:T(8,128)S(1)} %copy-done.6, s32[8,128]{1,0:T(8,128)S(1)} %get-tuple-element.64.refs_0_, ...), custom_call_target="tpu_custom_call" | custom-call | flops 2147483648 | bytes 8388608 | tf_op jit(solution)/shard_map/own_and_mean/pallas_call | solution.py:290
  55.2 10.1 %all-to-all-start.1 = ((bf16[32,32,256]{2,1,0:T(8,128)(2,1)}), bf16[32,32,256]{2,1,0:T(8,128)(2,1)S(1)}, u32[]{:S(2)}, u32[]{:S(2)}) async-start(bf16[32,32,256]{2,1,0:T(8,128)(2,1)} %bitcast.21), calls=%async_computation.1 | async-start | bytes 1048576 | tf_op jit(solution)/shard_map/all_to_all | solution.py:438
  65.3 3.3 %collective-permute-start.7 = (bf16[1024,256]{1,0:T(8,128)(2,1)S(1)}, bf16[1024,256]{1,0:T(8,128)(2,1)S(1)}, u32[]{:S(2)}, u32[]{:S(2)}) collective-permute-start(bf16[1024,256]{1,0:T(8,128)(2,1)S(1)} %copy-done.2), channel_id=1, source_target_pairs={{0,1},{4,5},{1,0},{5,4},{2,3},{6,7},{3,2},{7,6},{8,9},{12,13},{9,8... | collective-permute-start | bytes 1572872 | tf_op jit(solution)/shard_map/ppermute | solution.py:37
  68.6 0.7 and_or_fusion.1.place_ref
  69.3 4.1 %collective-permute-start.10 = (bf16[256,256]{1,0:T(8,128)(2,1)}, bf16[256,256]{1,0:T(8,128)(2,1)S(1)}, u32[]{:S(2)}, u32[]{:S(2)}) collective-permute-start(bf16[256,256]{1,0:T(8,128)(2,1)} %collective-permute-done.5.refs_4_), channel_id=1, source_target_pairs={{0,2},{2,0},{1,3},{3,1},{4,6},{6,4},{5,7},{7,5},{8,10},{10,8},{9,1... | collective-permute-start | bytes 393224 | tf_op jit(solution)/shard_map/ppermute | solution.py:41
  74.0 5.0 %slot_counts.3 = (bf16[2048,4096]{1,0:T(8,128)(2,1)}, s32[8,128]{1,0:T(8,128)S(1)}) custom-call(s32[128,256]{1,0:T(8,128)S(1)} %reshape.62.code_ref, bf16[2048,4096]{1,0:T(8,128)(2,1)} %get-tuple-element.73.refs_0_), custom_call_target="tpu_custom_call", output_to_operand_aliasing={{0}: (1, {})} | custom-call | flops 2147483648 | bytes 8388608 | tf_op jit(solution)/shard_map/slot_counts/pallas_call | solution.py:183
  79.0 0.6 copy-done.18
  79.6 0.7 copy-done.10
  80.2 0.6 copy-done.12
  80.9 0.6 copy-done.14
  81.5 0.8 copy-done.3
  82.3 1.0 collective-permute-start.16
  83.3 2.1 %collective-permute-start.14 = (bf16[512,256]{1,0:T(8,128)(2,1)S(1)}, bf16[512,256]{1,0:T(8,128)(2,1)S(1)}, u32[]{:S(2)}, u32[]{:S(2)}) collective-permute-start(bf16[512,256]{1,0:T(8,128)(2,1)S(1)} %get-tuple-element.113), channel_id=1, source_target_pairs={{0,4},{4,1},{1,5},{5,0},{2,6},{6,3},{3,7},{7,2},{8,12},{12,9},{9,1... | collective-permute-start | bytes 786440 | tf_op jit(solution)/shard_map/ppermute | solution.py:37
  85.4 0.7 collective-permute-start.15
  86.1 0.8 collective-permute-start.12
  86.9 1.9 %collective-permute-start.13 = (bf16[512,256]{1,0:T(8,128)(2,1)S(1)}, bf16[512,256]{1,0:T(8,128)(2,1)S(1)}, u32[]{:S(2)}, u32[]{:S(2)}) collective-permute-start(bf16[512,256]{1,0:T(8,128)(2,1)S(1)} %get-tuple-element.113), channel_id=1, source_target_pairs={{0,5},{4,0},{1,4},{5,1},{2,7},{6,2},{3,6},{7,3},{8,13},{12,8},{9,1... | collective-permute-start | bytes 786440 | tf_op jit(solution)/shard_map/ppermute | solution.py:37
  88.8 1.0 copy-done.4
  89.9 0.9 copy-done.11
  90.8 0.9 copy-done.13
  91.7 0.9 copy-done.15
  92.6 1.7 %assemble.1 = (bf16[4,512,256]{2,1,0:T(8,128)(2,1)S(1)}, bf16[1024,512]{1,0:T(8,128)(2,1)S(1)}, s32[8,128]{1,0:T(8,128)S(1)}) custom-call(s32[2]{0:T(128)S(1)} %pad_add_fusion.at_ref, bf16[256,256]{1,0:T(8,128)(2,1)S(1)} %copy-done.9, bf16[256,256]{1,0:T(8,128)(2,1)S(1)} %copy-done.13, bf16[256,256]{1,0:T(8,128)(2,1)} %collective-permute-done.4.refs_2_, ...), custom_call_target="tpu_custom_call" | custom-call | tf_op jit(solution)/shard_map/assemble/pallas_call | solution.py:233
  94.4 0.7 copy-done.19
  95.1 2.8 %project.2 = (f32[1024,256]{1,0:T(8,128)S(1)}, bf16[1024,256]{1,0:T(8,128)(2,1)S(1)}) custom-call(bf16[4,512,256]{2,1,0:T(8,128)(2,1)S(1)} %get-tuple-element.92.first_ref, bf16[1024,512]{1,0:T(8,128)(2,1)S(1)} %get-tuple-element.93.second_ref, s32[8,128]{1,0:T(8,128)S(1)} %copy-done.19, s32[8,128]{1,0:T(8,128)S(1)} %get-tuple-element.97.refs_1_, ...), custom_call_target="tpu_custom_call" | custom-call | flops 2147483648 | bytes 2621440 | tf_op jit(solution)/shard_map/project/pallas_call | solution.py:345
  98.1 0.5 collective-permute-done.13.refs_0_
  98.6 1.1 collective-permute-start.19
  100.3 0.6 collective-permute-start.17
  100.9 2.0 %collective-permute-start.18 = (bf16[512,256]{1,0:T(8,128)(2,1)S(1)}, bf16[512,256]{1,0:T(8,128)(2,1)S(1)}, u32[]{:S(2)}, u32[]{:S(2)}) collective-permute-start(bf16[512,256]{1,0:T(8,128)(2,1)S(1)} %collective-permute-done.15.refs_2_), channel_id=1, source_target_pairs={{0,5},{4,0},{1,4},{5,1},{2,7},{6,2},{3,6},{7,3},{8,13},{12,8},{9,1... | collective-permute-start | bytes 786440 | tf_op jit(solution)/shard_map/ppermute | solution.py:37
  103.0 5.5 %project.3 = (f32[2048,256]{1,0:T(8,128)S(1)}, bf16[2048,256]{1,0:T(8,128)(2,1)S(1)}) custom-call(bf16[4,512,256]{2,1,0:T(8,128)(2,1)S(1)} %get-tuple-element.92.first_ref, bf16[1024,512]{1,0:T(8,128)(2,1)S(1)} %get-tuple-element.93.second_ref, bf16[512,256]{1,0:T(8,128)(2,1)S(1)} %collective-permute-done.13.refs_0_, ...), custom_call_target="tpu_custom_call" | custom-call | flops 4294967296 | bytes 5242880 | tf_op jit(solution)/shard_map/project/pallas_call | solution.py:345
  108.8 1.4 %collective-permute-start.23 = (bf16[512,256]{1,0:T(8,128)(2,1)S(1)}, bf16[512,256]{1,0:T(8,128)(2,1)S(1)}, u32[]{:S(2)}, u32[]{:S(2)}) collective-permute-start(bf16[512,256]{1,0:T(8,128)(2,1)S(1)} %collective-permute-done.17.refs_4_), channel_id=1, source_target_pairs={{0,2},{2,0},{1,3},{3,1},{4,6},{6,4},{5,7},{7,5},{8,10},{10,8},{9,1... | collective-permute-start | bytes 786440 | tf_op jit(solution)/shard_map/ppermute | solution.py:41
  110.2 1.2 collective-permute-done.23.refs_5_
  111.7 16.7 %seeds.1 = bf16[2048,256]{1,0:T(8,128)(2,1)} custom-call(s32[2048]{0:T(1024)S(1)} %and_or_fusion.1.place_ref, bf16[2048,4096]{1,0:T(8,128)(2,1)} %get-tuple-element.81.counts_ref, s32[1,2048]{1,0:T(1,128)S(1)} %bitcast.20, bf16[4,512,256]{2,1,0:T(8,128)(2,1)S(1)} %get-tuple-element.92.first_ref, bf16[1024,512]{1,0:T(8,128)(2,1)S(1)} %get-tuple-element.93.second_ref, ...), custom_call_target="tpu_custom_call" | custom-call | flops 4294967296 | bytes 16777216 | tf_op jit(solution)/shard_map/seeds/pallas_call | solution.py:386
  (74 shorter events, 3.6 us)
Async XLA Ops:
  0.0 1.6 %copy-start = (bf16[4096,256]{1,0:T(8,128)(2,1)S(1)}, bf16[4096,256]{1,0:T(8,128)(2,1)}, u32[]{:S(2)}) copy-start(bf16[4096,256]{1,0:T(8,128)(2,1)} %param.11) | copy-start | bytes 6291460
  0.0 20.4 %copy-start.1 = (s32[8192,10]{0,1:T(8,128)S(1)}, s32[8192,10]{0,1:T(8,128)}, u32[]{:S(2)}) copy-start(s32[8192,10]{0,1:T(8,128)} %param.13) | copy-start | bytes 983044
  0.0 20.4 %copy-start.7 = (s32[8192]{0:T(1024)S(1)}, s32[8192]{0:T(1024)}, u32[]{:S(2)}) copy-start(s32[8192]{0:T(1024)} %param.14) | copy-start | bytes 98308
  0.0 20.4 %copy-start.16 = (s32[8192]{0:T(1024)S(1)}, s32[8192]{0:T(1024)}, u32[]{:S(2)}) copy-start(s32[8192]{0:T(1024)} %param.15) | copy-start | bytes 98308
  8.3 21.7 %all-to-all-start = ((bf16[32,32,128]{2,1,0:T(8,128)(2,1)}), bf16[32,32,128]{2,1,0:T(8,128)(2,1)S(1)}, u32[]{:S(2)}, u32[]{:S(2)}) async-start(bf16[32,32,128]{2,1,0:T(8,128)(2,1)} %bitcast.1), calls=%async_computation | async-start | bytes 524288 | tf_op jit(solution)/shard_map/all_to_all | solution.py:438
  22.3 10.3 %copy-start.17 = (s32[2048]{0:T(1024)S(1)}, s32[2048]{0:T(1024)}, u32[]{:S(2)}) copy-start(s32[2048]{0:T(1024)} %param.20) | copy-start | bytes 24580
  22.3 10.3 %copy-start.20 = (s32[2048,15]{0,1:T(8,128)S(1)}, s32[2048,15]{0,1:T(8,128)}, u32[]{:S(2)}) copy-start(s32[2048,15]{0,1:T(8,128)} %param.18) | copy-start | bytes 368644
  28.9 0.8 copy-start.5
  30.0 6.4 %collective-permute-start = (bf16[1024,128]{1,0:T(8,128)(2,1)S(1)}, bf16[1024,128]{1,0:T(8,128)(2,1)S(1)}, u32[]{:S(2)}, u32[]{:S(2)}) collective-permute-start(bf16[1024,128]{1,0:T(8,128)(2,1)S(1)} %bitcast.14), channel_id=1, source_target_pairs={{0,4},{4,1},{1,5},{5,0},{2,6},{6,3},{3,7},{7,2},{8,12},{12,9},{9,1... | collective-permute-start | bytes 786440 | tf_op jit(solution)/shard_map/ppermute | solution.py:37
  31.2 5.2 %collective-permute-start.1 = (bf16[1024,128]{1,0:T(8,128)(2,1)S(1)}, bf16[1024,128]{1,0:T(8,128)(2,1)S(1)}, u32[]{:S(2)}, u32[]{:S(2)}) collective-permute-start(bf16[1024,128]{1,0:T(8,128)(2,1)S(1)} %bitcast.15), channel_id=1, source_target_pairs={{0,5},{4,0},{1,4},{5,1},{2,7},{6,2},{3,6},{7,3},{8,13},{12,8},{9,1... | collective-permute-start | bytes 786440 | tf_op jit(solution)/shard_map/ppermute | solution.py:37
  35.7 8.6 %copy-start.8 = (bf16[256,256]{1,0:T(8,128)(2,1)S(1)}, bf16[256,256]{1,0:T(8,128)(2,1)}, u32[]{:S(2)}) copy-start(bf16[256,256]{1,0:T(8,128)(2,1)} %refs_0_) | copy-start | bytes 393220
  35.7 10.7 %copy-start.6 = (s32[1024,16]{1,0:T(8,128)S(1)}, s32[1024,16]{1,0:T(8,128)}, u32[]{:S(2)}) copy-start(s32[1024,16]{1,0:T(8,128)} %copy-done.5) | copy-start | bytes 196612
  36.4 10.0 %collective-permute-start.2 = (bf16[512,128]{1,0:T(8,128)(2,1)S(1)}, bf16[512,128]{1,0:T(8,128)(2,1)S(1)}, u32[]{:S(2)}, u32[]{:S(2)}) collective-permute-start(bf16[512,128]{1,0:T(8,128)(2,1)S(1)} %slice.12), channel_id=1, source_target_pairs={{0,4},{4,1},{1,5},{5,0},{2,6},{6,3},{3,7},{7,2},{8,12},{12,9},{9,1... | collective-permute-start | bytes 393224 | tf_op jit(solution)/shard_map/ppermute | solution.py:37
  37.7 8.7 %collective-permute-start.3 = (bf16[512,128]{1,0:T(8,128)(2,1)S(1)}, bf16[512,128]{1,0:T(8,128)(2,1)S(1)}, u32[]{:S(2)}, u32[]{:S(2)}) collective-permute-start(bf16[512,128]{1,0:T(8,128)(2,1)S(1)} %slice.13), channel_id=1, source_target_pairs={{0,5},{4,0},{1,4},{5,1},{2,7},{6,2},{3,6},{7,3},{8,13},{12,8},{9,1... | collective-permute-start | bytes 393224 | tf_op jit(solution)/shard_map/ppermute | solution.py:37
  44.3 10.9 %collective-permute-start.4 = (bf16[256,256]{1,0:T(8,128)(2,1)S(1)}, bf16[256,256]{1,0:T(8,128)(2,1)}, u32[]{:S(2)}, u32[]{:S(2)}) collective-permute-start(bf16[256,256]{1,0:T(8,128)(2,1)S(1)} %copy-done.8), channel_id=1, source_target_pairs={{0,5},{4,0},{1,4},{5,1},{2,7},{6,2},{3,6},{7,3},{8,13},{12,8},{9,1... | collective-permute-start | bytes 393224 | tf_op jit(solution)/shard_map/ppermute | solution.py:37
  45.8 9.4 %collective-permute-start.5 = (bf16[256,256]{1,0:T(8,128)(2,1)S(1)}, bf16[256,256]{1,0:T(8,128)(2,1)}, u32[]{:S(2)}, u32[]{:S(2)}) collective-permute-start(bf16[256,256]{1,0:T(8,128)(2,1)S(1)} %copy-done.8), channel_id=1, source_target_pairs={{0,1},{4,5},{1,0},{5,4},{2,3},{6,7},{3,2},{7,6},{8,9},{12,13},{9,8... | collective-permute-start | bytes 393224 | tf_op jit(solution)/shard_map/ppermute | solution.py:37
  46.1 9.1 %collective-permute-start.6 = (bf16[256,256]{1,0:T(8,128)(2,1)S(1)}, bf16[256,256]{1,0:T(8,128)(2,1)}, u32[]{:S(2)}, u32[]{:S(2)}) collective-permute-start(bf16[256,256]{1,0:T(8,128)(2,1)S(1)} %copy-done.8), channel_id=1, source_target_pairs={{0,4},{4,1},{1,5},{5,0},{2,6},{6,3},{3,7},{7,2},{8,12},{12,9},{9,1... | collective-permute-start | bytes 393224 | tf_op jit(solution)/shard_map/ppermute | solution.py:37
  46.4 18.9 %copy-start.2 = (bf16[1024,256]{1,0:T(8,128)(2,1)S(1)}, bf16[1024,256]{1,0:T(8,128)(2,1)}, u32[]{:S(2)}) copy-start(bf16[1024,256]{1,0:T(8,128)(2,1)} %refs_8_) | copy-start | bytes 1572868
  55.2 27.1 %all-to-all-start.1 = ((bf16[32,32,256]{2,1,0:T(8,128)(2,1)}), bf16[32,32,256]{2,1,0:T(8,128)(2,1)S(1)}, u32[]{:S(2)}, u32[]{:S(2)}) async-start(bf16[32,32,256]{2,1,0:T(8,128)(2,1)} %bitcast.21), calls=%async_computation.1 | async-start | bytes 1048576 | tf_op jit(solution)/shard_map/all_to_all | solution.py:438
  65.3 16.3 %collective-permute-start.7 = (bf16[1024,256]{1,0:T(8,128)(2,1)S(1)}, bf16[1024,256]{1,0:T(8,128)(2,1)S(1)}, u32[]{:S(2)}, u32[]{:S(2)}) collective-permute-start(bf16[1024,256]{1,0:T(8,128)(2,1)S(1)} %copy-done.2), channel_id=1, source_target_pairs={{0,1},{4,5},{1,0},{5,4},{2,3},{6,7},{3,2},{7,6},{8,9},{12,13},{9,8... | collective-permute-start | bytes 1572872 | tf_op jit(solution)/shard_map/ppermute | solution.py:37
  69.3 10.3 %collective-permute-start.10 = (bf16[256,256]{1,0:T(8,128)(2,1)}, bf16[256,256]{1,0:T(8,128)(2,1)S(1)}, u32[]{:S(2)}, u32[]{:S(2)}) collective-permute-start(bf16[256,256]{1,0:T(8,128)(2,1)} %collective-permute-done.5.refs_4_), channel_id=1, source_target_pairs={{0,2},{2,0},{1,3},{3,1},{4,6},{6,4},{5,7},{7,5},{8,10},{10,8},{9,1... | collective-permute-start | bytes 393224 | tf_op jit(solution)/shard_map/ppermute | solution.py:41
  73.3 6.2 %collective-permute-start.11 = (bf16[256,256]{1,0:T(8,128)(2,1)}, bf16[256,256]{1,0:T(8,128)(2,1)S(1)}, u32[]{:S(2)}, u32[]{:S(2)}) collective-permute-start(bf16[256,256]{1,0:T(8,128)(2,1)} %collective-permute-done.6.refs_6_), channel_id=1, source_target_pairs={{0,2},{2,0},{1,3},{3,1},{4,6},{6,4},{5,7},{7,5},{8,10},{10,8},{9,1... | collective-permute-start | bytes 393224 | tf_op jit(solution)/shard_map/ppermute | solution.py:41
  73.4 6.8 %collective-permute-start.8 = (bf16[256,256]{1,0:T(8,128)(2,1)}, bf16[256,256]{1,0:T(8,128)(2,1)S(1)}, u32[]{:S(2)}, u32[]{:S(2)}) collective-permute-start(bf16[256,256]{1,0:T(8,128)(2,1)} %refs_0_), channel_id=1, source_target_pairs={{0,2},{2,0},{1,3},{3,1},{4,6},{6,4},{5,7},{7,5},{8,10},{10,8},{9,1... | collective-permute-start | bytes 393224 | tf_op jit(solution)/shard_map/ppermute | solution.py:41
  73.8 7.0 %collective-permute-start.9 = (bf16[256,256]{1,0:T(8,128)(2,1)}, bf16[256,256]{1,0:T(8,128)(2,1)S(1)}, u32[]{:S(2)}, u32[]{:S(2)}) collective-permute-start(bf16[256,256]{1,0:T(8,128)(2,1)} %collective-permute-done.4.refs_2_), channel_id=1, source_target_pairs={{0,2},{2,0},{1,3},{3,1},{4,6},{6,4},{5,7},{7,5},{8,10},{10,8},{9,1... | collective-permute-start | bytes 393224 | tf_op jit(solution)/shard_map/ppermute | solution.py:41
  73.9 14.9 %copy-start.9 = (bf16[256,256]{1,0:T(8,128)(2,1)S(1)}, bf16[256,256]{1,0:T(8,128)(2,1)}, u32[]{:S(2)}) copy-start(bf16[256,256]{1,0:T(8,128)(2,1)} %refs_0_) | copy-start | bytes 393220
  78.9 0.6 copy-start.18
  79.5 0.7 copy-start.10
  80.2 0.6 copy-start.12
  80.9 0.6 copy-start.14
  81.5 0.8 copy-start.3
  82.3 12.0 %collective-permute-start.16 = (bf16[1024,256]{1,0:T(8,128)(2,1)S(1)}, bf16[1024,256]{1,0:T(8,128)(2,1)S(1)}, u32[]{:S(2)}, u32[]{:S(2)}) collective-permute-start(bf16[1024,256]{1,0:T(8,128)(2,1)S(1)} %bitcast.11), channel_id=1, source_target_pairs={{0,2},{2,0},{1,3},{3,1},{4,6},{6,4},{5,7},{7,5},{8,10},{10,8},{9,1... | collective-permute-start | bytes 1572872 | tf_op jit(solution)/shard_map/ppermute | solution.py:41
  83.3 11.0 %collective-permute-start.14 = (bf16[512,256]{1,0:T(8,128)(2,1)S(1)}, bf16[512,256]{1,0:T(8,128)(2,1)S(1)}, u32[]{:S(2)}, u32[]{:S(2)}) collective-permute-start(bf16[512,256]{1,0:T(8,128)(2,1)S(1)} %get-tuple-element.113), channel_id=1, source_target_pairs={{0,4},{4,1},{1,5},{5,0},{2,6},{6,3},{3,7},{7,2},{8,12},{12,9},{9,1... | collective-permute-start | bytes 786440 | tf_op jit(solution)/shard_map/ppermute | solution.py:37
  85.4 8.9 %collective-permute-start.15 = (bf16[512,256]{1,0:T(8,128)(2,1)S(1)}, bf16[512,256]{1,0:T(8,128)(2,1)S(1)}, u32[]{:S(2)}, u32[]{:S(2)}) collective-permute-start(bf16[512,256]{1,0:T(8,128)(2,1)S(1)} %get-tuple-element.114), channel_id=1, source_target_pairs={{0,5},{4,0},{1,4},{5,1},{2,7},{6,2},{3,6},{7,3},{8,13},{12,8},{9,1... | collective-permute-start | bytes 786440 | tf_op jit(solution)/shard_map/ppermute | solution.py:37
  86.1 12.0 %collective-permute-start.12 = (bf16[512,256]{1,0:T(8,128)(2,1)S(1)}, bf16[512,256]{1,0:T(8,128)(2,1)S(1)}, u32[]{:S(2)}, u32[]{:S(2)}) collective-permute-start(bf16[512,256]{1,0:T(8,128)(2,1)S(1)} %get-tuple-element.114), channel_id=1, source_target_pairs={{0,4},{4,1},{1,5},{5,0},{2,6},{6,3},{3,7},{7,2},{8,12},{12,9},{9,1... | collective-permute-start | bytes 786440 | tf_op jit(solution)/shard_map/ppermute | solution.py:37
  86.9 11.7 %collective-permute-start.13 = (bf16[512,256]{1,0:T(8,128)(2,1)S(1)}, bf16[512,256]{1,0:T(8,128)(2,1)S(1)}, u32[]{:S(2)}, u32[]{:S(2)}) collective-permute-start(bf16[512,256]{1,0:T(8,128)(2,1)S(1)} %get-tuple-element.113), channel_id=1, source_target_pairs={{0,5},{4,0},{1,4},{5,1},{2,7},{6,2},{3,6},{7,3},{8,13},{12,8},{9,1... | collective-permute-start | bytes 786440 | tf_op jit(solution)/shard_map/ppermute | solution.py:37
  88.8 1.0 copy-start.4
  89.9 0.9 copy-start.11
  90.8 0.9 copy-start.13
  91.7 0.9 copy-start.15
  94.4 0.7 copy-start.19
  98.6 2.3 %collective-permute-start.19 = (bf16[512,256]{1,0:T(8,128)(2,1)S(1)}, bf16[512,256]{1,0:T(8,128)(2,1)S(1)}, u32[]{:S(2)}, u32[]{:S(2)}) collective-permute-start(bf16[512,256]{1,0:T(8,128)(2,1)S(1)} %collective-permute-done.13.refs_0_), channel_id=1, source_target_pairs={{0,2},{2,0},{1,3},{3,1},{4,6},{6,4},{5,7},{7,5},{8,10},{10,8},{9,1... | collective-permute-start | bytes 786440 | tf_op jit(solution)/shard_map/ppermute | solution.py:41
  99.7 3.2 %collective-permute-start.22 = (bf16[512,256]{1,0:T(8,128)(2,1)S(1)}, bf16[512,256]{1,0:T(8,128)(2,1)S(1)}, u32[]{:S(2)}, u32[]{:S(2)}) collective-permute-start(bf16[512,256]{1,0:T(8,128)(2,1)S(1)} %collective-permute-done.12.refs_6_), channel_id=1, source_target_pairs={{0,2},{2,0},{1,3},{3,1},{4,6},{6,4},{5,7},{7,5},{8,10},{10,8},{9,1... | collective-permute-start | bytes 786440 | tf_op jit(solution)/shard_map/ppermute | solution.py:41
  99.8 3.2 %collective-permute-start.20 = (bf16[512,256]{1,0:T(8,128)(2,1)S(1)}, bf16[512,256]{1,0:T(8,128)(2,1)S(1)}, u32[]{:S(2)}, u32[]{:S(2)}) collective-permute-start(bf16[512,256]{1,0:T(8,128)(2,1)S(1)} %collective-permute-done.15.refs_2_), channel_id=1, source_target_pairs={{0,2},{2,0},{1,3},{3,1},{4,6},{6,4},{5,7},{7,5},{8,10},{10,8},{9,1... | collective-permute-start | bytes 786440 | tf_op jit(solution)/shard_map/ppermute | solution.py:41
  100.3 2.7 %collective-permute-start.21 = (bf16[512,256]{1,0:T(8,128)(2,1)S(1)}, bf16[512,256]{1,0:T(8,128)(2,1)S(1)}, u32[]{:S(2)}, u32[]{:S(2)}) collective-permute-start(bf16[512,256]{1,0:T(8,128)(2,1)S(1)} %collective-permute-done.14.refs_4_), channel_id=1, source_target_pairs={{0,2},{2,0},{1,3},{3,1},{4,6},{6,4},{5,7},{7,5},{8,10},{10,8},{9,1... | collective-permute-start | bytes 786440 | tf_op jit(solution)/shard_map/ppermute | solution.py:41
  100.3 8.6 %collective-permute-start.17 = (bf16[512,256]{1,0:T(8,128)(2,1)S(1)}, bf16[512,256]{1,0:T(8,128)(2,1)S(1)}, u32[]{:S(2)}, u32[]{:S(2)}) collective-permute-start(bf16[512,256]{1,0:T(8,128)(2,1)S(1)} %collective-permute-done.14.refs_4_), channel_id=1, source_target_pairs={{0,4},{4,1},{1,5},{5,0},{2,6},{6,3},{3,7},{7,2},{8,12},{12,9},{9,1... | collective-permute-start | bytes 786440 | tf_op jit(solution)/shard_map/ppermute | solution.py:37
  100.9 7.9 %collective-permute-start.18 = (bf16[512,256]{1,0:T(8,128)(2,1)S(1)}, bf16[512,256]{1,0:T(8,128)(2,1)S(1)}, u32[]{:S(2)}, u32[]{:S(2)}) collective-permute-start(bf16[512,256]{1,0:T(8,128)(2,1)S(1)} %collective-permute-done.15.refs_2_), channel_id=1, source_target_pairs={{0,5},{4,0},{1,4},{5,1},{2,7},{6,2},{3,6},{7,3},{8,13},{12,8},{9,1... | collective-permute-start | bytes 786440 | tf_op jit(solution)/shard_map/ppermute | solution.py:37
  108.8 2.5 %collective-permute-start.23 = (bf16[512,256]{1,0:T(8,128)(2,1)S(1)}, bf16[512,256]{1,0:T(8,128)(2,1)S(1)}, u32[]{:S(2)}, u32[]{:S(2)}) collective-permute-start(bf16[512,256]{1,0:T(8,128)(2,1)S(1)} %collective-permute-done.17.refs_4_), channel_id=1, source_target_pairs={{0,2},{2,0},{1,3},{3,1},{4,6},{6,4},{5,7},{7,5},{8,10},{10,8},{9,1... | collective-permute-start | bytes 786440 | tf_op jit(solution)/shard_map/ppermute | solution.py:41
  110.2 1.5 %collective-permute-start.24 = (bf16[512,256]{1,0:T(8,128)(2,1)S(1)}, bf16[512,256]{1,0:T(8,128)(2,1)S(1)}, u32[]{:S(2)}, u32[]{:S(2)}) collective-permute-start(bf16[512,256]{1,0:T(8,128)(2,1)S(1)} %collective-permute-done.18.refs_6_), channel_id=1, source_target_pairs={{0,2},{2,0},{1,3},{3,1},{4,6},{6,4},{5,7},{7,5},{8,10},{10,8},{9,1... | collective-permute-start | bytes 786440 | tf_op jit(solution)/shard_map/ppermute | solution.py:41

commit v3 on v2

v3 whole, which is shorter than its diff:
```python
import functools

import jax
import jax.numpy as jnp
from jax import lax
from jax.experimental import pallas as pl
from jax.experimental.pallas import tpu as pltpu
from jax.sharding import Mesh, PartitionSpec as P


BF16 = jnp.bfloat16
F32 = jnp.float32
MIB = 1 << 20
CHIPS = 4
LINE = ("xlo", "wt")
SLOTS = 16
FAN = 10
TOKEN = pltpu.HBM((8, 128), jnp.int32)
SPLIT = 4
LOW = 256


def in_place(count):
    return [pl.BlockSpec(memory_space=pl.ANY)] * count


def to_hbm(array):
    return pltpu.with_memory_space_constraint(array, pltpu.HBM)


def in_vmem(count):
    return [pl.BlockSpec(memory_space=pltpu.VMEM)] * count


def spot(x):
    return (x % 2) * 2 + x // 2


UP = [(spot(x), spot((x + 1) % CHIPS)) for x in range(CHIPS)]
DOWN = [(spot(x), spot((x - 1) % CHIPS)) for x in range(CHIPS)]
ACROSS = [(spot(x), spot((x + 2) % CHIPS)) for x in range(CHIPS)]
SWAP = [(0, 1), (1, 0)]


def send(block, pairs):
    return lax.ppermute(block, LINE, pairs)


def swap(block):
    return lax.ppermute(block, "core", SWAP)


def place(position, x):
    return ((((position >> 5) - x) & 3) << 10) | ((position >> 7) << 5) | (position & 31)


def write_counts(high, low, out_refs):
    slot = lax.broadcasted_iota(jnp.int32, (SLOTS, LOW), 0)
    lane = lax.broadcasted_iota(jnp.int32, (SLOTS, LOW), 1)
    expand = jnp.where((lane & (SLOTS - 1)) == slot, 1.0, 0.0).astype(BF16)
    high = dot(high.astype(F32).astype(BF16), expand)
    low = dot(low.astype(F32).astype(BF16), expand)
    target = lax.broadcasted_iota(jnp.int32, high.shape, 0)
    lane = lax.broadcasted_iota(jnp.int32, high.shape, 1)
    mine = (target & (SLOTS - 1)) == (lane >> 4)
    high = jnp.where(mine, high, -1.0).astype(BF16)
    low = jnp.where(mine, low, 0.0)
    rows = lax.broadcasted_iota(jnp.int32, (LOW, LOW), 0).astype(F32).astype(BF16)
    one = jnp.ones((), BF16)
    zero = jnp.zeros((), BF16)
    for g in range(high.shape[0] // SLOTS):
        mine_high = high[g * SLOTS : (g + 1) * SLOTS, :]
        left = jnp.concatenate(
            [jnp.where(mine_high == jnp.full((), k, BF16), one, zero) for k in range(SLOTS)], 0
        )
        mine_low = jnp.sum(low[g * SLOTS : (g + 1) * SLOTS, :], axis=0, keepdims=True).astype(BF16)
        right = jnp.where(rows == mine_low, one, zero)
        counts = lax.dot_general(left, right, (((1,), (1,)), ((), ())), preferred_element_type=F32)
        counts = counts.astype(BF16)
        store_counts(counts, out_refs, g * SLOTS)


def store_counts(counts, out_refs, start):
    each = SLOTS // SPLIT
    for k in range(SLOTS):
        out_refs[k // each][pl.ds(start, SLOTS), k % each * LOW : (k % each + 1) * LOW] = counts[
            k * SLOTS : (k + 1) * SLOTS, :
        ]


def rows_at(index, data_ref):
    rows = index.shape[0]
    lane = lax.broadcasted_iota(jnp.int32, (rows, LOW), 1).astype(F32).astype(BF16)
    spread = lambda a: jnp.broadcast_to(a.astype(F32), (rows, LOW)).astype(BF16)
    found = jnp.where(lane == spread(index & (LOW - 1)), spread(index >> 8), jnp.full((), -1, BF16))
    one, zero = jnp.ones((), BF16), jnp.zeros((), BF16)
    step = data_ref.shape[0] // SPLIT
    total = 0.0
    for start in range(0, data_ref.shape[0], step):
        hot = [
            jnp.where(found == jnp.full((), k, BF16), one, zero)
            for k in range(start // LOW, (start + step) // LOW)
        ]
        total = total + dot(jnp.concatenate(hot, 1), data_ref[start : start + step, :])
    return total


def counted(copy, buffer_ref, first, data_ref):
    step = data_ref.shape[0] // SPLIT
    total = 0.0
    for k in range(SPLIT):
        copy(first + k).wait()
        total = total + dot(buffer_ref[first + k], data_ref[k * step : (k + 1) * step, :])
    return total


def fetch_counts(counts_refs, buffer_ref, sems):
    rows = buffer_ref.shape[1]
    for k in range(buffer_ref.shape[0]):
        part = k // SPLIT * rows
        source = counts_refs[k % SPLIT].at[part : part + rows, :]
        pltpu.make_async_copy(source, buffer_ref.at[k], sems.at[k]).start()
    source = counts_refs[0].at[:rows, :]
    return lambda k: pltpu.make_async_copy(source, buffer_ref.at[k], sems.at[k])


def table_kernel(slots_ref, own_ref, size_ref, out_ref, lines_ref):
    lines_ref[...] = jnp.zeros(lines_ref.shape, jnp.int32)
    lanes = lines_ref.shape[1]
    width = slots_ref.shape[1]
    base = pl.program_id(0) * width
    for b in range(width // lanes):
        at = slice(b * lanes, (b + 1) * lanes)
        lines_ref[:FAN, :] = slots_ref[:, at]
        lines_ref[FAN : FAN + 1, :] = own_ref[:, at]
        lines_ref[FAN + 1 : FAN + 2, :] = size_ref[:, at]
        start = pl.multiple_of(base + b * lanes, lanes)
        out_ref[pl.ds(start, lanes), :] = lines_ref[...].T


def node_table(slots, own, sizes):
    stored = slots.shape[1]
    step = 512
    return pl.pallas_call(
        table_kernel,
        grid=(stored // step,),
        in_specs=[pl.BlockSpec((a.shape[0], step), lambda i: (0, i)) for a in (slots, own, sizes)],
        out_specs=in_vmem(1)[0],
        out_shape=jax.ShapeDtypeStruct((stored, SLOTS), jnp.int32),
        scratch_shapes=[pltpu.VMEM((SLOTS, 128), jnp.int32)],
        compiler_params=pltpu.CompilerParams(vmem_limit_bytes=2 * MIB),
        name="node_table",
    )(slots, own, sizes)


def node_kernel(request_ref, x_ref, table_ref, nodes_ref, *refs):
    out_refs, rows_ref = refs[:SPLIT], refs[-1]
    step = rows_ref.shape[0]
    base = pl.multiple_of(pl.program_id(0) * step, step)

    @pl.loop(0, step, step=32)
    def _(start):
        for i in range(32):
            rows_ref[pl.ds(start + i, 1), :] = table_ref[pl.ds(request_ref[base + start + i], 1), :]

    rows = rows_ref[...]
    nodes_ref[...] = rows
    size = rows[:, FAN + 1 : FAN + 2]
    at = place(rows, x_ref[0])
    valid = lax.broadcasted_iota(jnp.int32, rows.shape, 1) < size
    high = jnp.where(valid, at >> 8, -1)
    write_counts(high, at & (LOW - 1), out_refs)


def node_counts(requests, x, table, positions):
    targets = requests.shape[0]
    step = 128
    return pl.pallas_call(
        node_kernel,
        grid_spec=pltpu.PrefetchScalarGridSpec(
            num_scalar_prefetch=2,
            grid=(targets // step,),
            in_specs=in_vmem(1),
            out_specs=(
                *[pl.BlockSpec((step, SLOTS), lambda i, r, x: (i, 0))],
                *[pl.BlockSpec((step, positions // SPLIT), lambda i, r, x: (i, 0))] * SPLIT,
                *in_place(1),
            ),
            scratch_shapes=[pltpu.VMEM((step, SLOTS), jnp.int32)],
        ),
        out_shape=(
            pltpu.HBM((targets, SLOTS), jnp.int32),
            *[pltpu.HBM((targets, positions // SPLIT), BF16)] * SPLIT,
            TOKEN,
        ),
        compiler_params=pltpu.CompilerParams(vmem_limit_bytes=10 * MIB),
        cost_estimate=pl.CostEstimate(
            flops=targets * 2 * SLOTS * LOW * LOW, transcendentals=0, bytes_accessed=targets * positions * 2
        ),
        name="node_counts",
    )(requests, x.reshape(1), table)


def codes(neighbours, counts, x):
    targets, fan = neighbours.shape
    at = place(jnp.pad(neighbours, ((0, 0), (0, SLOTS - fan))), x)
    valid = lax.broadcasted_iota(jnp.int32, at.shape, 1) < counts[:, None]
    target = lax.broadcasted_iota(jnp.int32, at.shape, 0) & (SLOTS - 1)
    high = jnp.where(valid, (at >> 8) * SLOTS + target + 1, 0)
    return (high * LOW + (at & (LOW - 1))).reshape(targets // SLOTS, SLOTS * SLOTS)


def slot_kernel(code_ref, *refs):
    out_refs = refs[-SPLIT - 1 : -1]
    rows = lax.broadcasted_iota(jnp.int32, (LOW, LOW), 0).astype(F32).astype(BF16)
    one = jnp.ones((), BF16)
    zero = jnp.zeros((), BF16)

    @pl.loop(0, code_ref.shape[0], step=4)
    def _(first):
        for i in range(4):
            code = code_ref[pl.ds(first + i, 1), :]
            left = jnp.where(rows == ((code >> 8) - 1).astype(F32).astype(BF16), one, zero)
            right = jnp.where(rows == (code & (LOW - 1)).astype(F32).astype(BF16), one, zero)
            counts = lax.dot_general(left, right, (((1,), (1,)), ((), ())), preferred_element_type=F32)
            store_counts(counts.astype(BF16), out_refs, pl.multiple_of((first + i) * SLOTS, SLOTS))


def slot_counts(code, positions, part, before=()):
    groups, width = code.shape
    step = 8
    steps = groups // step // 2
    width_out = positions // SPLIT
    return pl.pallas_call(
        slot_kernel,
        grid=(steps,),
        in_specs=[pl.BlockSpec((step, width), lambda i: (i + part * steps, 0))]
        + in_place(len(before)),
        out_specs=(
            *[pl.BlockSpec((step * SLOTS, width_out), lambda i: (i + part * steps, 0))] * SPLIT,
            *in_place(1),
        ),
        out_shape=(*[pltpu.HBM((groups * SLOTS, width_out), BF16)] * SPLIT, TOKEN),
        input_output_aliases={i + 1: i for i in range(len(before))},
        compiler_params=pltpu.CompilerParams(vmem_limit_bytes=10 * MIB),
        cost_estimate=pl.CostEstimate(
            flops=groups * LOW * LOW * LOW,
            transcendentals=0,
            bytes_accessed=groups // 2 * SLOTS * positions * 2,
        ),
        name="slot_counts",
    )(code, *before)


def weight_kernel(at_ref, *refs):
    blocks, (mine_ref, other_ref, first_ref, second_ref, token_ref) = refs[:-5], refs[-5:]
    x, core = at_ref[0], at_ref[1]
    half = first_ref.shape[1] // 4
    for i, block in enumerate(blocks):
        chip = (x + i // 2) & (CHIPS - 1)
        column = 2 * (chip & 1) + (core if i % 2 == 0 else 1 - core)
        for side in range(2):
            start = pl.multiple_of(half * (core if side == 0 else 1 - core), half)
            at = pl.multiple_of((2 * side + (chip >> 1)) * half, half)
            first_ref[column, pl.ds(at, half), :] = block[pl.ds(start, half), :]
    columns = mine_ref.shape[1]

    def join(left_ref, right_ref):
        @pl.loop(0, second_ref.shape[0] // half)
        def _(i):
            rows = pl.ds(pl.multiple_of(i * half, half), half)
            second_ref[rows, :columns] = left_ref[rows, :]
            second_ref[rows, columns:] = right_ref[rows, :]

    pl.when(x < 2)(lambda: join(mine_ref, other_ref))
    pl.when(x >= 2)(lambda: join(other_ref, mine_ref))


def assemble(at, blocks, mine, other):
    k, width = blocks[0].shape
    first = (CHIPS, 2 * k, width)
    second = (mine.shape[0], 2 * mine.shape[1])
    return pl.pallas_call(
        weight_kernel,
        grid_spec=pltpu.PrefetchScalarGridSpec(
            num_scalar_prefetch=1,
            grid=(1,),
            in_specs=[
                pl.BlockSpec(b.shape, lambda i, at: (0, 0), pipeline_mode=pl.Buffered(1))
                for b in (*blocks, mine, other)
            ],
            out_specs=(*in_vmem(2), *in_place(1)),
        ),
        out_shape=(jax.ShapeDtypeStruct(first, BF16), jax.ShapeDtypeStruct(second, BF16), TOKEN),
        compiler_params=pltpu.CompilerParams(vmem_limit_bytes=10 * MIB),
        name="assemble",
    )(at, *[to_hbm(b) for b in (*blocks, mine, other)])


def column(row):
    shape = (row.shape[1], row.shape[1])
    diagonal = lax.broadcasted_iota(jnp.int32, shape, 0) == lax.broadcasted_iota(jnp.int32, shape, 1)
    return jnp.sum(jnp.where(diagonal, row.astype(F32), 0.0), axis=1, keepdims=True)


def dot(a, b):
    return jnp.dot(a, b, preferred_element_type=F32)


def load_rows(out_ref, data_ref, positions):
    for i, at in enumerate(positions):
        out_ref[i : i + 1, :] = data_ref[pl.ds(at, 1), :]


def pick_kernel(want_ref, at_ref, *refs):
    blocks, (out_ref, wide_ref, rows_ref) = refs[:-3], refs[-3:]
    start = 0
    for block in blocks:
        wide_ref[start : start + block.shape[0], :] = block[...].astype(F32)
        start += block.shape[0]
    parts = want_ref.shape[0]
    block = out_ref.shape[0] // parts
    base = at_ref[0] * block

    @pl.loop(0, parts)
    def _(p):
        load_rows(rows_ref, wide_ref, [want_ref[p, base + i] for i in range(block)])
        out_ref[pl.ds(pl.multiple_of(p * block, block), block), :] = rows_ref[...].astype(BF16)


def pick(want, at, stored, targets):
    rows, width = stored.shape[0] // SPLIT, stored.shape[1] // 2
    block = targets // want.shape[0]
    return pl.pallas_call(
        pick_kernel,
        grid_spec=pltpu.PrefetchScalarGridSpec(
            num_scalar_prefetch=2,
            grid=(1,),
            in_specs=[
                pl.BlockSpec((rows, width), lambda i, w, at, k=k: (k, at[1])) for k in range(SPLIT)
            ],
            out_specs=pl.BlockSpec((targets, width), lambda i, w, at: (0, 0)),
            scratch_shapes=[
                pltpu.VMEM((stored.shape[0], width), F32),
                pltpu.VMEM((block, width), F32),
            ],
        ),
        out_shape=jax.ShapeDtypeStruct((targets, width), BF16),
        compiler_params=pltpu.CompilerParams(vmem_limit_bytes=8 * MIB),
        name="pick",
    )(want, at, *[to_hbm(stored)] * SPLIT)


def mean_kernel(tokens, x_ref, *refs):
    counts_refs, nodes_ref, refs = refs[:SPLIT], refs[SPLIT], refs[SPLIT + 1 :]
    pieces, (out_ref, data_ref, buffer_ref, sems) = refs[tokens:-4], refs[-4:]
    width = out_ref.shape[1] // 2
    copy = fetch_counts(counts_refs, buffer_ref, sems)
    start = 0
    for piece in pieces:
        data_ref[start : start + piece.shape[0], :] = piece[...]
        start += piece.shape[0]
    own_at = place(nodes_ref[:, FAN : FAN + 1], x_ref[0])
    size = nodes_ref[:, FAN + 1 : FAN + 2].astype(F32)
    out_ref[:, :width] = rows_at(own_at, data_ref).astype(BF16)
    total = counted(copy, buffer_ref, 0, data_ref)
    out_ref[:, width:] = (total / size).astype(BF16)


def own_and_mean(x, counts, nodes, pieces, after):
    targets, each = counts[0].shape
    width = pieces[0].shape[1]
    return pl.pallas_call(
        functools.partial(mean_kernel, len(after)),
        grid_spec=pltpu.PrefetchScalarGridSpec(
            num_scalar_prefetch=1,
            grid=(1,),
            in_specs=in_place(SPLIT)
            + [pl.BlockSpec(nodes.shape, lambda i, x: (0, 0))]
            + in_place(len(after))
            + in_vmem(len(pieces)),
            out_specs=pl.BlockSpec((targets, 2 * width), lambda i, x: (0, 0)),
            scratch_shapes=[
                pltpu.VMEM((SPLIT * each, width), BF16),
                pltpu.VMEM((SPLIT, targets, each), BF16),
                pltpu.SemaphoreType.DMA((SPLIT,)),
            ],
        ),
        out_shape=pltpu.HBM((targets, 2 * width), BF16),
        compiler_params=pltpu.CompilerParams(vmem_limit_bytes=24 * MIB),
        cost_estimate=pl.CostEstimate(
            flops=4 * targets * SPLIT * each * width,
            transcendentals=0,
            bytes_accessed=targets * SPLIT * each * 2,
        ),
        name="own_and_mean",
    )(x.reshape(1), *[to_hbm(c) for c in counts], to_hbm(nodes), *map(to_hbm, after), *pieces)


def project_into(out_ref, start, sides, first_ref, second_ref):
    mine, other = (side[...] for side in sides)
    rows, k = mine.shape
    acc = jnp.zeros((rows, out_ref.shape[1]), F32)
    for h in range(first_ref.shape[0]):
        pre = dot(mine, first_ref[h, :k, :]) + dot(other, first_ref[h, k:, :])
        hidden = jnp.maximum(pre, 0.0).astype(BF16)
        width = hidden.shape[1]
        acc = acc + dot(hidden, second_ref[h * width : (h + 1) * width, :])
    out_ref[pl.ds(start, rows), :] = acc.astype(BF16)


def stage(side_refs, pieces):
    start = 0
    for mine, other in zip(pieces[::2], pieces[1::2]):
        for side, piece in zip(side_refs, (mine, other)):
            side[start : start + piece.shape[0], :] = piece[...]
        start += mine.shape[0]


def project_kernel(tokens, first_ref, second_ref, *refs):
    pieces, (out_ref, mine_ref, other_ref) = refs[tokens:-3], refs[-3:]
    if len(pieces) == 2:
        project_into(out_ref, 0, pieces, first_ref, second_ref)
        return
    stage((mine_ref, other_ref), pieces)
    rows = 1024

    @pl.loop(0, out_ref.shape[0] // rows)
    def _(part):
        at = pl.multiple_of(part * rows, rows)
        sides = [side.at[pl.ds(at, rows), :] for side in (mine_ref, other_ref)]
        project_into(out_ref, at, sides, first_ref, second_ref)


def project(first, second, *pieces, after=()):
    rows = sum(p.shape[0] for p in pieces[::2])
    k, width = pieces[0].shape[1], second.shape[1]
    return pl.pallas_call(
        functools.partial(project_kernel, len(after)),
        in_specs=in_vmem(2) + in_place(len(after)) + in_vmem(len(pieces)),
        out_specs=in_vmem(1)[0],
        out_shape=jax.ShapeDtypeStruct((rows, width), BF16),
        scratch_shapes=[pltpu.VMEM((rows, k), BF16)] * 2,
        compiler_params=pltpu.CompilerParams(vmem_limit_bytes=10 * MIB),
        cost_estimate=pl.CostEstimate(
            flops=2 * rows * second.shape[0] * (2 * k + width),
            transcendentals=0,
            bytes_accessed=rows * (2 * k + width) * 2,
        ),
        name="project",
    )(first, second, *map(to_hbm, after), *pieces)


def seed_kernel(*refs):
    counts_refs, (own_ref, size_ref, first_ref, second_ref), refs = refs[:SPLIT], refs[SPLIT : SPLIT + 4], refs[SPLIT + 4 :]
    (mine_ref, near_ref), far, refs = refs[:2], refs[2:-6], refs[-6:]
    out_ref, data_ref, buffer_ref, sides, sems = *refs[:3], refs[3:5], refs[5]
    width = out_ref.shape[1]
    block = mine_ref.shape[0]
    copy = fetch_counts(counts_refs, buffer_ref, sems)
    data_ref[:block, :] = mine_ref[...]
    data_ref[block : 2 * block, :] = near_ref[:block, :]
    data_ref[3 * block :, :] = near_ref[block:, :]
    stage(sides, far)
    project_into(data_ref, 2 * block, sides, first_ref, second_ref)
    rows = buffer_ref.shape[1]

    @pl.loop(0, out_ref.shape[0] // rows)
    def _(part):
        places, sizes = own_ref[pl.ds(part, 1), :], size_ref[pl.ds(part, 1), :]
        tiles = range(0, rows, LOW)
        own_at = jnp.concatenate([column(places[:, t : t + LOW]) for t in tiles], 0).astype(jnp.int32)
        size = jnp.concatenate([column(sizes[:, t : t + LOW]) for t in tiles], 0)
        own = rows_at(own_at, data_ref.at[:, :width])
        total = counted(copy, buffer_ref, part * SPLIT, data_ref.at[:, width:])
        start = pl.multiple_of(part * rows, rows)
        out_ref[pl.ds(start, rows), :] = (own + total / size).astype(BF16)


def seeds(counts, places, sizes, first, second, own, near, far):
    targets, each = counts[0].shape
    width = second.shape[1] // 2
    parts, rows = places.shape
    return pl.pallas_call(
        seed_kernel,
        in_specs=in_place(SPLIT) + in_vmem(6 + len(far)),
        out_specs=in_vmem(1)[0],
        out_shape=jax.ShapeDtypeStruct((targets, width), BF16),
        scratch_shapes=[
            pltpu.VMEM((SPLIT * each, 2 * width), BF16),
            pltpu.VMEM((parts * SPLIT, rows, each), BF16),
            *[pltpu.VMEM((own.shape[0], first.shape[1] // 2), BF16)] * 2,
            pltpu.SemaphoreType.DMA((parts * SPLIT,)),
        ],
        compiler_params=pltpu.CompilerParams(vmem_limit_bytes=30 * MIB),
        cost_estimate=pl.CostEstimate(
            flops=4 * targets * SPLIT * each * width,
            transcendentals=0,
            bytes_accessed=targets * SPLIT * each * 2,
        ),
        name="seeds",
    )(*[to_hbm(c) for c in counts], places, sizes, first, second, own, near, *far)


def shards(
    store_feat,
    want_in,
    nbr_in,
    self_in,
    count_in,
    weight_one,
    want_hid,
    nbr_hid,
    self_hid,
    count_hid,
    weight_two,
):
    x = lax.axis_index("wt") * 2 + lax.axis_index("xlo")
    core = lax.axis_index("core")
    parts = want_in.shape[1]
    block = want_in.shape[2] // CHIPS

    def mine(wanted):
        return lax.dynamic_slice_in_dim(wanted[0], block * x, block, 1).reshape(-1)

    def exchange(rows):
        pieces = rows.reshape(parts, block, rows.shape[1])
        return lax.all_to_all(pieces, "dom", 0, 0, tiled=True).reshape(rows.shape)

    together = lax.optimization_barrier
    positions = parts * block * CHIPS

    at = jnp.stack([x, core]).astype(jnp.int32)
    fetched = exchange(pick(want_in[0], at, store_feat, parts * block))

    table = node_table(nbr_in.T, self_in[None], count_in[None])
    requests = mine(want_hid)
    nodes, *counts, token = node_counts(requests, x, table, positions)
    fetched, token = together((fetched, token))
    below, above = send(fetched, UP), send(fetched, DOWN)
    code = codes(nbr_hid, count_hid, x)
    below, above, code = together((below, above, code))
    cut = below.shape[0] // 2
    far_low, far_high = send(below[:cut], UP), send(above[cut:], DOWN)
    *counts_two, token_two = slot_counts(code, positions, 0)
    weight_one, token_two = together((weight_one, token_two))
    first_blocks = [weight_one] + [send(weight_one, pairs) for pairs in (DOWN, ACROSS, UP)]
    pieces = (fetched, above, far_low, far_high, below)
    ready = own_and_mean(x, counts, nodes, pieces, (token, token_two))

    ready, weight_two, code, *first_blocks = together((ready, weight_two, code, *first_blocks))
    arrived = exchange(ready)
    other_rows = send(weight_two, ACROSS)
    *counts_two, token = slot_counts(code, positions, 1, counts_two)
    first_blocks = [b for block in first_blocks for b in (block, to_hbm(swap(block)))]
    own_at = place(self_hid, x).reshape(2, -1)
    sizes = count_hid.reshape(2, -1)
    arrived, own_at, sizes, token, weight_two, other_rows, *first_blocks = together(
        (arrived, own_at, sizes, token, weight_two, other_rows, *first_blocks)
    )
    first, second, ready = assemble(at, first_blocks, weight_two, other_rows)
    cut = arrived.shape[0] // 2
    low, high = arrived[:cut], arrived[cut:]
    below_low, above_high = send(low, UP), send(high, DOWN)
    below_high, above_low = send(high, UP), send(low, DOWN)
    other = swap(arrived)
    below_low, above_high, other, ready = together((below_low, above_high, other, ready))
    far_low = send(below_low, UP)
    far_high = send(above_high, DOWN)
    own = project(first, second, arrived, other, after=(token, ready))
    below_high, above_low, own = together((below_high, above_low, own))
    near = []
    for piece in (above_low, above_high, below_low, below_high):
        near += [piece, swap(piece)]
    near = project(first, second, *near)
    far_low, far_high, near = together((far_low, far_high, near))
    far = (far_low, swap(far_low), far_high, swap(far_high))
    return seeds(counts_two, own_at, sizes, first, second, own, near, far)


def solution(mesh):
    mesh = Mesh(mesh.devices.reshape(32, 2, 2, 2), ("dom", "xlo", "core", "wt"))
    columns = ("xlo", "core")
    return jax.shard_map(
        shards,
        mesh=mesh,
        in_specs=(
            P("dom", None),
            P("dom", None, None),
            P("dom", None),
            P("dom"),
            P("dom"),
            P("wt", columns),
            P("dom", None, None),
            P("dom", None),
            P("dom"),
            P("dom"),
            P("wt", columns),
        ),
        out_specs=P("dom", columns),
        check_vma=False,
    )
```

time: 129 us -> 141 us (1.093)
  Pallas kernels: 54 us -> 77.6 us
  local copies, waits for them, and re-layouts: 19.9 us -> 1.79 us
  waiting for transfers between devices: 3.75 us -> 9.4 us
  starting transfers between devices: 49.7 us -> 51.4 us
    pallas_call x1 -> x2, Pallas kernels: 16.7 us -> 28.4 us  [the longest x1 22.9 us: seeds(): pl.pallas_call(seed_kernel, in_specs=in_place(SPLIT) + in_vmem(6 + len(fa...]
    unnamed x42 -> x36, local copies, waits for them, and re-layouts: 9.13 us -> 0.8 us
    ppermute x14, waiting for transfers between devices: 1.79 us -> 7.86 us  [send(): return lax.ppermute(block, LINE, pairs)]
    gather x1 -> x0, local copies, waits for them, and re-layouts: 4.98 us -> none  [shards(): picked = store_feat.at[mine(want_in)].get(mode='promise_in_bounds')]
    pallas_call x2, Pallas kernels: 10 us -> 14.7 us  [slot_counts(): pl.pallas_call(slot_kernel, grid=(steps,), in_specs=[pl.BlockSpec((step,...]
    pallas_call x1, Pallas kernels: 8.77 us -> 12.9 us  [own_and_mean(): pl.pallas_call(functools.partial(mean_kernel, len(after)), grid_spec=pltp...]
    dynamic_slice x1 -> x0, local copies, waits for them, and re-layouts: 1.66 us -> none  [shards(): picked = lax.dynamic_slice_in_dim(picked, half * core, half, 1)]
    pallas_call x1, Pallas kernels: 6.52 us -> 8.07 us  [node_counts(): pl.pallas_call(node_kernel, grid_spec=pltpu.PrefetchScalarGridSpec(num_sc...]
  transfers between devices with their start and end apart: 27 -> 27, of which waited for: 8 -> 9; matrix products, arithmetic and copies ran while one was open for 3% -> 1% of each run, Pallas kernels for 29% -> 35%
where the time goes in v3:
time: 141 us
  Pallas kernels  77.6 us (55%)
  starting transfers between devices  51.4 us (36%)
  waiting for transfers between devices  9.4 us (7%)
  local copies, waits for them, and re-layouts  1.79 us (1%)
    pallas_call x1, Pallas kernels, seeds(): pl.pallas_call(seed_kernel, in_specs=in_place(SPLIT) + in_vmem(6 + len(fa...  22.9 us
    all_to_all x2, starting transfers between devices, exchange(): return lax.all_to_all(pieces, 'dom', 0, 0, tiled=True).reshape(rows.shape)  22.1 us
    ppermute x14, starting transfers between devices, send(): return lax.ppermute(block, LINE, pairs)  19.3 us
    pallas_call x2, Pallas kernels, slot_counts(): pl.pallas_call(slot_kernel, grid=(steps,), in_specs=[pl.BlockSpec((step,...  14.7 us
    pallas_call x1, Pallas kernels, own_and_mean(): pl.pallas_call(functools.partial(mean_kernel, len(after)), grid_spec=pltp...  12.9 us
    ppermute x11, starting transfers between devices, swap(): return lax.ppermute(block, 'core', SWAP)  9.97 us
    pallas_call x2, Pallas kernels, project(): pl.pallas_call(functools.partial(project_kernel, len(after)), in_specs=in...  8.36 us
    pallas_call x1, Pallas kernels, node_counts(): pl.pallas_call(node_kernel, grid_spec=pltpu.PrefetchScalarGridSpec(num_sc...  8.07 us
  transfers between devices with their start and end apart: 27, of which 9 were waited for; matrix products, arithmetic and copies ran while one was open for 1% of the time, Pallas kernels for 35%

profile of v3, /device:TPU:1, one launch (start us, length us, event | category | flops | bytes accessed | tf_op | source)
XLA Modules:
  0.0 140.8 jit_solution(10499742224772143663)
XLA Ops:
  0.1 0.7 copy-done.4
  0.8 5.6 %pick.1 = bf16[1024,128]{1,0:T(8,128)(2,1)} custom-call(s32[32,128]{1,0:T(8,128)S(1)} %bitcast.19, s32[2]{0:T(128)S(1)} %pad_add_fusion.at_ref, bf16[4096,256]{1,0:T(8,128)(2,1)} %refs_3_.1, bf16[4096,256]{1,0:T(8,128)(2,1)} %refs_3_.1, bf16[4096,256]{1,0:T(8,128)(2,1)} %refs_3_.1, bf16[4096,256]{1,0:T(8,128)(2,1)} %refs_3_.1), custom_call_target="tpu_custom_call" | custom-call | tf_op jit(solution)/shard_map/pick/pallas_call | solution.py:334
  6.4 12.0 %all-to-all-start = ((bf16[32,32,128]{2,1,0:T(8,128)(2,1)}), bf16[32,32,128]{2,1,0:T(8,128)(2,1)S(1)}, u32[]{:S(2)}, u32[]{:S(2)}) async-start(bf16[32,32,128]{2,1,0:T(8,128)(2,1)} %bitcast.6), calls=%async_computation | async-start | bytes 524288 | tf_op jit(solution)/shard_map/all_to_all | solution.py:528
  18.6 2.5 %node_table.1.table_ref = s32[8192,16]{1,0:T(8,128)S(1)} custom-call(s32[10,8192]{1,0:T(8,128)S(1)} %bitcast.16, s32[1,8192]{1,0:T(1,128)S(1)} %bitcast.17, s32[1,8192]{1,0:T(1,128)S(1)} %bitcast.18), custom_call_target="tpu_custom_call" | custom-call | tf_op jit(solution)/shard_map/node_table/pallas_call | solution.py:144
  21.1 8.1 %node_counts.1 = (s32[1024,16]{1,0:T(8,128)}, bf16[1024,1024]{1,0:T(8,128)(2,1)}, bf16[1024,1024]{1,0:T(8,128)(2,1)}, bf16[1024,1024]{1,0:T(8,128)(2,1)}, bf16[1024,1024]{1,0:T(8,128)(2,1)}, /*index=5*/s32[8,128]{1,0:T(8,128)}) custom-call(s32[1024]{0:T(1024)S(1)} %reshape.32.request_ref, s32[1]{0:T(128)} %bitcast.x_ref, s32[8192,16]{1,0:T(8,128)S(1)} %node_table.1.table_ref), custom_call_target="tpu_custom_call" | custom-call | flops 2147483648 | bytes 8388608 | tf_op jit(solution)/shard_map/node_counts/pallas_call | solution.py:178
  29.2 1.2 collective-permute-start
  30.4 1.5 %collective-permute-start.1 = (bf16[1024,128]{1,0:T(8,128)(2,1)S(1)}, bf16[1024,128]{1,0:T(8,128)(2,1)S(1)}, u32[]{:S(2)}, u32[]{:S(2)}) collective-permute-start(bf16[1024,128]{1,0:T(8,128)(2,1)S(1)} %bitcast.14), channel_id=1, source_target_pairs={{0,5},{4,0},{1,4},{5,1},{2,7},{6,2},{3,6},{7,3},{8,13},{12,8},{9,1... | collective-permute-start | bytes 786440 | tf_op jit(solution)/shard_map/ppermute | solution.py:46
  31.9 0.1 and_add_fusion
  32.0 0.3 copy.17
  32.3 0.4 reshape.35.code_ref
  32.8 2.9 %collective-permute-done.refs_11_ = bf16[1024,128]{1,0:T(8,128)(2,1)S(1)} collective-permute-done((bf16[1024,128]{1,0:T(8,128)(2,1)S(1)}, bf16[1024,128]{1,0:T(8,128)(2,1)S(1)}, u32[]{:S(2)}, u32[]{:S(2)}) %collective-permute-start) | collective-permute-done | bytes 262176 | tf_op jit(solution)/shard_map/ppermute | solution.py:46
  35.7 1.6 %collective-permute-start.2 = (bf16[512,128]{1,0:T(8,128)(2,1)S(1)}, bf16[512,128]{1,0:T(8,128)(2,1)S(1)}, u32[]{:S(2)}, u32[]{:S(2)}) collective-permute-start(bf16[512,128]{1,0:T(8,128)(2,1)S(1)} %slice.12), channel_id=1, source_target_pairs={{0,4},{4,1},{1,5},{5,0},{2,6},{6,3},{3,7},{7,2},{8,12},{12,9},{9,1... | collective-permute-start | bytes 393224 | tf_op jit(solution)/shard_map/ppermute | solution.py:46
  37.2 1.3 collective-permute-start.3
  38.5 7.3 %slot_counts.2 = (bf16[2048,1024]{1,0:T(8,128)(2,1)}, bf16[2048,1024]{1,0:T(8,128)(2,1)}, bf16[2048,1024]{1,0:T(8,128)(2,1)}, bf16[2048,1024]{1,0:T(8,128)(2,1)}, s32[8,128]{1,0:T(8,128)}) custom-call(s32[128,256]{1,0:T(8,128)S(1)} %reshape.35.code_ref), custom_call_target="tpu_custom_call" | custom-call | flops 2147483648 | bytes 8388608 | tf_op jit(solution)/shard_map/slot_counts/pallas_call | solution.py:234
  45.9 1.5 %collective-permute-start.4 = (bf16[256,256]{1,0:T(8,128)(2,1)S(1)}, bf16[256,256]{1,0:T(8,128)(2,1)S(1)}, u32[]{:S(2)}, u32[]{:S(2)}) collective-permute-start(bf16[256,256]{1,0:T(8,128)(2,1)S(1)} %copy-done.7), channel_id=1, source_target_pairs={{0,5},{4,0},{1,4},{5,1},{2,7},{6,2},{3,6},{7,3},{8,13},{12,8},{9,1... | collective-permute-start | bytes 393224 | tf_op jit(solution)/shard_map/ppermute | solution.py:46
  47.3 0.6 collective-permute-start.5
  47.9 0.3 collective-permute-start.6
  48.3 12.9 %own_and_mean.1 = bf16[1024,256]{1,0:T(8,128)(2,1)} custom-call(s32[1]{0:T(128)} %bitcast.x_ref, bf16[1024,1024]{1,0:T(8,128)(2,1)} %get-tuple-element.62.refs_0_, bf16[1024,1024]{1,0:T(8,128)(2,1)} %get-tuple-element.63.refs_1_, bf16[1024,1024]{1,0:T(8,128)(2,1)} %get-tuple-element.64.refs_2_, bf16[1024,1024]{1,0:T(8,128)(2,1)} %get-tuple-element.65.refs_3_, ...), custom_call_target="tpu_custom_call" | custom-call | flops 2147483648 | bytes 8388608 | tf_op jit(solution)/shard_map/own_and_mean/pallas_call | solution.py:373
  61.2 10.1 %all-to-all-start.1 = ((bf16[32,32,256]{2,1,0:T(8,128)(2,1)}), bf16[32,32,256]{2,1,0:T(8,128)(2,1)S(1)}, u32[]{:S(2)}, u32[]{:S(2)}) async-start(bf16[32,32,256]{2,1,0:T(8,128)(2,1)} %bitcast.20), calls=%async_computation.1 | async-start | bytes 1048576 | tf_op jit(solution)/shard_map/all_to_all | solution.py:528
  71.4 3.3 %collective-permute-start.7 = (bf16[1024,256]{1,0:T(8,128)(2,1)S(1)}, bf16[1024,256]{1,0:T(8,128)(2,1)S(1)}, u32[]{:S(2)}, u32[]{:S(2)}) collective-permute-start(bf16[1024,256]{1,0:T(8,128)(2,1)S(1)} %copy-done.5), channel_id=1, source_target_pairs={{0,1},{4,5},{1,0},{5,4},{2,3},{6,7},{3,2},{7,6},{8,9},{12,13},{9,8... | collective-permute-start | bytes 1572872 | tf_op jit(solution)/shard_map/ppermute | solution.py:46
  74.7 4.1 %collective-permute-start.10 = (bf16[256,256]{1,0:T(8,128)(2,1)S(1)}, bf16[256,256]{1,0:T(8,128)(2,1)S(1)}, u32[]{:S(2)}, u32[]{:S(2)}) collective-permute-start(bf16[256,256]{1,0:T(8,128)(2,1)S(1)} %collective-permute-done.5.refs_4_), channel_id=1, source_target_pairs={{0,2},{2,0},{1,3},{3,1},{4,6},{6,4},{5,7},{7,5},{8,10},{10,8},{9,1... | collective-permute-start | bytes 393224 | tf_op jit(solution)/shard_map/ppermute | solution.py:50
  78.8 0.1 collective-permute-start.11
  78.9 0.4 collective-permute-start.8
  79.3 0.1 collective-permute-start.9
  79.4 7.4 %slot_counts.3 = (bf16[2048,1024]{1,0:T(8,128)(2,1)}, bf16[2048,1024]{1,0:T(8,128)(2,1)}, bf16[2048,1024]{1,0:T(8,128)(2,1)}, bf16[2048,1024]{1,0:T(8,128)(2,1)}, s32[8,128]{1,0:T(8,128)}) custom-call(s32[128,256]{1,0:T(8,128)S(1)} %reshape.35.code_ref, ...), custom_call_target="tpu_custom_call", output_to_operand_aliasing={{0}: (1, {}), {1}: (2, {}), {2}: (3, {}), {3}: (4, {})} | custom-call | flops 2147483648 | bytes 8388608 | tf_op jit(solution)/shard_map/slot_counts/pallas_call | solution.py:234
  86.9 2.1 %collective-permute-start.16 = (bf16[1024,256]{1,0:T(8,128)(2,1)S(1)}, bf16[1024,256]{1,0:T(8,128)(2,1)S(1)}, u32[]{:S(2)}, u32[]{:S(2)}) collective-permute-start(bf16[1024,256]{1,0:T(8,128)(2,1)S(1)} %bitcast.10), channel_id=1, source_target_pairs={{0,2},{2,0},{1,3},{3,1},{4,6},{6,4},{5,7},{7,5},{8,10},{10,8},{9,1... | collective-permute-start | bytes 1572872 | tf_op jit(solution)/shard_map/ppermute | solution.py:50
  89.1 2.4 %collective-permute-start.14 = (bf16[512,256]{1,0:T(8,128)(2,1)S(1)}, bf16[512,256]{1,0:T(8,128)(2,1)S(1)}, u32[]{:S(2)}, u32[]{:S(2)}) collective-permute-start(bf16[512,256]{1,0:T(8,128)(2,1)S(1)} %get-tuple-element.119), channel_id=1, source_target_pairs={{0,4},{4,1},{1,5},{5,0},{2,6},{6,3},{3,7},{7,2},{8,12},{12,9},{9,1... | collective-permute-start | bytes 786440 | tf_op jit(solution)/shard_map/ppermute | solution.py:46
  91.5 0.4 collective-permute-start.15
  91.9 1.0 collective-permute-start.12
  92.9 1.7 %collective-permute-start.13 = (bf16[512,256]{1,0:T(8,128)(2,1)S(1)}, bf16[512,256]{1,0:T(8,128)(2,1)S(1)}, u32[]{:S(2)}, u32[]{:S(2)}) collective-permute-start(bf16[512,256]{1,0:T(8,128)(2,1)S(1)} %get-tuple-element.119), channel_id=1, source_target_pairs={{0,5},{4,0},{1,4},{5,1},{2,7},{6,2},{3,6},{7,3},{8,13},{12,8},{9,1... | collective-permute-start | bytes 786440 | tf_op jit(solution)/shard_map/ppermute | solution.py:46
  94.6 2.6 %assemble.1 = (bf16[4,512,256]{2,1,0:T(8,128)(2,1)S(1)}, bf16[1024,512]{1,0:T(8,128)(2,1)S(1)}, s32[8,128]{1,0:T(8,128)}) custom-call(s32[2]{0:T(128)S(1)} %pad_add_fusion.at_ref, bf16[256,256]{1,0:T(8,128)(2,1)} %refs_0_.2, bf16[256,256]{1,0:T(8,128)(2,1)} %copy-done.13, bf16[256,256]{1,0:T(8,128)(2,1)} %copy-done.8, bf16[256,256]{1,0:T(8,128)(2,1)} %copy-done.14, ...), custom_call_target="tpu_custom_call" | custom-call | tf_op jit(solution)/shard_map/assemble/pallas_call | solution.py:283
  97.2 1.0 collective-permute-done.14.refs_4_
  98.2 0.8 collective-permute-done.15.refs_2_
  99.0 2.7 %project.2.refs_8_ = bf16[1024,512]{1,0:T(8,128)(2,1)S(1)} custom-call(bf16[4,512,256]{2,1,0:T(8,128)(2,1)S(1)} %get-tuple-element.104.first_ref.refs_6_, bf16[1024,512]{1,0:T(8,128)(2,1)S(1)} %get-tuple-element.105.second_ref.refs_7_, s32[8,128]{1,0:T(8,128)} %get-tuple-element.107.refs_0_, s32[8,128]{1,0:T(8,128)} %get-tuple-element.109.refs_1_, ...), custom_call_target="tpu_custom_call" | custom-call | flops 2147483648 | bytes 2097152 | tf_op jit(solution)/shard_map/project/pallas_call | solution.py:438
  101.8 2.1 %collective-permute-done.12.refs_6_ = bf16[512,256]{1,0:T(8,128)(2,1)S(1)} collective-permute-done((bf16[512,256]{1,0:T(8,128)(2,1)S(1)}, bf16[512,256]{1,0:T(8,128)(2,1)S(1)}, u32[]{:S(2)}, u32[]{:S(2)}) %collective-permute-start.12) | collective-permute-done | bytes 262176 | tf_op jit(solution)/shard_map/ppermute | solution.py:46
  103.8 0.8 collective-permute-done.13.refs_0_
  104.7 1.1 collective-permute-start.19
  105.8 0.5 collective-permute-start.20
  106.3 0.6 collective-permute-start.17
  106.9 0.1 collective-permute-done.19.refs_1_
  107.0 2.0 %collective-permute-start.18 = (bf16[512,256]{1,0:T(8,128)(2,1)S(1)}, bf16[512,256]{1,0:T(8,128)(2,1)S(1)}, u32[]{:S(2)}, u32[]{:S(2)}) collective-permute-start(bf16[512,256]{1,0:T(8,128)(2,1)S(1)} %collective-permute-done.15.refs_2_), channel_id=1, source_target_pairs={{0,5},{4,0},{1,4},{5,1},{2,7},{6,2},{3,6},{7,3},{8,13},{12,8},{9,1... | collective-permute-start | bytes 786440 | tf_op jit(solution)/shard_map/ppermute | solution.py:46
  109.0 5.6 %project.3.refs_9_ = bf16[2048,512]{1,0:T(8,128)(2,1)S(1)} custom-call(bf16[4,512,256]{2,1,0:T(8,128)(2,1)S(1)} %get-tuple-element.104.first_ref.refs_6_, bf16[1024,512]{1,0:T(8,128)(2,1)S(1)} %get-tuple-element.105.second_ref.refs_7_, bf16[512,256]{1,0:T(8,128)(2,1)S(1)} %collective-permute-done.13.refs_0_, ...), custom_call_target="tpu_custom_call" | custom-call | flops 4294967296 | bytes 4194304 | tf_op jit(solution)/shard_map/project/pallas_call | solution.py:438
  114.6 0.3 collective-permute-done.17.refs_10_
  114.9 1.4 collective-permute-start.23
  116.2 0.1 collective-permute-start.24
  116.4 1.1 collective-permute-done.23.refs_11_
  117.4 0.4 collective-permute-done.24.refs_13_
  117.8 22.9 %seeds.1 = bf16[2048,256]{1,0:T(8,128)(2,1)} custom-call(bf16[2048,1024]{1,0:T(8,128)(2,1)} %get-tuple-element.81.refs_0_, bf16[2048,1024]{1,0:T(8,128)(2,1)} %get-tuple-element.82.refs_1_, bf16[2048,1024]{1,0:T(8,128)(2,1)} %get-tuple-element.83.refs_2_, bf16[2048,1024]{1,0:T(8,128)(2,1)} %get-tuple-element.84.refs_3_, s32[2,1024]{1,0:T(2,128)S(1)} %reshape.38.refs_4_, ...), custom_call_target="tpu_custom_call" | custom-call | flops 8589934592 | bytes 16777216 | tf_op jit(solution)/shard_map/seeds/pallas_call | solution.py:484
  (65 shorter events, 0.4 us)
Async XLA Ops:
  0.0 18.4 %copy-start = (s32[1,32,128]{2,1,0:T(8,128)S(1)}, s32[1,32,128]{2,1,0:T(8,128)}, u32[]{:S(2)}) copy-start(s32[1,32,128]{2,1,0:T(8,128)} %param.17) | copy-start | bytes 49156
  0.1 0.7 copy-start.4
  0.8 17.8 %copy-start.1 = (s32[8192,10]{0,1:T(8,128)S(1)}, s32[8192,10]{0,1:T(8,128)}, u32[]{:S(2)}) copy-start(s32[8192,10]{0,1:T(8,128)} %param.13) | copy-start | bytes 983044
  0.8 17.8 %copy-start.2 = (s32[8192]{0:T(1024)S(1)}, s32[8192]{0:T(1024)}, u32[]{:S(2)}) copy-start(s32[8192]{0:T(1024)} %param.14) | copy-start | bytes 98308
  0.8 17.8 %copy-start.3 = (s32[8192]{0:T(1024)S(1)}, s32[8192]{0:T(1024)}, u32[]{:S(2)}) copy-start(s32[8192]{0:T(1024)} %param.15) | copy-start | bytes 98308
  6.4 22.8 %all-to-all-start = ((bf16[32,32,128]{2,1,0:T(8,128)(2,1)}), bf16[32,32,128]{2,1,0:T(8,128)(2,1)S(1)}, u32[]{:S(2)}, u32[]{:S(2)}) async-start(bf16[32,32,128]{2,1,0:T(8,128)(2,1)} %bitcast.6), calls=%async_computation | async-start | bytes 524288 | tf_op jit(solution)/shard_map/all_to_all | solution.py:528
  21.1 10.8 %copy-start.15 = (s32[2048,15]{0,1:T(8,128)S(1)}, s32[2048,15]{0,1:T(8,128)}, u32[]{:S(2)}) copy-start(s32[2048,15]{0,1:T(8,128)} %param.18) | copy-start | bytes 368644
  21.1 10.8 %copy-start.16 = (s32[2048]{0:T(1024)S(1)}, s32[2048]{0:T(1024)}, u32[]{:S(2)}) copy-start(s32[2048]{0:T(1024)} %param.20) | copy-start | bytes 24580
  29.2 6.4 %collective-permute-start = (bf16[1024,128]{1,0:T(8,128)(2,1)S(1)}, bf16[1024,128]{1,0:T(8,128)(2,1)S(1)}, u32[]{:S(2)}, u32[]{:S(2)}) collective-permute-start(bf16[1024,128]{1,0:T(8,128)(2,1)S(1)} %bitcast.13), channel_id=1, source_target_pairs={{0,4},{4,1},{1,5},{5,0},{2,6},{6,3},{3,7},{7,2},{8,12},{12,9},{9,1... | collective-permute-start | bytes 786440 | tf_op jit(solution)/shard_map/ppermute | solution.py:46
  30.4 5.2 %collective-permute-start.1 = (bf16[1024,128]{1,0:T(8,128)(2,1)S(1)}, bf16[1024,128]{1,0:T(8,128)(2,1)S(1)}, u32[]{:S(2)}, u32[]{:S(2)}) collective-permute-start(bf16[1024,128]{1,0:T(8,128)(2,1)S(1)} %bitcast.14), channel_id=1, source_target_pairs={{0,5},{4,0},{1,4},{5,1},{2,7},{6,2},{3,6},{7,3},{8,13},{12,8},{9,1... | collective-permute-start | bytes 786440 | tf_op jit(solution)/shard_map/ppermute | solution.py:46
  32.8 13.1 %copy-start.7 = (bf16[256,256]{1,0:T(8,128)(2,1)S(1)}, bf16[256,256]{1,0:T(8,128)(2,1)}, u32[]{:S(2)}) copy-start(bf16[256,256]{1,0:T(8,128)(2,1)} %refs_0_.2) | copy-start | bytes 393220
  35.7 12.6 %collective-permute-start.2 = (bf16[512,128]{1,0:T(8,128)(2,1)S(1)}, bf16[512,128]{1,0:T(8,128)(2,1)S(1)}, u32[]{:S(2)}, u32[]{:S(2)}) collective-permute-start(bf16[512,128]{1,0:T(8,128)(2,1)S(1)} %slice.12), channel_id=1, source_target_pairs={{0,4},{4,1},{1,5},{5,0},{2,6},{6,3},{3,7},{7,2},{8,12},{12,9},{9,1... | collective-permute-start | bytes 393224 | tf_op jit(solution)/shard_map/ppermute | solution.py:46
  37.2 11.0 %collective-permute-start.3 = (bf16[512,128]{1,0:T(8,128)(2,1)S(1)}, bf16[512,128]{1,0:T(8,128)(2,1)S(1)}, u32[]{:S(2)}, u32[]{:S(2)}) collective-permute-start(bf16[512,128]{1,0:T(8,128)(2,1)S(1)} %slice.13), channel_id=1, source_target_pairs={{0,5},{4,0},{1,4},{5,1},{2,7},{6,2},{3,6},{7,3},{8,13},{12,8},{9,1... | collective-permute-start | bytes 393224 | tf_op jit(solution)/shard_map/ppermute | solution.py:46
  45.9 15.3 %collective-permute-start.4 = (bf16[256,256]{1,0:T(8,128)(2,1)S(1)}, bf16[256,256]{1,0:T(8,128)(2,1)S(1)}, u32[]{:S(2)}, u32[]{:S(2)}) collective-permute-start(bf16[256,256]{1,0:T(8,128)(2,1)S(1)} %copy-done.7), channel_id=1, source_target_pairs={{0,5},{4,0},{1,4},{5,1},{2,7},{6,2},{3,6},{7,3},{8,13},{12,8},{9,1... | collective-permute-start | bytes 393224 | tf_op jit(solution)/shard_map/ppermute | solution.py:46
  47.3 13.9 %collective-permute-start.5 = (bf16[256,256]{1,0:T(8,128)(2,1)S(1)}, bf16[256,256]{1,0:T(8,128)(2,1)S(1)}, u32[]{:S(2)}, u32[]{:S(2)}) collective-permute-start(bf16[256,256]{1,0:T(8,128)(2,1)S(1)} %copy-done.7), channel_id=1, source_target_pairs={{0,1},{4,5},{1,0},{5,4},{2,3},{6,7},{3,2},{7,6},{8,9},{12,13},{9,8... | collective-permute-start | bytes 393224 | tf_op jit(solution)/shard_map/ppermute | solution.py:46
  47.9 13.3 %collective-permute-start.6 = (bf16[256,256]{1,0:T(8,128)(2,1)S(1)}, bf16[256,256]{1,0:T(8,128)(2,1)S(1)}, u32[]{:S(2)}, u32[]{:S(2)}) collective-permute-start(bf16[256,256]{1,0:T(8,128)(2,1)S(1)} %copy-done.7), channel_id=1, source_target_pairs={{0,4},{4,1},{1,5},{5,0},{2,6},{6,3},{3,7},{7,2},{8,12},{12,9},{9,1... | collective-permute-start | bytes 393224 | tf_op jit(solution)/shard_map/ppermute | solution.py:46
  48.3 23.1 %copy-start.5 = (bf16[1024,256]{1,0:T(8,128)(2,1)S(1)}, bf16[1024,256]{1,0:T(8,128)(2,1)}, u32[]{:S(2)}) copy-start(bf16[1024,256]{1,0:T(8,128)(2,1)} %refs_8_) | copy-start | bytes 1572868
  48.3 26.4 %copy-start.17 = (s32[2048]{0:T(1024)S(1)}, s32[2048]{0:T(1024)}, u32[]{:S(2)}) copy-start(s32[2048]{0:T(1024)} %param.19) | copy-start | bytes 24580
  61.2 25.6 %copy-start.8 = (bf16[256,256]{1,0:T(8,128)(2,1)}, bf16[256,256]{1,0:T(8,128)(2,1)S(1)}, u32[]{:S(2)}) copy-start(bf16[256,256]{1,0:T(8,128)(2,1)S(1)} %collective-permute-done.4.refs_2_) | copy-start | bytes 393220
  61.2 25.6 %copy-start.9 = (bf16[256,256]{1,0:T(8,128)(2,1)}, bf16[256,256]{1,0:T(8,128)(2,1)S(1)}, u32[]{:S(2)}) copy-start(bf16[256,256]{1,0:T(8,128)(2,1)S(1)} %collective-permute-done.5.refs_4_) | copy-start | bytes 393220
  61.2 25.6 %copy-start.10 = (bf16[256,256]{1,0:T(8,128)(2,1)}, bf16[256,256]{1,0:T(8,128)(2,1)S(1)}, u32[]{:S(2)}) copy-start(bf16[256,256]{1,0:T(8,128)(2,1)S(1)} %collective-permute-done.6.refs_6_) | copy-start | bytes 393220
  61.2 25.7 %all-to-all-start.1 = ((bf16[32,32,256]{2,1,0:T(8,128)(2,1)}), bf16[32,32,256]{2,1,0:T(8,128)(2,1)S(1)}, u32[]{:S(2)}, u32[]{:S(2)}) async-start(bf16[32,32,256]{2,1,0:T(8,128)(2,1)} %bitcast.20), calls=%async_computation.1 | async-start | bytes 1048576 | tf_op jit(solution)/shard_map/all_to_all | solution.py:528
  71.4 15.5 %collective-permute-start.7 = (bf16[1024,256]{1,0:T(8,128)(2,1)S(1)}, bf16[1024,256]{1,0:T(8,128)(2,1)S(1)}, u32[]{:S(2)}, u32[]{:S(2)}) collective-permute-start(bf16[1024,256]{1,0:T(8,128)(2,1)S(1)} %copy-done.5), channel_id=1, source_target_pairs={{0,1},{4,5},{1,0},{5,4},{2,3},{6,7},{3,2},{7,6},{8,9},{12,13},{9,8... | collective-permute-start | bytes 1572872 | tf_op jit(solution)/shard_map/ppermute | solution.py:46
  74.7 12.1 %collective-permute-start.10 = (bf16[256,256]{1,0:T(8,128)(2,1)S(1)}, bf16[256,256]{1,0:T(8,128)(2,1)S(1)}, u32[]{:S(2)}, u32[]{:S(2)}) collective-permute-start(bf16[256,256]{1,0:T(8,128)(2,1)S(1)} %collective-permute-done.5.refs_4_), channel_id=1, source_target_pairs={{0,2},{2,0},{1,3},{3,1},{4,6},{6,4},{5,7},{7,5},{8,10},{10,8},{9,1... | collective-permute-start | bytes 393224 | tf_op jit(solution)/shard_map/ppermute | solution.py:50
  78.8 8.0 %collective-permute-start.11 = (bf16[256,256]{1,0:T(8,128)(2,1)S(1)}, bf16[256,256]{1,0:T(8,128)(2,1)S(1)}, u32[]{:S(2)}, u32[]{:S(2)}) collective-permute-start(bf16[256,256]{1,0:T(8,128)(2,1)S(1)} %collective-permute-done.6.refs_6_), channel_id=1, source_target_pairs={{0,2},{2,0},{1,3},{3,1},{4,6},{6,4},{5,7},{7,5},{8,10},{10,8},{9,1... | collective-permute-start | bytes 393224 | tf_op jit(solution)/shard_map/ppermute | solution.py:50
  78.9 8.0 %collective-permute-start.8 = (bf16[256,256]{1,0:T(8,128)(2,1)S(1)}, bf16[256,256]{1,0:T(8,128)(2,1)S(1)}, u32[]{:S(2)}, u32[]{:S(2)}) collective-permute-start(bf16[256,256]{1,0:T(8,128)(2,1)S(1)} %copy-done.7), channel_id=1, source_target_pairs={{0,2},{2,0},{1,3},{3,1},{4,6},{6,4},{5,7},{7,5},{8,10},{10,8},{9,1... | collective-permute-start | bytes 393224 | tf_op jit(solution)/shard_map/ppermute | solution.py:50
  79.3 7.6 %collective-permute-start.9 = (bf16[256,256]{1,0:T(8,128)(2,1)S(1)}, bf16[256,256]{1,0:T(8,128)(2,1)S(1)}, u32[]{:S(2)}, u32[]{:S(2)}) collective-permute-start(bf16[256,256]{1,0:T(8,128)(2,1)S(1)} %collective-permute-done.4.refs_2_), channel_id=1, source_target_pairs={{0,2},{2,0},{1,3},{3,1},{4,6},{6,4},{5,7},{7,5},{8,10},{10,8},{9,1... | collective-permute-start | bytes 393224 | tf_op jit(solution)/shard_map/ppermute | solution.py:50
  86.8 7.7 %copy-start.11 = (bf16[256,256]{1,0:T(8,128)(2,1)}, bf16[256,256]{1,0:T(8,128)(2,1)S(1)}, u32[]{:S(2)}) copy-start(bf16[256,256]{1,0:T(8,128)(2,1)S(1)} %collective-permute-done.10.refs_5_) | copy-start | bytes 393220
  86.8 7.7 %copy-start.12 = (bf16[256,256]{1,0:T(8,128)(2,1)}, bf16[256,256]{1,0:T(8,128)(2,1)S(1)}, u32[]{:S(2)}) copy-start(bf16[256,256]{1,0:T(8,128)(2,1)S(1)} %collective-permute-done.11.refs_7_) | copy-start | bytes 393220
  86.9 7.7 %copy-start.13 = (bf16[256,256]{1,0:T(8,128)(2,1)}, bf16[256,256]{1,0:T(8,128)(2,1)S(1)}, u32[]{:S(2)}) copy-start(bf16[256,256]{1,0:T(8,128)(2,1)S(1)} %collective-permute-done.8.refs_1_) | copy-start | bytes 393220
  86.9 7.7 %copy-start.14 = (bf16[256,256]{1,0:T(8,128)(2,1)}, bf16[256,256]{1,0:T(8,128)(2,1)S(1)}, u32[]{:S(2)}) copy-start(bf16[256,256]{1,0:T(8,128)(2,1)S(1)} %collective-permute-done.9.refs_3_) | copy-start | bytes 393220
  86.9 7.7 %copy-start.6 = (bf16[1024,256]{1,0:T(8,128)(2,1)}, bf16[1024,256]{1,0:T(8,128)(2,1)S(1)}, u32[]{:S(2)}) copy-start(bf16[1024,256]{1,0:T(8,128)(2,1)S(1)} %collective-permute-done.7.refs_9_) | copy-start | bytes 1572868
  86.9 12.1 %collective-permute-start.16 = (bf16[1024,256]{1,0:T(8,128)(2,1)S(1)}, bf16[1024,256]{1,0:T(8,128)(2,1)S(1)}, u32[]{:S(2)}, u32[]{:S(2)}) collective-permute-start(bf16[1024,256]{1,0:T(8,128)(2,1)S(1)} %bitcast.10), channel_id=1, source_target_pairs={{0,2},{2,0},{1,3},{3,1},{4,6},{6,4},{5,7},{7,5},{8,10},{10,8},{9,1... | collective-permute-start | bytes 1572872 | tf_op jit(solution)/shard_map/ppermute | solution.py:50
  89.1 9.1 %collective-permute-start.14 = (bf16[512,256]{1,0:T(8,128)(2,1)S(1)}, bf16[512,256]{1,0:T(8,128)(2,1)S(1)}, u32[]{:S(2)}, u32[]{:S(2)}) collective-permute-start(bf16[512,256]{1,0:T(8,128)(2,1)S(1)} %get-tuple-element.119), channel_id=1, source_target_pairs={{0,4},{4,1},{1,5},{5,0},{2,6},{6,3},{3,7},{7,2},{8,12},{12,9},{9,1... | collective-permute-start | bytes 786440 | tf_op jit(solution)/shard_map/ppermute | solution.py:46
  91.5 7.6 %collective-permute-start.15 = (bf16[512,256]{1,0:T(8,128)(2,1)S(1)}, bf16[512,256]{1,0:T(8,128)(2,1)S(1)}, u32[]{:S(2)}, u32[]{:S(2)}) collective-permute-start(bf16[512,256]{1,0:T(8,128)(2,1)S(1)} %get-tuple-element.120), channel_id=1, source_target_pairs={{0,5},{4,0},{1,4},{5,1},{2,7},{6,2},{3,6},{7,3},{8,13},{12,8},{9,1... | collective-permute-start | bytes 786440 | tf_op jit(solution)/shard_map/ppermute | solution.py:46
  91.9 11.9 %collective-permute-start.12 = (bf16[512,256]{1,0:T(8,128)(2,1)S(1)}, bf16[512,256]{1,0:T(8,128)(2,1)S(1)}, u32[]{:S(2)}, u32[]{:S(2)}) collective-permute-start(bf16[512,256]{1,0:T(8,128)(2,1)S(1)} %get-tuple-element.120), channel_id=1, source_target_pairs={{0,4},{4,1},{1,5},{5,0},{2,6},{6,3},{3,7},{7,2},{8,12},{12,9},{9,1... | collective-permute-start | bytes 786440 | tf_op jit(solution)/shard_map/ppermute | solution.py:46
  92.9 11.7 %collective-permute-start.13 = (bf16[512,256]{1,0:T(8,128)(2,1)S(1)}, bf16[512,256]{1,0:T(8,128)(2,1)S(1)}, u32[]{:S(2)}, u32[]{:S(2)}) collective-permute-start(bf16[512,256]{1,0:T(8,128)(2,1)S(1)} %get-tuple-element.119), channel_id=1, source_target_pairs={{0,5},{4,0},{1,4},{5,1},{2,7},{6,2},{3,6},{7,3},{8,13},{12,8},{9,1... | collective-permute-start | bytes 786440 | tf_op jit(solution)/shard_map/ppermute | solution.py:46
  104.7 2.3 %collective-permute-start.19 = (bf16[512,256]{1,0:T(8,128)(2,1)S(1)}, bf16[512,256]{1,0:T(8,128)(2,1)S(1)}, u32[]{:S(2)}, u32[]{:S(2)}) collective-permute-start(bf16[512,256]{1,0:T(8,128)(2,1)S(1)} %collective-permute-done.13.refs_0_), channel_id=1, source_target_pairs={{0,2},{2,0},{1,3},{3,1},{4,6},{6,4},{5,7},{7,5},{8,10},{10,8},{9,1... | collective-permute-start | bytes 786440 | tf_op jit(solution)/shard_map/ppermute | solution.py:50
  105.8 3.2 %collective-permute-start.22 = (bf16[512,256]{1,0:T(8,128)(2,1)S(1)}, bf16[512,256]{1,0:T(8,128)(2,1)S(1)}, u32[]{:S(2)}, u32[]{:S(2)}) collective-permute-start(bf16[512,256]{1,0:T(8,128)(2,1)S(1)} %collective-permute-done.12.refs_6_), channel_id=1, source_target_pairs={{0,2},{2,0},{1,3},{3,1},{4,6},{6,4},{5,7},{7,5},{8,10},{10,8},{9,1... | collective-permute-start | bytes 786440 | tf_op jit(solution)/shard_map/ppermute | solution.py:50
  105.8 3.2 %collective-permute-start.20 = (bf16[512,256]{1,0:T(8,128)(2,1)S(1)}, bf16[512,256]{1,0:T(8,128)(2,1)S(1)}, u32[]{:S(2)}, u32[]{:S(2)}) collective-permute-start(bf16[512,256]{1,0:T(8,128)(2,1)S(1)} %collective-permute-done.15.refs_2_), channel_id=1, source_target_pairs={{0,2},{2,0},{1,3},{3,1},{4,6},{6,4},{5,7},{7,5},{8,10},{10,8},{9,1... | collective-permute-start | bytes 786440 | tf_op jit(solution)/shard_map/ppermute | solution.py:50
  106.3 2.7 %collective-permute-start.21 = (bf16[512,256]{1,0:T(8,128)(2,1)S(1)}, bf16[512,256]{1,0:T(8,128)(2,1)S(1)}, u32[]{:S(2)}, u32[]{:S(2)}) collective-permute-start(bf16[512,256]{1,0:T(8,128)(2,1)S(1)} %collective-permute-done.14.refs_4_), channel_id=1, source_target_pairs={{0,2},{2,0},{1,3},{3,1},{4,6},{6,4},{5,7},{7,5},{8,10},{10,8},{9,1... | collective-permute-start | bytes 786440 | tf_op jit(solution)/shard_map/ppermute | solution.py:50
  106.3 8.6 %collective-permute-start.17 = (bf16[512,256]{1,0:T(8,128)(2,1)S(1)}, bf16[512,256]{1,0:T(8,128)(2,1)S(1)}, u32[]{:S(2)}, u32[]{:S(2)}) collective-permute-start(bf16[512,256]{1,0:T(8,128)(2,1)S(1)} %collective-permute-done.14.refs_4_), channel_id=1, source_target_pairs={{0,4},{4,1},{1,5},{5,0},{2,6},{6,3},{3,7},{7,2},{8,12},{12,9},{9,1... | collective-permute-start | bytes 786440 | tf_op jit(solution)/shard_map/ppermute | solution.py:46
  107.0 7.9 %collective-permute-start.18 = (bf16[512,256]{1,0:T(8,128)(2,1)S(1)}, bf16[512,256]{1,0:T(8,128)(2,1)S(1)}, u32[]{:S(2)}, u32[]{:S(2)}) collective-permute-start(bf16[512,256]{1,0:T(8,128)(2,1)S(1)} %collective-permute-done.15.refs_2_), channel_id=1, source_target_pairs={{0,5},{4,0},{1,4},{5,1},{2,7},{6,2},{3,6},{7,3},{8,13},{12,8},{9,1... | collective-permute-start | bytes 786440 | tf_op jit(solution)/shard_map/ppermute | solution.py:46
  114.9 2.5 %collective-permute-start.23 = (bf16[512,256]{1,0:T(8,128)(2,1)S(1)}, bf16[512,256]{1,0:T(8,128)(2,1)S(1)}, u32[]{:S(2)}, u32[]{:S(2)}) collective-permute-start(bf16[512,256]{1,0:T(8,128)(2,1)S(1)} %collective-permute-done.17.refs_10_), channel_id=1, source_target_pairs={{0,2},{2,0},{1,3},{3,1},{4,6},{6,4},{5,7},{7,5},{8,10},{10,8},{9,1... | collective-permute-start | bytes 786440 | tf_op jit(solution)/shard_map/ppermute | solution.py:50
  116.2 1.5 %collective-permute-start.24 = (bf16[512,256]{1,0:T(8,128)(2,1)S(1)}, bf16[512,256]{1,0:T(8,128)(2,1)S(1)}, u32[]{:S(2)}, u32[]{:S(2)}) collective-permute-start(bf16[512,256]{1,0:T(8,128)(2,1)S(1)} %collective-permute-done.18.refs_12_), channel_id=1, source_target_pairs={{0,2},{2,0},{1,3},{3,1},{4,6},{6,4},{5,7},{7,5},{8,10},{10,8},{9,1... | collective-permute-start | bytes 786440 | tf_op jit(solution)/shard_map/ppermute | solution.py:50

commit v4 on v3

--- a/solution.py
+++ b/solution.py
@@ -83,45 +83,28 @@
 def store_counts(counts, out_refs, start):
     each = SLOTS // SPLIT
     for k in range(SLOTS):
-        out_refs[k // each][pl.ds(start, SLOTS), k % each * LOW : (k % each + 1) * LOW] = counts[
+        out_refs[k // each][start : start + SLOTS, k % each * LOW : (k % each + 1) * LOW] = counts[
             k * SLOTS : (k + 1) * SLOTS, :
         ]
 
 
-def rows_at(index, data_ref):
+def own_and_total(index, counts_refs, self_ref, near_ref):
     rows = index.shape[0]
     lane = lax.broadcasted_iota(jnp.int32, (rows, LOW), 1).astype(F32).astype(BF16)
     spread = lambda a: jnp.broadcast_to(a.astype(F32), (rows, LOW)).astype(BF16)
     found = jnp.where(lane == spread(index & (LOW - 1)), spread(index >> 8), jnp.full((), -1, BF16))
     one, zero = jnp.ones((), BF16), jnp.zeros((), BF16)
-    step = data_ref.shape[0] // SPLIT
-    total = 0.0
-    for start in range(0, data_ref.shape[0], step):
+    own, total, start = 0.0, 0.0, 0
+    for ref in counts_refs:
+        stop = start + ref.shape[1]
         hot = [
             jnp.where(found == jnp.full((), k, BF16), one, zero)
-            for k in range(start // LOW, (start + step) // LOW)
+            for k in range(start // LOW, stop // LOW)
         ]
-        total = total + dot(jnp.concatenate(hot, 1), data_ref[start : start + step, :])
-    return total
-
-
-def counted(copy, buffer_ref, first, data_ref):
-    step = data_ref.shape[0] // SPLIT
-    total = 0.0
-    for k in range(SPLIT):
-        copy(first + k).wait()
-        total = total + dot(buffer_ref[first + k], data_ref[k * step : (k + 1) * step, :])
-    return total
-
-
-def fetch_counts(counts_refs, buffer_ref, sems):
-    rows = buffer_ref.shape[1]
-    for k in range(buffer_ref.shape[0]):
-        part = k // SPLIT * rows
-        source = counts_refs[k % SPLIT].at[part : part + rows, :]
-        pltpu.make_async_copy(source, buffer_ref.at[k], sems.at[k]).start()
-    source = counts_refs[0].at[:rows, :]
-    return lambda k: pltpu.make_async_copy(source, buffer_ref.at[k], sems.at[k])
+        own = own + dot(jnp.concatenate(hot, 1), self_ref[start:stop, :])
+        total = total + dot(ref[...], near_ref[start:stop, :])
+        start = stop
+    return own, total
 
 
 def table_kernel(slots_ref, own_ref, size_ref, out_ref, lines_ref):
@@ -140,7 +123,7 @@
 
 def node_table(slots, own, sizes):
     stored = slots.shape[1]
-    step = 512
+    step = 1024
     return pl.pallas_call(
         table_kernel,
         grid=(stored // step,),
@@ -157,12 +140,8 @@
     out_refs, rows_ref = refs[:SPLIT], refs[-1]
     step = rows_ref.shape[0]
     base = pl.multiple_of(pl.program_id(0) * step, step)
-
-    @pl.loop(0, step, step=32)
-    def _(start):
-        for i in range(32):
-            rows_ref[pl.ds(start + i, 1), :] = table_ref[pl.ds(request_ref[base + start + i], 1), :]
-
+    for i in range(step):
+        rows_ref[i : i + 1, :] = table_ref[pl.ds(request_ref[base + i], 1), :]
     rows = rows_ref[...]
     nodes_ref[...] = rows
     size = rows[:, FAN + 1 : FAN + 2]
@@ -174,7 +153,7 @@
 
 def node_counts(requests, x, table, positions):
     targets = requests.shape[0]
-    step = 128
+    step = 256
     return pl.pallas_call(
         node_kernel,
         grid_spec=pltpu.PrefetchScalarGridSpec(
@@ -215,20 +194,19 @@
     rows = lax.broadcasted_iota(jnp.int32, (LOW, LOW), 0).astype(F32).astype(BF16)
     one = jnp.ones((), BF16)
     zero = jnp.zeros((), BF16)
-
-    @pl.loop(0, code_ref.shape[0], step=4)
-    def _(first):
-        for i in range(4):
-            code = code_ref[pl.ds(first + i, 1), :]
-            left = jnp.where(rows == ((code >> 8) - 1).astype(F32).astype(BF16), one, zero)
-            right = jnp.where(rows == (code & (LOW - 1)).astype(F32).astype(BF16), one, zero)
-            counts = lax.dot_general(left, right, (((1,), (1,)), ((), ())), preferred_element_type=F32)
-            store_counts(counts.astype(BF16), out_refs, pl.multiple_of((first + i) * SLOTS, SLOTS))
+    code = code_ref[...]
+    high = ((code >> 8) - 1).astype(F32)
+    low = (code & (LOW - 1)).astype(F32)
+    for g in range(code_ref.shape[0]):
+        left = jnp.where(rows == high[g : g + 1, :].astype(BF16), one, zero)
+        right = jnp.where(rows == low[g : g + 1, :].astype(BF16), one, zero)
+        counts = lax.dot_general(left, right, (((1,), (1,)), ((), ())), preferred_element_type=F32)
+        store_counts(counts.astype(BF16), out_refs, g * SLOTS)
 
 
 def slot_counts(code, positions, part, before=()):
     groups, width = code.shape
-    step = 8
+    step = 16
     steps = groups // step // 2
     width_out = positions // SPLIT
     return pl.pallas_call(
@@ -265,15 +243,15 @@
             first_ref[column, pl.ds(at, half), :] = block[pl.ds(start, half), :]
     columns = mine_ref.shape[1]
 
-    def join(left_ref, right_ref):
-        @pl.loop(0, second_ref.shape[0] // half)
-        def _(i):
-            rows = pl.ds(pl.multiple_of(i * half, half), half)
-            second_ref[rows, :columns] = left_ref[rows, :]
-            second_ref[rows, columns:] = right_ref[rows, :]
-
-    pl.when(x < 2)(lambda: join(mine_ref, other_ref))
-    pl.when(x >= 2)(lambda: join(other_ref, mine_ref))
+    @pl.when(x < 2)
+    def _():
+        second_ref[:, :columns] = mine_ref[...]
+        second_ref[:, columns:] = other_ref[...]
+
+    @pl.when(x >= 2)
+    def _():
+        second_ref[:, :columns] = other_ref[...]
+        second_ref[:, columns:] = mine_ref[...]
 
 
 def assemble(at, blocks, mine, other):
@@ -353,83 +331,72 @@
 
 def mean_kernel(tokens, x_ref, *refs):
     counts_refs, nodes_ref, refs = refs[:SPLIT], refs[SPLIT], refs[SPLIT + 1 :]
-    pieces, (out_ref, data_ref, buffer_ref, sems) = refs[tokens:-4], refs[-4:]
+    pieces, (out_ref, data_ref) = refs[tokens:-2], refs[-2:]
     width = out_ref.shape[1] // 2
-    copy = fetch_counts(counts_refs, buffer_ref, sems)
-    start = 0
-    for piece in pieces:
-        data_ref[start : start + piece.shape[0], :] = piece[...]
-        start += piece.shape[0]
+
+    @pl.when(pl.program_id(0) == 0)
+    def _():
+        start = 0
+        for piece in pieces:
+            data_ref[start : start + piece.shape[0], :] = piece[...]
+            start += piece.shape[0]
+
     own_at = place(nodes_ref[:, FAN : FAN + 1], x_ref[0])
     size = nodes_ref[:, FAN + 1 : FAN + 2].astype(F32)
-    out_ref[:, :width] = rows_at(own_at, data_ref).astype(BF16)
-    total = counted(copy, buffer_ref, 0, data_ref)
+    own, total = own_and_total(own_at, counts_refs, data_ref, data_ref)
+    out_ref[:, :width] = own.astype(BF16)
     out_ref[:, width:] = (total / size).astype(BF16)
 
 
 def own_and_mean(x, counts, nodes, pieces, after):
-    targets, each = counts[0].shape
+    targets, positions = counts[0].shape[0], SPLIT * counts[0].shape[1]
     width = pieces[0].shape[1]
+    tile = 256
     return pl.pallas_call(
         functools.partial(mean_kernel, len(after)),
         grid_spec=pltpu.PrefetchScalarGridSpec(
             num_scalar_prefetch=1,
-            grid=(1,),
-            in_specs=in_place(SPLIT)
-            + [pl.BlockSpec(nodes.shape, lambda i, x: (0, 0))]
+            grid=(targets // tile,),
+            in_specs=[pl.BlockSpec((tile, positions // SPLIT), lambda i, x: (i, 0))] * SPLIT
+            + [pl.BlockSpec((tile, SLOTS), lambda i, x: (i, 0))]
             + in_place(len(after))
             + in_vmem(len(pieces)),
-            out_specs=pl.BlockSpec((targets, 2 * width), lambda i, x: (0, 0)),
+            out_specs=pl.BlockSpec((tile, 2 * width), lambda i, x: (i, 0)),
             scratch_shapes=[
-                pltpu.VMEM((SPLIT * each, width), BF16),
-                pltpu.VMEM((SPLIT, targets, each), BF16),
-                pltpu.SemaphoreType.DMA((SPLIT,)),
+                pltpu.VMEM((positions, width), BF16),
             ],
         ),
         out_shape=pltpu.HBM((targets, 2 * width), BF16),
-        compiler_params=pltpu.CompilerParams(vmem_limit_bytes=24 * MIB),
+        compiler_params=pltpu.CompilerParams(vmem_limit_bytes=14 * MIB),
         cost_estimate=pl.CostEstimate(
-            flops=4 * targets * SPLIT * each * width,
+            flops=4 * targets * positions * width,
             transcendentals=0,
-            bytes_accessed=targets * SPLIT * each * 2,
+            bytes_accessed=targets * positions * 2,
         ),
         name="own_and_mean",
     )(x.reshape(1), *[to_hbm(c) for c in counts], to_hbm(nodes), *map(to_hbm, after), *pieces)
 
 
-def project_into(out_ref, start, sides, first_ref, second_ref):
-    mine, other = (side[...] for side in sides)
-    rows, k = mine.shape
-    acc = jnp.zeros((rows, out_ref.shape[1]), F32)
-    for h in range(first_ref.shape[0]):
-        pre = dot(mine, first_ref[h, :k, :]) + dot(other, first_ref[h, k:, :])
-        hidden = jnp.maximum(pre, 0.0).astype(BF16)
-        width = hidden.shape[1]
-        acc = acc + dot(hidden, second_ref[h * width : (h + 1) * width, :])
-    out_ref[pl.ds(start, rows), :] = acc.astype(BF16)
-
-
-def stage(side_refs, pieces):
+def project_into(out_ref, start, mine_ref, other_ref, first_ref, second_ref):
+    rows, k = mine_ref.shape
+    tile = min(rows, 512)
+    for at in range(0, rows, tile):
+        mine, other = mine_ref[at : at + tile, :], other_ref[at : at + tile, :]
+        acc = jnp.zeros((tile, out_ref.shape[1]), F32)
+        for h in range(first_ref.shape[0]):
+            pre = dot(mine, first_ref[h, :k, :]) + dot(other, first_ref[h, k:, :])
+            hidden = jnp.maximum(pre, 0.0).astype(BF16)
+            width = hidden.shape[1]
+            acc = acc + dot(hidden, second_ref[h * width : (h + 1) * width, :])
+        out_ref[start + at : start + at + tile, :] = acc.astype(BF16)
+
+
+def project_kernel(tokens, first_ref, second_ref, *refs):
+    pieces, out_ref = refs[tokens:-1], refs[-1]
     start = 0
     for mine, other in zip(pieces[::2], pieces[1::2]):
-        for side, piece in zip(side_refs, (mine, other)):
-            side[start : start + piece.shape[0], :] = piece[...]
+        project_into(out_ref, start, mine, other, first_ref, second_ref)
         start += mine.shape[0]
-
-
-def project_kernel(tokens, first_ref, second_ref, *refs):
-    pieces, (out_ref, mine_ref, other_ref) = refs[tokens:-3], refs[-3:]
-    if len(pieces) == 2:
-        project_into(out_ref, 0, pieces, first_ref, second_ref)
-        return
-    stage((mine_ref, other_ref), pieces)
-    rows = 1024
-
-    @pl.loop(0, out_ref.shape[0] // rows)
-    def _(part):
-        at = pl.multiple_of(part * rows, rows)
-        sides = [side.at[pl.ds(at, rows), :] for side in (mine_ref, other_ref)]
-        project_into(out_ref, at, sides, first_ref, second_ref)
 
 
 def project(first, second, *pieces, after=()):
@@ -440,8 +407,7 @@
         in_specs=in_vmem(2) + in_place(len(after)) + in_vmem(len(pieces)),
         out_specs=in_vmem(1)[0],
         out_shape=jax.ShapeDtypeStruct((rows, width), BF16),
-        scratch_shapes=[pltpu.VMEM((rows, k), BF16)] * 2,
-        compiler_params=pltpu.CompilerParams(vmem_limit_bytes=10 * MIB),
+        compiler_params=pltpu.CompilerParams(vmem_limit_bytes=8 * MIB),
         cost_estimate=pl.CostEstimate(
             flops=2 * rows * second.shape[0] * (2 * k + width),
             transcendentals=0,
@@ -453,50 +419,43 @@
 
 def seed_kernel(*refs):
     counts_refs, (own_ref, size_ref, first_ref, second_ref), refs = refs[:SPLIT], refs[SPLIT : SPLIT + 4], refs[SPLIT + 4 :]
-    (mine_ref, near_ref), far, refs = refs[:2], refs[2:-6], refs[-6:]
-    out_ref, data_ref, buffer_ref, sides, sems = *refs[:3], refs[3:5], refs[5]
+    (mine_ref, near_ref), far, (out_ref, data_ref) = refs[:2], refs[2:-2], refs[-2:]
     width = out_ref.shape[1]
     block = mine_ref.shape[0]
-    copy = fetch_counts(counts_refs, buffer_ref, sems)
-    data_ref[:block, :] = mine_ref[...]
-    data_ref[block : 2 * block, :] = near_ref[:block, :]
-    data_ref[3 * block :, :] = near_ref[block:, :]
-    stage(sides, far)
-    project_into(data_ref, 2 * block, sides, first_ref, second_ref)
-    rows = buffer_ref.shape[1]
-
-    @pl.loop(0, out_ref.shape[0] // rows)
-    def _(part):
-        places, sizes = own_ref[pl.ds(part, 1), :], size_ref[pl.ds(part, 1), :]
-        tiles = range(0, rows, LOW)
-        own_at = jnp.concatenate([column(places[:, t : t + LOW]) for t in tiles], 0).astype(jnp.int32)
-        size = jnp.concatenate([column(sizes[:, t : t + LOW]) for t in tiles], 0)
-        own = rows_at(own_at, data_ref.at[:, :width])
-        total = counted(copy, buffer_ref, part * SPLIT, data_ref.at[:, width:])
-        start = pl.multiple_of(part * rows, rows)
-        out_ref[pl.ds(start, rows), :] = (own + total / size).astype(BF16)
-
-
-def seeds(counts, places, sizes, first, second, own, near, far):
-    targets, each = counts[0].shape
+
+    @pl.when(pl.program_id(0) == 0)
+    def _():
+        data_ref[:block, :] = mine_ref[...]
+        data_ref[block : 2 * block, :] = near_ref[:block, :]
+        data_ref[3 * block :, :] = near_ref[block:, :]
+        start = 2 * block
+        for mine, other in zip(far[::2], far[1::2]):
+            project_into(data_ref, start, mine, other, first_ref, second_ref)
+            start += mine.shape[0]
+
+    own_at = column(own_ref[...]).astype(jnp.int32)
+    own, total = own_and_total(own_at, counts_refs, data_ref.at[:, :width], data_ref.at[:, width:])
+    out_ref[...] = (own + total / column(size_ref[...])).astype(BF16)
+
+
+def seeds(places, counts, sizes, first, second, own, near, far):
+    targets, positions = counts[0].shape[0], SPLIT * counts[0].shape[1]
     width = second.shape[1] // 2
-    parts, rows = places.shape
+    tile = 256
     return pl.pallas_call(
         seed_kernel,
-        in_specs=in_place(SPLIT) + in_vmem(6 + len(far)),
-        out_specs=in_vmem(1)[0],
+        grid=(targets // tile,),
+        in_specs=[pl.BlockSpec((tile, positions // SPLIT), lambda i: (i, 0))] * SPLIT
+        + [pl.BlockSpec((1, tile), lambda i: (0, i))] * 2
+        + in_vmem(4 + len(far)),
+        out_specs=pl.BlockSpec((tile, width), lambda i: (i, 0)),
         out_shape=jax.ShapeDtypeStruct((targets, width), BF16),
-        scratch_shapes=[
-            pltpu.VMEM((SPLIT * each, 2 * width), BF16),
-            pltpu.VMEM((parts * SPLIT, rows, each), BF16),
-            *[pltpu.VMEM((own.shape[0], first.shape[1] // 2), BF16)] * 2,
-            pltpu.SemaphoreType.DMA((parts * SPLIT,)),
-        ],
-        compiler_params=pltpu.CompilerParams(vmem_limit_bytes=30 * MIB),
+        scratch_shapes=[pltpu.VMEM((positions, 2 * width), BF16)],
+        compiler_params=pltpu.CompilerParams(vmem_limit_bytes=18 * MIB),
         cost_estimate=pl.CostEstimate(
-            flops=4 * targets * SPLIT * each * width,
+            flops=4 * targets * positions * width,
             transcendentals=0,
-            bytes_accessed=targets * SPLIT * each * 2,
+            bytes_accessed=targets * positions * 2,
         ),
         name="seeds",
     )(*[to_hbm(c) for c in counts], places, sizes, first, second, own, near, *far)
@@ -553,10 +512,9 @@
     other_rows = send(weight_two, ACROSS)
     *counts_two, token = slot_counts(code, positions, 1, counts_two)
     first_blocks = [b for block in first_blocks for b in (block, to_hbm(swap(block)))]
-    own_at = place(self_hid, x).reshape(2, -1)
-    sizes = count_hid.reshape(2, -1)
-    arrived, own_at, sizes, token, weight_two, other_rows, *first_blocks = together(
-        (arrived, own_at, sizes, token, weight_two, other_rows, *first_blocks)
+    own_at = place(self_hid, x)[None]
+    arrived, own_at, token, weight_two, other_rows, *first_blocks = together(
+        (arrived, own_at, token, weight_two, other_rows, *first_blocks)
     )
     first, second, ready = assemble(at, first_blocks, weight_two, other_rows)
     cut = arrived.shape[0] // 2
@@ -575,7 +533,7 @@
     near = project(first, second, *near)
     far_low, far_high, near = together((far_low, far_high, near))
     far = (far_low, swap(far_low), far_high, swap(far_high))
-    return seeds(counts_two, own_at, sizes, first, second, own, near, far)
+    return seeds(own_at, counts_two, count_hid[None], first, second, own, near, far)
 
 
 def solution(mesh):

time: 141 us -> 125 us (0.89)
  Pallas kernels: 77.6 us -> 58.6 us
  waiting for transfers between devices: 9.4 us -> 10.9 us
    pallas_call x1, Pallas kernels: 22.9 us -> 16.6 us  [seeds(): pl.pallas_call(seed_kernel, grid=(targets // tile,), in_specs=[pl.BlockSp...]
    pallas_call x2, Pallas kernels: 14.7 us -> 9.53 us  [slot_counts(): pl.pallas_call(slot_kernel, grid=(steps,), in_specs=[pl.BlockSpec((step,...]
    pallas_call x1, Pallas kernels: 12.9 us -> 7.97 us  [own_and_mean(): pl.pallas_call(functools.partial(mean_kernel, len(after)), grid_spec=pltp...]
    ppermute x11, starting transfers between devices: 9.97 us -> 12.5 us  [swap(): return lax.ppermute(block, 'core', SWAP)]
    pallas_call x1, Pallas kernels: 8.07 us -> 6.34 us  [node_counts(): pl.pallas_call(node_kernel, grid_spec=pltpu.PrefetchScalarGridSpec(num_sc...]
  transfers between devices with their start and end apart: 27 -> 27, of which waited for: 9 -> 10; matrix products, arithmetic and copies ran while one was open for 1% -> 1% of each run, Pallas kernels for 35% -> 29%
where the time goes in v4:
time: 125 us; the launch traced here: 124 us
  Pallas kernels  58.6 us (47%)
  starting transfers between devices  52.7 us (42%)
  waiting for transfers between devices  10.9 us (9%)
  local copies, waits for them, and re-layouts  1.77 us (1%)
    all_to_all x2, starting transfers between devices, exchange(): return lax.all_to_all(pieces, 'dom', 0, 0, tiled=True).reshape(rows.shape)  21.2 us
    ppermute x14, starting transfers between devices, send(): return lax.ppermute(block, LINE, pairs)  19 us
    pallas_call x1, Pallas kernels, seeds(): pl.pallas_call(seed_kernel, grid=(targets // tile,), in_specs=[pl.BlockSp...  16.6 us
    ppermute x11, starting transfers between devices, swap(): return lax.ppermute(block, 'core', SWAP)  12.5 us
    pallas_call x2, Pallas kernels, slot_counts(): pl.pallas_call(slot_kernel, grid=(steps,), in_specs=[pl.BlockSpec((step,...  9.53 us
    pallas_call x2, Pallas kernels, project(): pl.pallas_call(functools.partial(project_kernel, len(after)), in_specs=in...  8.35 us
    ppermute x14, waiting for transfers between devices, send(): return lax.ppermute(block, LINE, pairs)  8.09 us
    pallas_call x1, Pallas kernels, own_and_mean(): pl.pallas_call(functools.partial(mean_kernel, len(after)), grid_spec=pltp...  7.97 us
  transfers between devices with their start and end apart: 27, of which 10 were waited for; matrix products, arithmetic and copies ran while one was open for 1% of the time, Pallas kernels for 29%

profile of v4, /device:TPU:1, one launch (start us, length us, event | category | flops | bytes accessed | tf_op | source)
XLA Modules:
  0.0 124.5 jit_solution(4509764561632001990)
XLA Ops:
  0.1 0.7 copy-done.4
  0.8 5.6 %pick.1 = bf16[1024,128]{1,0:T(8,128)(2,1)} custom-call(s32[32,128]{1,0:T(8,128)S(1)} %bitcast.21, s32[2]{0:T(128)S(1)} %pad_add_fusion.at_ref, bf16[4096,256]{1,0:T(8,128)(2,1)} %refs_3_.1, bf16[4096,256]{1,0:T(8,128)(2,1)} %refs_3_.1, bf16[4096,256]{1,0:T(8,128)(2,1)} %refs_3_.1, bf16[4096,256]{1,0:T(8,128)(2,1)} %refs_3_.1), custom_call_target="tpu_custom_call" | custom-call | tf_op jit(solution)/shard_map/pick/pallas_call | solution.py:312
  6.4 12.0 %all-to-all-start = ((bf16[32,32,128]{2,1,0:T(8,128)(2,1)}), bf16[32,32,128]{2,1,0:T(8,128)(2,1)S(1)}, u32[]{:S(2)}, u32[]{:S(2)}) async-start(bf16[32,32,128]{2,1,0:T(8,128)(2,1)} %bitcast.6), calls=%async_computation | async-start | bytes 524288 | tf_op jit(solution)/shard_map/all_to_all | solution.py:487
  18.6 1.9 %node_table.1.table_ref = s32[8192,16]{1,0:T(8,128)S(1)} custom-call(s32[10,8192]{1,0:T(8,128)S(1)} %bitcast.18, s32[1,8192]{1,0:T(1,128)S(1)} %bitcast.19, s32[1,8192]{1,0:T(1,128)S(1)} %bitcast.20), custom_call_target="tpu_custom_call" | custom-call | tf_op jit(solution)/shard_map/node_table/pallas_call | solution.py:127
  20.5 6.3 %node_counts.1 = (s32[1024,16]{1,0:T(8,128)}, bf16[1024,1024]{1,0:T(8,128)(2,1)}, bf16[1024,1024]{1,0:T(8,128)(2,1)}, bf16[1024,1024]{1,0:T(8,128)(2,1)}, bf16[1024,1024]{1,0:T(8,128)(2,1)}, /*index=5*/s32[8,128]{1,0:T(8,128)}) custom-call(s32[1024]{0:T(1024)S(1)} %reshape.26.request_ref, s32[1]{0:T(128)} %bitcast.x_ref, s32[8192,16]{1,0:T(8,128)S(1)} %node_table.1.table_ref), custom_call_target="tpu_custom_call" | custom-call | flops 2147483648 | bytes 8388608 | tf_op jit(solution)/shard_map/node_counts/pallas_call | solution.py:157
  26.9 1.2 all-to-all-done
  28.1 1.2 collective-permute-start
  29.3 1.5 %collective-permute-start.1 = (bf16[1024,128]{1,0:T(8,128)(2,1)S(1)}, bf16[1024,128]{1,0:T(8,128)(2,1)S(1)}, u32[]{:S(2)}, u32[]{:S(2)}) collective-permute-start(bf16[1024,128]{1,0:T(8,128)(2,1)S(1)} %bitcast.16), channel_id=1, source_target_pairs={{0,5},{4,0},{1,4},{5,1},{2,7},{6,2},{3,6},{7,3},{8,13},{12,8},{9,1... | collective-permute-start | bytes 786440 | tf_op jit(solution)/shard_map/ppermute | solution.py:46
  30.8 0.1 and_add_fusion
  30.9 0.3 copy.17
  31.2 0.4 reshape.29.code_ref
  31.6 2.9 %collective-permute-done.refs_11_ = bf16[1024,128]{1,0:T(8,128)(2,1)S(1)} collective-permute-done((bf16[1024,128]{1,0:T(8,128)(2,1)S(1)}, bf16[1024,128]{1,0:T(8,128)(2,1)S(1)}, u32[]{:S(2)}, u32[]{:S(2)}) %collective-permute-start) | collective-permute-done | bytes 262176 | tf_op jit(solution)/shard_map/ppermute | solution.py:46
  34.5 1.3 %collective-permute-start.2 = (bf16[512,128]{1,0:T(8,128)(2,1)S(1)}, bf16[512,128]{1,0:T(8,128)(2,1)S(1)}, u32[]{:S(2)}, u32[]{:S(2)}) collective-permute-start(bf16[512,128]{1,0:T(8,128)(2,1)S(1)} %slice.12), channel_id=1, source_target_pairs={{0,4},{4,1},{1,5},{5,0},{2,6},{6,3},{3,7},{7,2},{8,12},{12,9},{9,1... | collective-permute-start | bytes 393224 | tf_op jit(solution)/shard_map/ppermute | solution.py:46
  35.8 1.6 %collective-permute-start.3 = (bf16[512,128]{1,0:T(8,128)(2,1)S(1)}, bf16[512,128]{1,0:T(8,128)(2,1)S(1)}, u32[]{:S(2)}, u32[]{:S(2)}) collective-permute-start(bf16[512,128]{1,0:T(8,128)(2,1)S(1)} %slice.13), channel_id=1, source_target_pairs={{0,5},{4,0},{1,4},{5,1},{2,7},{6,2},{3,6},{7,3},{8,13},{12,8},{9,1... | collective-permute-start | bytes 393224 | tf_op jit(solution)/shard_map/ppermute | solution.py:46
  37.4 4.7 %slot_counts.2 = (bf16[2048,1024]{1,0:T(8,128)(2,1)}, bf16[2048,1024]{1,0:T(8,128)(2,1)}, bf16[2048,1024]{1,0:T(8,128)(2,1)}, bf16[2048,1024]{1,0:T(8,128)(2,1)}, s32[8,128]{1,0:T(8,128)}) custom-call(s32[128,256]{1,0:T(8,128)S(1)} %reshape.29.code_ref), custom_call_target="tpu_custom_call" | custom-call | flops 2147483648 | bytes 8388608 | tf_op jit(solution)/shard_map/slot_counts/pallas_call | solution.py:212
  42.1 1.4 %collective-permute-start.4 = (bf16[256,256]{1,0:T(8,128)(2,1)S(1)}, bf16[256,256]{1,0:T(8,128)(2,1)S(1)}, u32[]{:S(2)}, u32[]{:S(2)}) collective-permute-start(bf16[256,256]{1,0:T(8,128)(2,1)S(1)} %copy-done.8), channel_id=1, source_target_pairs={{0,5},{4,0},{1,4},{5,1},{2,7},{6,2},{3,6},{7,3},{8,13},{12,8},{9,1... | collective-permute-start | bytes 393224 | tf_op jit(solution)/shard_map/ppermute | solution.py:46
  43.6 0.3 collective-permute-start.5
  43.9 0.3 collective-permute-start.6
  44.3 8.0 %own_and_mean.1 = bf16[1024,256]{1,0:T(8,128)(2,1)} custom-call(s32[1]{0:T(128)} %bitcast.x_ref, bf16[1024,1024]{1,0:T(8,128)(2,1)} %get-tuple-element.61.refs_0_, bf16[1024,1024]{1,0:T(8,128)(2,1)} %get-tuple-element.62.refs_1_, bf16[1024,1024]{1,0:T(8,128)(2,1)} %get-tuple-element.63.refs_2_, bf16[1024,1024]{1,0:T(8,128)(2,1)} %get-tuple-element.64.refs_3_, ...), custom_call_target="tpu_custom_call" | custom-call | flops 2147483648 | bytes 8388608 | tf_op jit(solution)/shard_map/own_and_mean/pallas_call | solution.py:355
  52.3 9.2 %all-to-all-start.1 = ((bf16[32,32,256]{2,1,0:T(8,128)(2,1)}), bf16[32,32,256]{2,1,0:T(8,128)(2,1)S(1)}, u32[]{:S(2)}, u32[]{:S(2)}) async-start(bf16[32,32,256]{2,1,0:T(8,128)(2,1)} %bitcast.24), calls=%async_computation.1 | async-start | bytes 1048576 | tf_op jit(solution)/shard_map/all_to_all | solution.py:487
  61.5 3.3 %collective-permute-start.7 = (bf16[1024,256]{1,0:T(8,128)(2,1)S(1)}, bf16[1024,256]{1,0:T(8,128)(2,1)S(1)}, u32[]{:S(2)}, u32[]{:S(2)}) collective-permute-start(bf16[1024,256]{1,0:T(8,128)(2,1)S(1)} %copy-done.6), channel_id=1, source_target_pairs={{0,1},{4,5},{1,0},{5,4},{2,3},{6,7},{3,2},{7,6},{8,9},{12,13},{9,8... | collective-permute-start | bytes 1572872 | tf_op jit(solution)/shard_map/ppermute | solution.py:46
  64.8 4.1 %collective-permute-start.10 = (bf16[256,256]{1,0:T(8,128)(2,1)S(1)}, bf16[256,256]{1,0:T(8,128)(2,1)S(1)}, u32[]{:S(2)}, u32[]{:S(2)}) collective-permute-start(bf16[256,256]{1,0:T(8,128)(2,1)S(1)} %collective-permute-done.5.refs_4_), channel_id=1, source_target_pairs={{0,2},{2,0},{1,3},{3,1},{4,6},{6,4},{5,7},{7,5},{8,10},{10,8},{9,1... | collective-permute-start | bytes 393224 | tf_op jit(solution)/shard_map/ppermute | solution.py:50
  68.9 0.3 collective-permute-start.11
  69.2 0.2 collective-permute-start.8
  69.4 0.3 collective-permute-start.9
  69.7 4.8 %slot_counts.3 = (bf16[2048,1024]{1,0:T(8,128)(2,1)}, bf16[2048,1024]{1,0:T(8,128)(2,1)}, bf16[2048,1024]{1,0:T(8,128)(2,1)}, bf16[2048,1024]{1,0:T(8,128)(2,1)}, s32[8,128]{1,0:T(8,128)}) custom-call(s32[128,256]{1,0:T(8,128)S(1)} %reshape.29.code_ref, ...), custom_call_target="tpu_custom_call", output_to_operand_aliasing={{0}: (1, {}), {1}: (2, {}), {2}: (3, {}), {3}: (4, {})} | custom-call | flops 2147483648 | bytes 8388608 | tf_op jit(solution)/shard_map/slot_counts/pallas_call | solution.py:212
  74.6 4.5 %collective-permute-start.16 = (bf16[1024,256]{1,0:T(8,128)(2,1)S(1)}, bf16[1024,256]{1,0:T(8,128)(2,1)S(1)}, u32[]{:S(2)}, u32[]{:S(2)}) collective-permute-start(bf16[1024,256]{1,0:T(8,128)(2,1)S(1)} %bitcast.12), channel_id=1, source_target_pairs={{0,2},{2,0},{1,3},{3,1},{4,6},{6,4},{5,7},{7,5},{8,10},{10,8},{9,1... | collective-permute-start | bytes 1572872 | tf_op jit(solution)/shard_map/ppermute | solution.py:50
  79.2 2.4 %collective-permute-start.14 = (bf16[512,256]{1,0:T(8,128)(2,1)S(1)}, bf16[512,256]{1,0:T(8,128)(2,1)S(1)}, u32[]{:S(2)}, u32[]{:S(2)}) collective-permute-start(bf16[512,256]{1,0:T(8,128)(2,1)S(1)} %get-tuple-element.117), channel_id=1, source_target_pairs={{0,4},{4,1},{1,5},{5,0},{2,6},{6,3},{3,7},{7,2},{8,12},{12,9},{9,1... | collective-permute-start | bytes 786440 | tf_op jit(solution)/shard_map/ppermute | solution.py:46
  81.6 0.5 collective-permute-start.15
  82.0 1.0 collective-permute-start.12
  83.0 1.7 %collective-permute-start.13 = (bf16[512,256]{1,0:T(8,128)(2,1)S(1)}, bf16[512,256]{1,0:T(8,128)(2,1)S(1)}, u32[]{:S(2)}, u32[]{:S(2)}) collective-permute-start(bf16[512,256]{1,0:T(8,128)(2,1)S(1)} %get-tuple-element.117), channel_id=1, source_target_pairs={{0,5},{4,0},{1,4},{5,1},{2,7},{6,2},{3,6},{7,3},{8,13},{12,8},{9,1... | collective-permute-start | bytes 786440 | tf_op jit(solution)/shard_map/ppermute | solution.py:46
  84.7 2.3 %assemble.1 = (bf16[4,512,256]{2,1,0:T(8,128)(2,1)S(1)}, bf16[1024,512]{1,0:T(8,128)(2,1)S(1)}, s32[8,128]{1,0:T(8,128)}) custom-call(s32[2]{0:T(128)S(1)} %pad_add_fusion.at_ref, bf16[256,256]{1,0:T(8,128)(2,1)} %refs_0_.2, bf16[256,256]{1,0:T(8,128)(2,1)} %copy-done.14, bf16[256,256]{1,0:T(8,128)(2,1)} %copy-done.9, bf16[256,256]{1,0:T(8,128)(2,1)} %copy-done.15, ...), custom_call_target="tpu_custom_call" | custom-call | tf_op jit(solution)/shard_map/assemble/pallas_call | solution.py:261
  87.1 1.3 %collective-permute-done.14.refs_4_ = bf16[512,256]{1,0:T(8,128)(2,1)S(1)} collective-permute-done((bf16[512,256]{1,0:T(8,128)(2,1)S(1)}, bf16[512,256]{1,0:T(8,128)(2,1)S(1)}, u32[]{:S(2)}, u32[]{:S(2)}) %collective-permute-start.14) | collective-permute-done | bytes 262176 | tf_op jit(solution)/shard_map/ppermute | solution.py:46
  88.3 0.8 collective-permute-done.15.refs_2_
  89.2 2.8 %project.2.refs_8_ = bf16[1024,512]{1,0:T(8,128)(2,1)S(1)} custom-call(bf16[4,512,256]{2,1,0:T(8,128)(2,1)S(1)} %get-tuple-element.102.first_ref.refs_6_, bf16[1024,512]{1,0:T(8,128)(2,1)S(1)} %get-tuple-element.103.second_ref.refs_7_, s32[8,128]{1,0:T(8,128)} %get-tuple-element.105.refs_0_, s32[8,128]{1,0:T(8,128)} %get-tuple-element.107.refs_1_, ...), custom_call_target="tpu_custom_call" | custom-call | flops 2147483648 | bytes 2097152 | tf_op jit(solution)/shard_map/project/pallas_call | solution.py:405
  92.0 1.9 %collective-permute-done.12.refs_6_ = bf16[512,256]{1,0:T(8,128)(2,1)S(1)} collective-permute-done((bf16[512,256]{1,0:T(8,128)(2,1)S(1)}, bf16[512,256]{1,0:T(8,128)(2,1)S(1)}, u32[]{:S(2)}, u32[]{:S(2)}) %collective-permute-start.12) | collective-permute-done | bytes 262176 | tf_op jit(solution)/shard_map/ppermute | solution.py:46
  94.0 0.8 collective-permute-done.13.refs_0_
  94.8 1.1 collective-permute-start.19
  95.9 0.5 collective-permute-start.20
  96.4 0.6 collective-permute-start.17
  97.0 0.1 collective-permute-done.19.refs_1_
  97.1 2.0 %collective-permute-start.18 = (bf16[512,256]{1,0:T(8,128)(2,1)S(1)}, bf16[512,256]{1,0:T(8,128)(2,1)S(1)}, u32[]{:S(2)}, u32[]{:S(2)}) collective-permute-start(bf16[512,256]{1,0:T(8,128)(2,1)S(1)} %collective-permute-done.15.refs_2_), channel_id=1, source_target_pairs={{0,5},{4,0},{1,4},{5,1},{2,7},{6,2},{3,6},{7,3},{8,13},{12,8},{9,1... | collective-permute-start | bytes 786440 | tf_op jit(solution)/shard_map/ppermute | solution.py:46
  99.1 5.5 %project.3.refs_9_ = bf16[2048,512]{1,0:T(8,128)(2,1)S(1)} custom-call(bf16[4,512,256]{2,1,0:T(8,128)(2,1)S(1)} %get-tuple-element.102.first_ref.refs_6_, bf16[1024,512]{1,0:T(8,128)(2,1)S(1)} %get-tuple-element.103.second_ref.refs_7_, bf16[512,256]{1,0:T(8,128)(2,1)S(1)} %collective-permute-done.13.refs_0_, ...), custom_call_target="tpu_custom_call" | custom-call | flops 4294967296 | bytes 4194304 | tf_op jit(solution)/shard_map/project/pallas_call | solution.py:405
  104.6 0.4 collective-permute-done.17.refs_10_
  105.0 1.4 %collective-permute-start.23 = (bf16[512,256]{1,0:T(8,128)(2,1)S(1)}, bf16[512,256]{1,0:T(8,128)(2,1)S(1)}, u32[]{:S(2)}, u32[]{:S(2)}) collective-permute-start(bf16[512,256]{1,0:T(8,128)(2,1)S(1)} %collective-permute-done.17.refs_10_), channel_id=1, source_target_pairs={{0,2},{2,0},{1,3},{3,1},{4,6},{6,4},{5,7},{7,5},{8,10},{10,8},{9,1... | collective-permute-start | bytes 786440 | tf_op jit(solution)/shard_map/ppermute | solution.py:50
  106.4 1.2 collective-permute-done.23.refs_11_
  107.5 0.4 collective-permute-done.24.refs_13_
  107.9 16.6 %seeds.1 = bf16[2048,256]{1,0:T(8,128)(2,1)} custom-call(bf16[2048,1024]{1,0:T(8,128)(2,1)} %get-tuple-element.80.refs_0_, bf16[2048,1024]{1,0:T(8,128)(2,1)} %get-tuple-element.81.refs_1_, bf16[2048,1024]{1,0:T(8,128)(2,1)} %get-tuple-element.82.refs_2_, bf16[2048,1024]{1,0:T(8,128)(2,1)} %get-tuple-element.83.refs_3_, s32[1,2048]{1,0:T(1,128)S(1)} %bitcast.23, ...), custom_call_target="tpu_custom_call" | custom-call | flops 8589934592 | bytes 16777216 | tf_op jit(solution)/shard_map/seeds/pallas_call | solution.py:445
  (63 shorter events, 0.4 us)
Async XLA Ops:
  0.0 18.4 %copy-start = (s32[1,32,128]{2,1,0:T(8,128)S(1)}, s32[1,32,128]{2,1,0:T(8,128)}, u32[]{:S(2)}) copy-start(s32[1,32,128]{2,1,0:T(8,128)} %param.17) | copy-start | bytes 49156
  0.1 0.7 copy-start.4
  0.8 17.8 %copy-start.1 = (s32[8192,10]{0,1:T(8,128)S(1)}, s32[8192,10]{0,1:T(8,128)}, u32[]{:S(2)}) copy-start(s32[8192,10]{0,1:T(8,128)} %param.13) | copy-start | bytes 983044
  0.8 17.8 %copy-start.2 = (s32[8192]{0:T(1024)S(1)}, s32[8192]{0:T(1024)}, u32[]{:S(2)}) copy-start(s32[8192]{0:T(1024)} %param.14) | copy-start | bytes 98308
  0.8 17.8 %copy-start.3 = (s32[8192]{0:T(1024)S(1)}, s32[8192]{0:T(1024)}, u32[]{:S(2)}) copy-start(s32[8192]{0:T(1024)} %param.15) | copy-start | bytes 98308
  6.4 21.7 %all-to-all-start = ((bf16[32,32,128]{2,1,0:T(8,128)(2,1)}), bf16[32,32,128]{2,1,0:T(8,128)(2,1)S(1)}, u32[]{:S(2)}, u32[]{:S(2)}) async-start(bf16[32,32,128]{2,1,0:T(8,128)(2,1)} %bitcast.6), calls=%async_computation | async-start | bytes 524288 | tf_op jit(solution)/shard_map/all_to_all | solution.py:487
  20.5 10.3 %copy-start.5 = (s32[2048]{0:T(1024)S(1)}, s32[2048]{0:T(1024)}, u32[]{:S(2)}) copy-start(s32[2048]{0:T(1024)} %param.20) | copy-start | bytes 24580
  20.5 10.2 %copy-start.16 = (s32[2048,15]{0,1:T(8,128)S(1)}, s32[2048,15]{0,1:T(8,128)}, u32[]{:S(2)}) copy-start(s32[2048,15]{0,1:T(8,128)} %param.18) | copy-start | bytes 368644
  28.1 6.4 %collective-permute-start = (bf16[1024,128]{1,0:T(8,128)(2,1)S(1)}, bf16[1024,128]{1,0:T(8,128)(2,1)S(1)}, u32[]{:S(2)}, u32[]{:S(2)}) collective-permute-start(bf16[1024,128]{1,0:T(8,128)(2,1)S(1)} %bitcast.15), channel_id=1, source_target_pairs={{0,4},{4,1},{1,5},{5,0},{2,6},{6,3},{3,7},{7,2},{8,12},{12,9},{9,1... | collective-permute-start | bytes 786440 | tf_op jit(solution)/shard_map/ppermute | solution.py:46
  29.3 5.2 %collective-permute-start.1 = (bf16[1024,128]{1,0:T(8,128)(2,1)S(1)}, bf16[1024,128]{1,0:T(8,128)(2,1)S(1)}, u32[]{:S(2)}, u32[]{:S(2)}) collective-permute-start(bf16[1024,128]{1,0:T(8,128)(2,1)S(1)} %bitcast.16), channel_id=1, source_target_pairs={{0,5},{4,0},{1,4},{5,1},{2,7},{6,2},{3,6},{7,3},{8,13},{12,8},{9,1... | collective-permute-start | bytes 786440 | tf_op jit(solution)/shard_map/ppermute | solution.py:46
  31.6 10.5 %copy-start.8 = (bf16[256,256]{1,0:T(8,128)(2,1)S(1)}, bf16[256,256]{1,0:T(8,128)(2,1)}, u32[]{:S(2)}) copy-start(bf16[256,256]{1,0:T(8,128)(2,1)} %refs_0_.2) | copy-start | bytes 393220
  34.5 9.7 %collective-permute-start.2 = (bf16[512,128]{1,0:T(8,128)(2,1)S(1)}, bf16[512,128]{1,0:T(8,128)(2,1)S(1)}, u32[]{:S(2)}, u32[]{:S(2)}) collective-permute-start(bf16[512,128]{1,0:T(8,128)(2,1)S(1)} %slice.12), channel_id=1, source_target_pairs={{0,4},{4,1},{1,5},{5,0},{2,6},{6,3},{3,7},{7,2},{8,12},{12,9},{9,1... | collective-permute-start | bytes 393224 | tf_op jit(solution)/shard_map/ppermute | solution.py:46
  35.8 8.4 %collective-permute-start.3 = (bf16[512,128]{1,0:T(8,128)(2,1)S(1)}, bf16[512,128]{1,0:T(8,128)(2,1)S(1)}, u32[]{:S(2)}, u32[]{:S(2)}) collective-permute-start(bf16[512,128]{1,0:T(8,128)(2,1)S(1)} %slice.13), channel_id=1, source_target_pairs={{0,5},{4,0},{1,4},{5,1},{2,7},{6,2},{3,6},{7,3},{8,13},{12,8},{9,1... | collective-permute-start | bytes 393224 | tf_op jit(solution)/shard_map/ppermute | solution.py:46
  42.1 10.1 %collective-permute-start.4 = (bf16[256,256]{1,0:T(8,128)(2,1)S(1)}, bf16[256,256]{1,0:T(8,128)(2,1)S(1)}, u32[]{:S(2)}, u32[]{:S(2)}) collective-permute-start(bf16[256,256]{1,0:T(8,128)(2,1)S(1)} %copy-done.8), channel_id=1, source_target_pairs={{0,5},{4,0},{1,4},{5,1},{2,7},{6,2},{3,6},{7,3},{8,13},{12,8},{9,1... | collective-permute-start | bytes 393224 | tf_op jit(solution)/shard_map/ppermute | solution.py:46
  43.6 8.7 %collective-permute-start.5 = (bf16[256,256]{1,0:T(8,128)(2,1)S(1)}, bf16[256,256]{1,0:T(8,128)(2,1)S(1)}, u32[]{:S(2)}, u32[]{:S(2)}) collective-permute-start(bf16[256,256]{1,0:T(8,128)(2,1)S(1)} %copy-done.8), channel_id=1, source_target_pairs={{0,1},{4,5},{1,0},{5,4},{2,3},{6,7},{3,2},{7,6},{8,9},{12,13},{9,8... | collective-permute-start | bytes 393224 | tf_op jit(solution)/shard_map/ppermute | solution.py:46
  43.9 8.4 %collective-permute-start.6 = (bf16[256,256]{1,0:T(8,128)(2,1)S(1)}, bf16[256,256]{1,0:T(8,128)(2,1)S(1)}, u32[]{:S(2)}, u32[]{:S(2)}) collective-permute-start(bf16[256,256]{1,0:T(8,128)(2,1)S(1)} %copy-done.8), channel_id=1, source_target_pairs={{0,4},{4,1},{1,5},{5,0},{2,6},{6,3},{3,7},{7,2},{8,12},{12,9},{9,1... | collective-permute-start | bytes 393224 | tf_op jit(solution)/shard_map/ppermute | solution.py:46
  44.3 17.2 %copy-start.6 = (bf16[1024,256]{1,0:T(8,128)(2,1)S(1)}, bf16[1024,256]{1,0:T(8,128)(2,1)}, u32[]{:S(2)}) copy-start(bf16[1024,256]{1,0:T(8,128)(2,1)} %refs_8_) | copy-start | bytes 1572868
  44.3 20.5 %copy-start.17 = (s32[2048]{0:T(1024)S(1)}, s32[2048]{0:T(1024)}, u32[]{:S(2)}) copy-start(s32[2048]{0:T(1024)} %param.19) | copy-start | bytes 24580
  52.3 22.2 %copy-start.9 = (bf16[256,256]{1,0:T(8,128)(2,1)}, bf16[256,256]{1,0:T(8,128)(2,1)S(1)}, u32[]{:S(2)}) copy-start(bf16[256,256]{1,0:T(8,128)(2,1)S(1)} %collective-permute-done.4.refs_2_) | copy-start | bytes 393220
  52.3 22.2 %copy-start.10 = (bf16[256,256]{1,0:T(8,128)(2,1)}, bf16[256,256]{1,0:T(8,128)(2,1)S(1)}, u32[]{:S(2)}) copy-start(bf16[256,256]{1,0:T(8,128)(2,1)S(1)} %collective-permute-done.5.refs_4_) | copy-start | bytes 393220
  52.3 22.2 %copy-start.11 = (bf16[256,256]{1,0:T(8,128)(2,1)}, bf16[256,256]{1,0:T(8,128)(2,1)S(1)}, u32[]{:S(2)}) copy-start(bf16[256,256]{1,0:T(8,128)(2,1)S(1)} %collective-permute-done.6.refs_6_) | copy-start | bytes 393220
  52.3 22.3 %all-to-all-start.1 = ((bf16[32,32,256]{2,1,0:T(8,128)(2,1)}), bf16[32,32,256]{2,1,0:T(8,128)(2,1)S(1)}, u32[]{:S(2)}, u32[]{:S(2)}) async-start(bf16[32,32,256]{2,1,0:T(8,128)(2,1)} %bitcast.24), calls=%async_computation.1 | async-start | bytes 1048576 | tf_op jit(solution)/shard_map/all_to_all | solution.py:487
  61.5 13.1 %collective-permute-start.7 = (bf16[1024,256]{1,0:T(8,128)(2,1)S(1)}, bf16[1024,256]{1,0:T(8,128)(2,1)S(1)}, u32[]{:S(2)}, u32[]{:S(2)}) collective-permute-start(bf16[1024,256]{1,0:T(8,128)(2,1)S(1)} %copy-done.6), channel_id=1, source_target_pairs={{0,1},{4,5},{1,0},{5,4},{2,3},{6,7},{3,2},{7,6},{8,9},{12,13},{9,8... | collective-permute-start | bytes 1572872 | tf_op jit(solution)/shard_map/ppermute | solution.py:46
  64.8 9.7 %collective-permute-start.10 = (bf16[256,256]{1,0:T(8,128)(2,1)S(1)}, bf16[256,256]{1,0:T(8,128)(2,1)S(1)}, u32[]{:S(2)}, u32[]{:S(2)}) collective-permute-start(bf16[256,256]{1,0:T(8,128)(2,1)S(1)} %collective-permute-done.5.refs_4_), channel_id=1, source_target_pairs={{0,2},{2,0},{1,3},{3,1},{4,6},{6,4},{5,7},{7,5},{8,10},{10,8},{9,1... | collective-permute-start | bytes 393224 | tf_op jit(solution)/shard_map/ppermute | solution.py:50
  68.9 5.6 %collective-permute-start.11 = (bf16[256,256]{1,0:T(8,128)(2,1)S(1)}, bf16[256,256]{1,0:T(8,128)(2,1)S(1)}, u32[]{:S(2)}, u32[]{:S(2)}) collective-permute-start(bf16[256,256]{1,0:T(8,128)(2,1)S(1)} %collective-permute-done.6.refs_6_), channel_id=1, source_target_pairs={{0,2},{2,0},{1,3},{3,1},{4,6},{6,4},{5,7},{7,5},{8,10},{10,8},{9,1... | collective-permute-start | bytes 393224 | tf_op jit(solution)/shard_map/ppermute | solution.py:50
  69.2 5.4 %collective-permute-start.8 = (bf16[256,256]{1,0:T(8,128)(2,1)S(1)}, bf16[256,256]{1,0:T(8,128)(2,1)S(1)}, u32[]{:S(2)}, u32[]{:S(2)}) collective-permute-start(bf16[256,256]{1,0:T(8,128)(2,1)S(1)} %copy-done.8), channel_id=1, source_target_pairs={{0,2},{2,0},{1,3},{3,1},{4,6},{6,4},{5,7},{7,5},{8,10},{10,8},{9,1... | collective-permute-start | bytes 393224 | tf_op jit(solution)/shard_map/ppermute | solution.py:50
  69.4 5.2 %collective-permute-start.9 = (bf16[256,256]{1,0:T(8,128)(2,1)S(1)}, bf16[256,256]{1,0:T(8,128)(2,1)S(1)}, u32[]{:S(2)}, u32[]{:S(2)}) collective-permute-start(bf16[256,256]{1,0:T(8,128)(2,1)S(1)} %collective-permute-done.4.refs_2_), channel_id=1, source_target_pairs={{0,2},{2,0},{1,3},{3,1},{4,6},{6,4},{5,7},{7,5},{8,10},{10,8},{9,1... | collective-permute-start | bytes 393224 | tf_op jit(solution)/shard_map/ppermute | solution.py:50
  74.5 10.2 %copy-start.12 = (bf16[256,256]{1,0:T(8,128)(2,1)}, bf16[256,256]{1,0:T(8,128)(2,1)S(1)}, u32[]{:S(2)}) copy-start(bf16[256,256]{1,0:T(8,128)(2,1)S(1)} %collective-permute-done.10.refs_5_) | copy-start | bytes 393220
  74.5 10.2 %copy-start.13 = (bf16[256,256]{1,0:T(8,128)(2,1)}, bf16[256,256]{1,0:T(8,128)(2,1)S(1)}, u32[]{:S(2)}) copy-start(bf16[256,256]{1,0:T(8,128)(2,1)S(1)} %collective-permute-done.11.refs_7_) | copy-start | bytes 393220
  74.6 10.2 %copy-start.14 = (bf16[256,256]{1,0:T(8,128)(2,1)}, bf16[256,256]{1,0:T(8,128)(2,1)S(1)}, u32[]{:S(2)}) copy-start(bf16[256,256]{1,0:T(8,128)(2,1)S(1)} %collective-permute-done.8.refs_1_) | copy-start | bytes 393220
  74.6 10.1 %copy-start.15 = (bf16[256,256]{1,0:T(8,128)(2,1)}, bf16[256,256]{1,0:T(8,128)(2,1)S(1)}, u32[]{:S(2)}) copy-start(bf16[256,256]{1,0:T(8,128)(2,1)S(1)} %collective-permute-done.9.refs_3_) | copy-start | bytes 393220
  74.6 10.1 %copy-start.7 = (bf16[1024,256]{1,0:T(8,128)(2,1)}, bf16[1024,256]{1,0:T(8,128)(2,1)S(1)}, u32[]{:S(2)}) copy-start(bf16[1024,256]{1,0:T(8,128)(2,1)S(1)} %collective-permute-done.7.refs_9_) | copy-start | bytes 1572868
  74.6 14.5 %collective-permute-start.16 = (bf16[1024,256]{1,0:T(8,128)(2,1)S(1)}, bf16[1024,256]{1,0:T(8,128)(2,1)S(1)}, u32[]{:S(2)}, u32[]{:S(2)}) collective-permute-start(bf16[1024,256]{1,0:T(8,128)(2,1)S(1)} %bitcast.12), channel_id=1, source_target_pairs={{0,2},{2,0},{1,3},{3,1},{4,6},{6,4},{5,7},{7,5},{8,10},{10,8},{9,1... | collective-permute-start | bytes 1572872 | tf_op jit(solution)/shard_map/ppermute | solution.py:50
  79.2 9.2 %collective-permute-start.14 = (bf16[512,256]{1,0:T(8,128)(2,1)S(1)}, bf16[512,256]{1,0:T(8,128)(2,1)S(1)}, u32[]{:S(2)}, u32[]{:S(2)}) collective-permute-start(bf16[512,256]{1,0:T(8,128)(2,1)S(1)} %get-tuple-element.117), channel_id=1, source_target_pairs={{0,4},{4,1},{1,5},{5,0},{2,6},{6,3},{3,7},{7,2},{8,12},{12,9},{9,1... | collective-permute-start | bytes 786440 | tf_op jit(solution)/shard_map/ppermute | solution.py:46
  81.6 7.6 %collective-permute-start.15 = (bf16[512,256]{1,0:T(8,128)(2,1)S(1)}, bf16[512,256]{1,0:T(8,128)(2,1)S(1)}, u32[]{:S(2)}, u32[]{:S(2)}) collective-permute-start(bf16[512,256]{1,0:T(8,128)(2,1)S(1)} %get-tuple-element.118), channel_id=1, source_target_pairs={{0,5},{4,0},{1,4},{5,1},{2,7},{6,2},{3,6},{7,3},{8,13},{12,8},{9,1... | collective-permute-start | bytes 786440 | tf_op jit(solution)/shard_map/ppermute | solution.py:46
  82.0 11.9 %collective-permute-start.12 = (bf16[512,256]{1,0:T(8,128)(2,1)S(1)}, bf16[512,256]{1,0:T(8,128)(2,1)S(1)}, u32[]{:S(2)}, u32[]{:S(2)}) collective-permute-start(bf16[512,256]{1,0:T(8,128)(2,1)S(1)} %get-tuple-element.118), channel_id=1, source_target_pairs={{0,4},{4,1},{1,5},{5,0},{2,6},{6,3},{3,7},{7,2},{8,12},{12,9},{9,1... | collective-permute-start | bytes 786440 | tf_op jit(solution)/shard_map/ppermute | solution.py:46
  83.0 11.7 %collective-permute-start.13 = (bf16[512,256]{1,0:T(8,128)(2,1)S(1)}, bf16[512,256]{1,0:T(8,128)(2,1)S(1)}, u32[]{:S(2)}, u32[]{:S(2)}) collective-permute-start(bf16[512,256]{1,0:T(8,128)(2,1)S(1)} %get-tuple-element.117), channel_id=1, source_target_pairs={{0,5},{4,0},{1,4},{5,1},{2,7},{6,2},{3,6},{7,3},{8,13},{12,8},{9,1... | collective-permute-start | bytes 786440 | tf_op jit(solution)/shard_map/ppermute | solution.py:46
  94.8 2.3 %collective-permute-start.19 = (bf16[512,256]{1,0:T(8,128)(2,1)S(1)}, bf16[512,256]{1,0:T(8,128)(2,1)S(1)}, u32[]{:S(2)}, u32[]{:S(2)}) collective-permute-start(bf16[512,256]{1,0:T(8,128)(2,1)S(1)} %collective-permute-done.13.refs_0_), channel_id=1, source_target_pairs={{0,2},{2,0},{1,3},{3,1},{4,6},{6,4},{5,7},{7,5},{8,10},{10,8},{9,1... | collective-permute-start | bytes 786440 | tf_op jit(solution)/shard_map/ppermute | solution.py:50
  95.9 3.2 %collective-permute-start.22 = (bf16[512,256]{1,0:T(8,128)(2,1)S(1)}, bf16[512,256]{1,0:T(8,128)(2,1)S(1)}, u32[]{:S(2)}, u32[]{:S(2)}) collective-permute-start(bf16[512,256]{1,0:T(8,128)(2,1)S(1)} %collective-permute-done.12.refs_6_), channel_id=1, source_target_pairs={{0,2},{2,0},{1,3},{3,1},{4,6},{6,4},{5,7},{7,5},{8,10},{10,8},{9,1... | collective-permute-start | bytes 786440 | tf_op jit(solution)/shard_map/ppermute | solution.py:50
  95.9 3.2 %collective-permute-start.20 = (bf16[512,256]{1,0:T(8,128)(2,1)S(1)}, bf16[512,256]{1,0:T(8,128)(2,1)S(1)}, u32[]{:S(2)}, u32[]{:S(2)}) collective-permute-start(bf16[512,256]{1,0:T(8,128)(2,1)S(1)} %collective-permute-done.15.refs_2_), channel_id=1, source_target_pairs={{0,2},{2,0},{1,3},{3,1},{4,6},{6,4},{5,7},{7,5},{8,10},{10,8},{9,1... | collective-permute-start | bytes 786440 | tf_op jit(solution)/shard_map/ppermute | solution.py:50
  96.4 2.7 %collective-permute-start.21 = (bf16[512,256]{1,0:T(8,128)(2,1)S(1)}, bf16[512,256]{1,0:T(8,128)(2,1)S(1)}, u32[]{:S(2)}, u32[]{:S(2)}) collective-permute-start(bf16[512,256]{1,0:T(8,128)(2,1)S(1)} %collective-permute-done.14.refs_4_), channel_id=1, source_target_pairs={{0,2},{2,0},{1,3},{3,1},{4,6},{6,4},{5,7},{7,5},{8,10},{10,8},{9,1... | collective-permute-start | bytes 786440 | tf_op jit(solution)/shard_map/ppermute | solution.py:50
  96.4 8.6 %collective-permute-start.17 = (bf16[512,256]{1,0:T(8,128)(2,1)S(1)}, bf16[512,256]{1,0:T(8,128)(2,1)S(1)}, u32[]{:S(2)}, u32[]{:S(2)}) collective-permute-start(bf16[512,256]{1,0:T(8,128)(2,1)S(1)} %collective-permute-done.14.refs_4_), channel_id=1, source_target_pairs={{0,4},{4,1},{1,5},{5,0},{2,6},{6,3},{3,7},{7,2},{8,12},{12,9},{9,1... | collective-permute-start | bytes 786440 | tf_op jit(solution)/shard_map/ppermute | solution.py:46
  97.1 7.9 %collective-permute-start.18 = (bf16[512,256]{1,0:T(8,128)(2,1)S(1)}, bf16[512,256]{1,0:T(8,128)(2,1)S(1)}, u32[]{:S(2)}, u32[]{:S(2)}) collective-permute-start(bf16[512,256]{1,0:T(8,128)(2,1)S(1)} %collective-permute-done.15.refs_2_), channel_id=1, source_target_pairs={{0,5},{4,0},{1,4},{5,1},{2,7},{6,2},{3,6},{7,3},{8,13},{12,8},{9,1... | collective-permute-start | bytes 786440 | tf_op jit(solution)/shard_map/ppermute | solution.py:46
  105.0 2.5 %collective-permute-start.23 = (bf16[512,256]{1,0:T(8,128)(2,1)S(1)}, bf16[512,256]{1,0:T(8,128)(2,1)S(1)}, u32[]{:S(2)}, u32[]{:S(2)}) collective-permute-start(bf16[512,256]{1,0:T(8,128)(2,1)S(1)} %collective-permute-done.17.refs_10_), channel_id=1, source_target_pairs={{0,2},{2,0},{1,3},{3,1},{4,6},{6,4},{5,7},{7,5},{8,10},{10,8},{9,1... | collective-permute-start | bytes 786440 | tf_op jit(solution)/shard_map/ppermute | solution.py:50
  106.4 1.5 %collective-permute-start.24 = (bf16[512,256]{1,0:T(8,128)(2,1)S(1)}, bf16[512,256]{1,0:T(8,128)(2,1)S(1)}, u32[]{:S(2)}, u32[]{:S(2)}) collective-permute-start(bf16[512,256]{1,0:T(8,128)(2,1)S(1)} %collective-permute-done.18.refs_12_), channel_id=1, source_target_pairs={{0,2},{2,0},{1,3},{3,1},{4,6},{6,4},{5,7},{7,5},{8,10},{10,8},{9,1... | collective-permute-start | bytes 786440 | tf_op jit(solution)/shard_map/ppermute | solution.py:50
